TPU v7x, 32 devices: a whole 2x2x4 slice. The times are simulated.
32 devices in a mesh: gx: 4 (over y, x), gy: 2 (over core), gz: 4 (over z).
Axes of the slice: x: 2, y: 2, z: 4, core: 2. Of those that a mesh axis runs over, the one named last changes fastest.
Arguments:
- residual_start: float32 [8, 4, 8, 81, 128], P('gx', 'gy', 'gz'), may hold values from -6 to 6
- patch_inverse: bfloat16 [8, 4, 8, 540, 540], P('gx', 'gy', 'gz'), may hold values from -0.05 to 0.4
- patch_order: int32 [8, 4, 8, 540], P('gx', 'gy', 'gz'), may hold values from 0 to 539, each once within a row
- element_matrix: float32 [8, 4, 8, 108, 108], P('gx', 'gy', 'gz'), may hold values from -1.6 to 6.5
- face_order: int32 [8, 4, 8, 6, 9], P('gx', 'gy', 'gz'), may hold values from 0 to 8, each once within a row
Outputs:
- solution: float32 [8, 4, 8, 81, 128], P('gx', 'gy', 'gz')
- residual: float32 [8, 4, 8, 81, 128], P('gx', 'gy', 'gz')
Inputs may be any that keep to these rules, and one draw needn't show every extreme that they name: `patch_order`: each row lists each of the 540 canonical rows of a star once. `face_order`: each face's row lists each of its 9 degrees of freedom once.
All inputs are finite; a program needn't handle non-finite values.
Results may differ from a plain program's by a relative error of at most 0.0068.
Values may be sent and summed in bfloat16 or wider, within the bound.
No kernel may reach another device: no remote copies, remote signals or barrier semaphores. Data moves between devices by JAX's collectives and lax.ppermute only.
A program may use at most 128 MiB of HBM per device.

v0:
```python
import jax
import jax.numpy as jnp
from jax import lax
from jax.sharding import PartitionSpec as P

INNER = 54
FACE = 9
SWEEPS = 2
PATCH = 540


def passed_along(value, axis, steps):
    count = lax.axis_size(axis)
    initial, last = (max(0, -steps), min(count, count - steps))
    return lax.ppermute(value, axis, [(source, source + steps) for source in range(initial, last)])


def from_behind(block, axis, distance):
    devices = range(lax.axis_size(axis))
    route = [((i - distance) % len(devices), i) for i in devices]
    return lax.ppermute(block, axis, route)


def face_mask(start_y, start_z, cells_y, cells_z):
    rows = jnp.arange(INNER + 3 * FACE, dtype=jnp.int32)
    in_second = (rows >= INNER + FACE) & (rows < INNER + 2 * FACE)
    in_third = rows >= INNER + 2 * FACE
    index_y = start_y + jnp.arange(cells_y, dtype=jnp.int32)
    index_z = start_z + jnp.arange(cells_z, dtype=jnp.int32)
    removed = (
        in_second[None, None, :] & (index_y == 0)[:, None, None]
        | in_third[None, None, :] & (index_z == 0)[None, :, None]
    )
    return jnp.where(removed, 0.0, 1.0).astype(jnp.float32)[None, :, :, :, None]


def star_vectors(extended, counts):
    cells_x, cells_y, cells_z = counts
    pieces = []
    for xoffset in (0, 1):
        for yoffset in (0, 1):
            for zoffset in (0, 1):
                pieces.append(
                    extended[
                        xoffset : xoffset + cells_x,
                        yoffset : yoffset + cells_y,
                        zoffset : zoffset + cells_z,
                        :INNER,
                    ]
                )
    for first in (0, 1):
        for second in (0, 1):
            pieces.append(
                extended[
                    1 : 1 + cells_x,
                    first : first + cells_y,
                    second : second + cells_z,
                    INNER : INNER + FACE,
                ]
            )
    for first in (0, 1):
        for second in (0, 1):
            pieces.append(
                extended[
                    first : first + cells_x,
                    1 : 1 + cells_y,
                    second : second + cells_z,
                    INNER + FACE : INNER + 2 * FACE,
                ]
            )
    for first in (0, 1):
        for second in (0, 1):
            pieces.append(
                extended[
                    first : first + cells_x,
                    second : second + cells_y,
                    1 : 1 + cells_z,
                    INNER + 2 * FACE :,
                ]
            )
    return jnp.concatenate(pieces, axis=3)


def place_corrections(solved):
    total = None
    face_base = 8 * INNER
    for xoffset in (0, 1):
        for yoffset in (0, 1):
            for zoffset in (0, 1):
                member = 4 * xoffset + 2 * yoffset + zoffset
                parts = [solved[..., INNER * member : INNER * (member + 1), :]]
                blank = jnp.zeros(solved.shape[:3] + (FACE, solved.shape[4]), jnp.float32)
                start = face_base + FACE * (2 * yoffset + zoffset)
                parts.append(solved[..., start : start + FACE, :] if xoffset == 1 else blank)
                start = face_base + 4 * FACE + FACE * (2 * xoffset + zoffset)
                parts.append(solved[..., start : start + FACE, :] if yoffset == 1 else blank)
                start = face_base + 8 * FACE + FACE * (2 * xoffset + yoffset)
                parts.append(solved[..., start : start + FACE, :] if zoffset == 1 else blank)
                block = jnp.concatenate(parts, axis=3)
                block = jnp.pad(
                    block,
                    (
                        (xoffset, 1 - xoffset),
                        (yoffset, 1 - yoffset),
                        (zoffset, 1 - zoffset),
                        (0, 0),
                        (0, 0),
                    ),
                )
                total = block if total is None else total + block
    return total


def canonical_matrices(matrices, face_order):
    cells = matrices.shape[:3]
    interior = jnp.broadcast_to(jnp.arange(INNER, dtype=jnp.int32), cells + (INNER,))
    offsets = (INNER + FACE * jnp.arange(6, dtype=jnp.int32))[:, None]
    slots = (face_order + offsets).reshape(cells + (6 * FACE,))
    forward = jnp.concatenate([interior, slots], axis=3)
    inverse = jnp.argsort(forward, axis=3)
    rows = jnp.take_along_axis(matrices, inverse[..., :, None], axis=3)
    return jnp.take_along_axis(rows, inverse[..., None, :], axis=4)


def element_change(owned, uppers, matrices_c):
    local = jnp.concatenate(
        [
            owned[..., :INNER, :],
            owned[..., INNER : INNER + FACE, :],
            uppers[0],
            owned[..., INNER + FACE : INNER + 2 * FACE, :],
            uppers[1],
            owned[..., INNER + 2 * FACE :, :],
            uppers[2],
        ],
        axis=3,
    )
    image = jnp.einsum("xyzij,xyzjr->xyzir", matrices_c, local, precision=lax.Precision.HIGHEST)
    base = INNER
    own_change = jnp.concatenate(
        [
            image[..., :INNER, :],
            image[..., base : base + FACE, :],
            image[..., base + 2 * FACE : base + 3 * FACE, :],
            image[..., base + 4 * FACE : base + 5 * FACE, :],
        ],
        axis=3,
    )
    return (
        own_change,
        (
            image[..., base + FACE : base + 2 * FACE, :],
            image[..., base + 3 * FACE : base + 4 * FACE, :],
            image[..., base + 5 * FACE :, :],
        ),
    )


def extend_along_z(rounded):
    received = passed_along(rounded[:, :, -1:], "gz", 1)
    extended = jnp.concatenate([received, rounded], axis=2)
    received = passed_along(extended[:, -1:], "gy", 1)
    extended = jnp.concatenate([received, extended], axis=1)
    received = from_behind(extended[-1:], "gx", 1)
    return jnp.concatenate([received, extended], axis=0)


def collect_along_x(placed):
    received = from_behind(placed[:1], "gx", -1)
    merged = placed[1:]
    merged = jnp.concatenate([merged[:-1], merged[-1:] + received], axis=0)
    received = passed_along(merged[:, :1], "gy", -1)
    merged = merged[:, 1:]
    merged = jnp.concatenate([merged[:, :-1], merged[:, -1:] + received], axis=1)
    received = passed_along(merged[:, :, :1], "gz", -1)
    merged = merged[:, :, 1:]
    return jnp.concatenate([merged[:, :, :-1], merged[:, :, -1:] + received], axis=2)


def body(residual_start, patch_inverse, patch_order, element_matrix, face_order):
    cells_x, cells_y, cells_z = residual_start.shape[:3]
    columns = residual_start.shape[4]
    counts = (cells_x, cells_y, cells_z)
    mask = face_mask(
        lax.axis_index("gy") * cells_y, lax.axis_index("gz") * cells_z, cells_y, cells_z
    )
    residual = residual_start * mask
    solution = jnp.zeros_like(residual)
    order = patch_order.reshape(-1, PATCH)
    back = jnp.argsort(order, axis=1)
    inverses = patch_inverse.reshape(-1, PATCH, PATCH)
    inverses = jnp.take_along_axis(inverses, back[:, :, None], axis=1)
    inverses = jnp.take_along_axis(inverses, back[:, None, :], axis=2)
    matrices_c = canonical_matrices(element_matrix, face_order)
    for repeat in range(SWEEPS):
        rounded = residual.astype(jnp.bfloat16)
        extended = extend_along_z(rounded)
        vectors = star_vectors(extended, counts).reshape(-1, PATCH, columns)
        solved = jnp.einsum("vts,vsr->vtr", inverses, vectors, preferred_element_type=jnp.float32)
        placed = place_corrections(solved.reshape(counts + (PATCH, columns)))
        owned = collect_along_x(placed)
        owned = owned * mask
        solution = solution + owned
        rows_x = owned[..., INNER : INNER + FACE, :]
        rows_y = owned[..., INNER + FACE : INNER + 2 * FACE, :]
        rows_z = owned[..., INNER + 2 * FACE :, :]
        upper_x = jnp.concatenate([rows_x[1:], from_behind(rows_x[:1], "gx", -1)], axis=0)
        upper_y = jnp.concatenate([rows_y[:, 1:], passed_along(rows_y[:, :1], "gy", -1)], axis=1)
        upper_z = jnp.concatenate(
            [rows_z[:, :, 1:], passed_along(rows_z[:, :, :1], "gz", -1)], axis=2
        )
        own_change, terms = element_change(owned, (upper_x, upper_y, upper_z), matrices_c)
        moved_x = jnp.concatenate([from_behind(terms[0][-1:], "gx", 1), terms[0][:-1]], axis=0)
        moved_y = jnp.concatenate(
            [passed_along(terms[1][:, -1:], "gy", 1), terms[1][:, :-1]], axis=1
        )
        moved_z = jnp.concatenate(
            [passed_along(terms[2][:, :, -1:], "gz", 1), terms[2][:, :, :-1]], axis=2
        )
        extra = jnp.concatenate(
            [jnp.zeros_like(owned[..., :INNER, :]), moved_x, moved_y, moved_z], axis=3
        )
        residual = residual - (own_change + extra) * mask
    return (solution, residual)


def solution(mesh):
    return jax.shard_map(
        body,
        mesh=mesh,
        in_specs=(
            P("gx", "gy", "gz", None, None),
            P("gx", "gy", "gz", None, None),
            P("gx", "gy", "gz", None),
            P("gx", "gy", "gz", None, None),
            P("gx", "gy", "gz", None, None),
        ),
        out_specs=(P("gx", "gy", "gz", None, None), P("gx", "gy", "gz", None, None)),
        check_vma=False,
    )
```

profile of v0, /device:TPU:0, one launch (start us, length us, event | category | flops | bytes accessed | tf_op | source)
XLA Modules:
  0.0 373.2 jit_solution(4703580855371854130)
XLA Ops:
  1.9 5.0 %collective-permute-start = (bf16[2,2,1,81,128]{4,3,2,1,0:T(8,128)(2,1)S(1)}, bf16[2,2,1,81,128]{4,3,2,1,0:T(8,128)(2,1)S(1)}, u32[]{:S(2)}, u32[]{:S(2)}) collective-permute-start(bf16[2,2,1,81,128]{4,3,2,1,0:T(8,128)(2,1)S(1)} %slice.636), channel_id=1, source_target_pairs={{0,1},{1,2},{2,3},{4,5},{5,6},{6,7},{8,9},{9,10},{10,11},{12,13},{... | collective-permute-start | bytes 248840 | tf_op jit(solution)/shard_map/ppermute | solution.py:15
  7.6 4.8 %sort.34 = (s32[8,540]{1,0:T(8,128)}, s32[8,540]{1,0:T(8,128)S(1)}) sort(s32[8,540]{1,0:T(8,128)S(1)} %reshape.167, s32[8,540]{1,0:T(8,128)S(1)} %iota.40), dimensions={1}, to_apply=%region_0.1 | sort | flops 56160 | bytes 69120 | tf_op jit(solution)/shard_map/jit(argsort)/sort | solution.py:190
  12.5 6.1 %copy.72 = bf16[2,2,2,540,540]{4,2,1,0,3:T(2,128)(2,1)} copy(bf16[2,2,2,540,540]{4,2,3,1,0:T(2,128)(2,1)} %param.6) | data formatting | bytes 9331200 | tf_op args[1]
  18.6 12.2 %reshape.168 = bf16[8,540,540]{2,0,1:T(8,128)(2,1)} reshape(bf16[2,2,2,540,540]{4,2,1,0,3:T(2,128)(2,1)} %copy.72) | data formatting | bytes 9331200 | tf_op jit(solution)/shard_map/reshape | solution.py:191
  30.8 67.0 %gather_fusion = bf16[4320,540]{1,0:T(8,128)(2,1)} fusion(bf16[8,540,540]{2,0,1:T(8,128)(2,1)} %reshape.168, s32[4320]{0:T(1024)S(1)} %reshape.174), kind=kCustom, calls=%fused_computation | custom fusion | bytes 9365760 | tf_op jit(solution)/shard_map/jit(take_along_axis)/gather | solution.py:192
  97.8 6.0 %reshape.208 = bf16[8,540,540]{2,1,0:T(8,128)(2,1)} reshape(bf16[4320,540]{1,0:T(8,128)(2,1)} %gather_fusion) | data formatting | bytes 9331200 | tf_op jit(solution)/shard_map/jit(take_along_axis)/gather | solution.py:192
  103.8 11.1 %copy.91 = bf16[8,540,540]{1,0,2:T(8,128)(2,1)} copy(bf16[8,540,540]{2,1,0:T(8,128)(2,1)} %reshape.208) | data formatting | bytes 9331200 | tf_op jit(solution)/shard_map/jit(take_along_axis)/gather | solution.py:192
  114.9 5.5 %broadcast_select_fusion = bf16[8,540,540]{1,0,2:T(8,128)(2,1)} fusion(bf16[8,540,540]{1,0,2:T(8,128)(2,1)} %copy.91, pred[8,540]{1,0:T(8,128)(4,1)S(1)} %compare_and_fusion), kind=kLoop, calls=%fused_computation.4 | loop fusion | flops 2332800 | bytes 9335520 | tf_op jit(solution)/shard_map/jit(take_along_axis)/select_n | solution.py:192
  120.4 67.0 %gather_fusion.1 = bf16[4320,540]{1,0:T(8,128)(2,1)} fusion(bf16[8,540,540]{1,0,2:T(8,128)(2,1)} %broadcast_select_fusion, s32[4320]{0:T(1024)S(1)} %reshape.174), kind=kCustom, calls=%fused_computation.1 | custom fusion | bytes 9365760 | tf_op jit(solution)/shard_map/jit(take_along_axis)/gather | solution.py:193
  187.4 6.0 %reshape.209 = bf16[8,540,540]{2,1,0:T(8,128)(2,1)} reshape(bf16[4320,540]{1,0:T(8,128)(2,1)} %gather_fusion.1) | data formatting | bytes 9331200 | tf_op jit(solution)/shard_map/jit(take_along_axis)/gather | solution.py:193
  193.3 11.1 %copy.92 = bf16[8,540,540]{1,0,2:T(8,128)(2,1)} copy(bf16[8,540,540]{2,1,0:T(8,128)(2,1)} %reshape.209) | data formatting | bytes 9331200 | tf_op jit(solution)/shard_map/jit(take_along_axis)/gather | solution.py:193
  204.4 5.6 %broadcast_select_fusion.1 = bf16[8,540,540]{1,0,2:T(8,128)(2,1)} fusion(bf16[8,540,540]{1,0,2:T(8,128)(2,1)} %copy.92, pred[8,540]{1,0:T(8,128)(4,1)S(1)} %compare_and_fusion), kind=kLoop, calls=%fused_computation.5 | loop fusion | flops 2332800 | bytes 9335520 | tf_op jit(solution)/shard_map/jit(take_along_axis)/select_n | solution.py:193
  214.3 6.6 %collective-permute-done.2 = bf16[1,3,3,81,128]{4,3,2,1,0:T(8,128)(2,1)S(1)} collective-permute-done((bf16[1,3,3,81,128]{4,3,2,1,0:T(8,128)(2,1)S(1)}, bf16[1,3,3,81,128]{4,3,2,1,0:T(8,128)(2,1)S(1)}, u32[]{:S(2)}, u32[]{:S(2)}) %collective-permute-start.2) | collective-permute-done | bytes 186656 | tf_op jit(solution)/shard_map/ppermute | solution.py:21
  221.1 3.1 concatenate.154
  224.2 4.2 %fusion.2 = f32[8,540,128]{2,1,0:T(8,128)S(1)} fusion(bf16[8,540,128]{2,1,0:T(8,128)(2,1)S(1)} %bitcast.25, bf16[8,540,540]{1,0,2:T(8,128)(2,1)} %broadcast_select_fusion.1), kind=kOutput, calls=%fused_computation.8 | convolution fusion | flops 597196800 | bytes 7983360 | tf_op jit(solution)/shard_map/vts,vsr->vtr/dot_general | solution.py:199
  231.9 4.4 %sort.35 = (s32[2,2,2,108]{2,3,1,0:T(8,128)}, s32[2,2,2,108]{2,3,1,0:T(8,128)}) sort(s32[2,2,2,108]{2,3,1,0:T(8,128)S(1)} %copy.78, s32[2,2,2,108]{2,3,1,0:T(8,128)S(1)} %iota.46), dimensions={3}, to_apply=%region_1.2 | sort | flops 8640 | bytes 13824 | tf_op jit(solution)/shard_map/jit(argsort)/sort | solution.py:120
  237.3 3.3 collective-permute-done.3
  242.9 10.7 %gather_fusion.2 = f32[864,108]{1,0:T(8,128)S(1)} fusion(f32[2,2,2,108,108]{4,2,3,1,0:T(2,128)S(1)} %copy-done, s32[864]{0:T(1024)S(1)} %reshape.186), kind=kCustom, calls=%fused_computation.2 | custom fusion | bytes 760320 | tf_op jit(solution)/shard_map/jit(take_along_axis)/gather | solution.py:121
  254.1 10.7 %gather_fusion.3 = f32[864,108]{1,0:T(8,128)S(1)} fusion(f32[2,2,2,108,108]{3,2,4,1,0:T(2,128)S(1)} %broadcast_select_fusion.2, s32[864]{0:T(1024)S(1)} %reshape.186), kind=kCustom, calls=%fused_computation.3 | custom fusion | bytes 760320 | tf_op jit(solution)/shard_map/jit(take_along_axis)/gather | solution.py:122
  267.9 6.7 %collective-permute-done.5 = f32[2,2,1,81,128]{4,3,2,1,0:T(8,128)S(1)} collective-permute-done((f32[2,2,1,81,128]{4,3,2,1,0:T(8,128)S(1)}, f32[2,2,1,81,128]{4,3,2,1,0:T(8,128)S(1)}, u32[]{:S(2)}, u32[]{:S(2)}) %collective-permute-start.5) | collective-permute-done | bytes 165920 | tf_op jit(solution)/shard_map/ppermute | solution.py:15
  277.5 2.5 collective-permute-start.6
  282.9 2.2 collective-permute-start.10
  285.1 4.5 %collective-permute-start.11 = (f32[2,2,1,9,128]{4,3,2,1,0:T(8,128)S(1)}, f32[2,2,1,9,128]{4,3,2,1,0:T(8,128)S(1)}, u32[]{:S(2)}, u32[]{:S(2)}) collective-permute-start(f32[2,2,1,9,128]{4,3,2,1,0:T(8,128)S(1)} %get-tuple-element.100), channel_id=1, source_target_pairs={{0,1},{1,2},{2,3},{4,5},{5,6},{6,7},{8,9},{9,10},{10,11},{12,13},{... | collective-permute-start | bytes 55304 | tf_op jit(solution)/shard_map/ppermute | solution.py:15
  289.7 2.3 collective-permute-start.9
  292.0 2.8 collective-permute-done.9
  295.0 3.5 collective-permute-start.12
  305.2 6.6 %collective-permute-done.14 = bf16[1,3,3,81,128]{4,3,2,1,0:T(8,128)(2,1)S(1)} collective-permute-done((bf16[1,3,3,81,128]{4,3,2,1,0:T(8,128)(2,1)S(1)}, bf16[1,3,3,81,128]{4,3,2,1,0:T(8,128)(2,1)S(1)}, u32[]{:S(2)}, u32[]{:S(2)}) %collective-permute-start.14) | collective-permute-done | bytes 186656 | tf_op jit(solution)/shard_map/ppermute | solution.py:21
  313.4 12.2 %concatenate.179 = bf16[2,2,2,540,128]{4,3,2,1,0:T(8,128)(2,1)S(1)} concatenate(bf16[2,2,2,54,128]{4,3,2,1,0:T(8,128)(2,1)} %get-tuple-element.73, bf16[2,2,2,54,128]{4,3,2,1,0:T(8,128)(2,1)} %get-tuple-element.72, bf16[2,2,2,54,128]{4,3,2,1,0:T(8,128)(2,1)} %get-tuple-element.71, bf16[2,2,2,54,128]{4,3,2,1,0:T(8,128)(2,1)} %get-tuple-element.70, ...), dimensions={3} | concatenate | bytes 2211840 | tf_op jit(solution)/shard_map/concatenate | solution.py:81
  325.6 4.2 %fusion = f32[8,540,128]{2,1,0:T(8,128)S(1)} fusion(bf16[8,540,128]{2,1,0:T(8,128)(2,1)S(1)} %bitcast.24, bf16[8,540,540]{1,0,2:T(8,128)(2,1)} %broadcast_select_fusion.1), kind=kOutput, calls=%fused_computation.6 | convolution fusion | flops 597196800 | bytes 7983360 | tf_op jit(solution)/shard_map/vts,vsr->vtr/dot_general | solution.py:199
  331.7 9.7 %collective-permute-done.15 = f32[1,3,3,81,128]{4,3,2,1,0:T(8,128)S(1)} collective-permute-done((f32[1,3,3,81,128]{4,3,2,1,0:T(8,128)S(1)}, f32[1,3,3,81,128]{4,3,2,1,0:T(8,128)S(1)}, u32[]{:S(2)}, u32[]{:S(2)}) %collective-permute-start.15) | collective-permute-done | bytes 373280 | tf_op jit(solution)/shard_map/ppermute | solution.py:21
  346.3 7.8 %collective-permute-done.17 = f32[2,2,1,81,128]{4,3,2,1,0:T(8,128)S(1)} collective-permute-done((f32[2,2,1,81,128]{4,3,2,1,0:T(8,128)S(1)}, f32[2,2,1,81,128]{4,3,2,1,0:T(8,128)S(1)}, u32[]{:S(2)}, u32[]{:S(2)}) %collective-permute-start.17) | collective-permute-done | bytes 165920 | tf_op jit(solution)/shard_map/ppermute | solution.py:15
  366.0 4.5 %collective-permute-start.23 = (f32[2,2,1,9,128]{4,3,2,1,0:T(8,128)S(1)}, f32[2,2,1,9,128]{4,3,2,1,0:T(8,128)S(1)}, u32[]{:S(2)}, u32[]{:S(2)}) collective-permute-start(f32[2,2,1,9,128]{4,3,2,1,0:T(8,128)S(1)} %get-tuple-element.90), channel_id=1, source_target_pairs={{0,1},{1,2},{2,3},{4,5},{5,6},{6,7},{8,9},{9,10},{10,11},{12,13},{... | collective-permute-start | bytes 55304 | tf_op jit(solution)/shard_map/ppermute | solution.py:15
  (156 shorter events, 51.8 us)
Async XLA Ops:
  0.6 242.2 %copy-start = (f32[2,2,2,108,108]{4,2,3,1,0:T(2,128)S(1)}, f32[2,2,2,108,108]{4,2,3,1,0:T(2,128)}, u32[]{:S(2)}) copy-start(f32[2,2,2,108,108]{4,2,3,1,0:T(2,128)} %param.8) | copy-start | bytes 1119748
  1.9 208.1 %collective-permute-start = (bf16[2,2,1,81,128]{4,3,2,1,0:T(8,128)(2,1)S(1)}, bf16[2,2,1,81,128]{4,3,2,1,0:T(8,128)(2,1)S(1)}, u32[]{:S(2)}, u32[]{:S(2)}) collective-permute-start(bf16[2,2,1,81,128]{4,3,2,1,0:T(8,128)(2,1)S(1)} %slice.636), channel_id=1, source_target_pairs={{0,1},{1,2},{2,3},{4,5},{5,6},{6,7},{8,9},{9,10},{10,11},{12,13},{... | collective-permute-start | bytes 248840 | tf_op jit(solution)/shard_map/ppermute | solution.py:15
  210.0 2.5 collective-permute-start.1
  212.6 8.3 %collective-permute-start.2 = (bf16[1,3,3,81,128]{4,3,2,1,0:T(8,128)(2,1)S(1)}, bf16[1,3,3,81,128]{4,3,2,1,0:T(8,128)(2,1)S(1)}, u32[]{:S(2)}, u32[]{:S(2)}) collective-permute-start(bf16[1,3,3,81,128]{4,3,2,1,0:T(8,128)(2,1)S(1)} %slice.639), channel_id=1, source_target_pairs={{24,0},{0,8},{8,16},{16,24},{25,1},{1,9},{9,17},{17,25},{26,2},{2,... | collective-permute-start | bytes 559880 | tf_op jit(solution)/shard_map/ppermute | solution.py:21
  228.5 0.7 copy-start.3
  229.7 1.7 copy-start.2
  229.8 10.8 %collective-permute-start.3 = (f32[1,3,3,81,128]{4,3,2,1,0:T(8,128)S(1)}, f32[1,3,3,81,128]{4,3,2,1,0:T(8,128)S(1)}, u32[]{:S(2)}, u32[]{:S(2)}) collective-permute-start(f32[1,3,3,81,128]{4,3,2,1,0:T(8,128)S(1)} %get-tuple-element.61), channel_id=1, source_target_pairs={{8,0},{16,8},{24,16},{0,24},{9,1},{17,9},{25,17},{1,25},{10,2},{18... | collective-permute-start | bytes 1119752 | tf_op jit(solution)/shard_map/ppermute | solution.py:21
  241.5 23.7 %collective-permute-start.4 = (f32[2,1,3,81,128]{4,3,2,1,0:T(8,128)}, f32[2,1,3,81,128]{4,3,2,1,0:T(8,128)}, u32[]{:S(2)}, u32[]{:S(2)}) collective-permute-start(f32[2,1,3,81,128]{4,3,2,1,0:T(8,128)} %get-tuple-element.65), channel_id=1, source_target_pairs={{4,0},{5,1},{6,2},{7,3},{12,8},{13,9},{14,10},{15,11},{20,16},{21,... | collective-permute-start | bytes 746504 | tf_op jit(solution)/shard_map/ppermute | solution.py:15
  266.2 8.5 %collective-permute-start.5 = (f32[2,2,1,81,128]{4,3,2,1,0:T(8,128)S(1)}, f32[2,2,1,81,128]{4,3,2,1,0:T(8,128)S(1)}, u32[]{:S(2)}, u32[]{:S(2)}) collective-permute-start(f32[2,2,1,81,128]{4,3,2,1,0:T(8,128)S(1)} %get-tuple-element.85), channel_id=1, source_target_pairs={{1,0},{2,1},{3,2},{5,4},{6,5},{7,6},{9,8},{10,9},{11,10},{13,12},{... | collective-permute-start | bytes 497672 | tf_op jit(solution)/shard_map/ppermute | solution.py:15
  274.8 5.9 %collective-permute-start.8 = (f32[2,2,1,9,128]{4,3,2,1,0:T(8,128)S(1)}, f32[2,2,1,9,128]{4,3,2,1,0:T(8,128)S(1)}, u32[]{:S(2)}, u32[]{:S(2)}) collective-permute-start(f32[2,2,1,9,128]{4,3,2,1,0:T(8,128)S(1)} %get-tuple-element.121), channel_id=1, source_target_pairs={{1,0},{2,1},{3,2},{5,4},{6,5},{7,6},{9,8},{10,9},{11,10},{13,12},{... | collective-permute-start | bytes 55304 | tf_op jit(solution)/shard_map/ppermute | solution.py:15
  276.2 4.5 %collective-permute-start.7 = (f32[2,1,2,9,128]{4,3,2,1,0:T(8,128)S(1)}, f32[2,1,2,9,128]{4,3,2,1,0:T(8,128)S(1)}, u32[]{:S(2)}, u32[]{:S(2)}) collective-permute-start(f32[2,1,2,9,128]{4,3,2,1,0:T(8,128)S(1)} %get-tuple-element.125), channel_id=1, source_target_pairs={{4,0},{5,1},{6,2},{7,3},{12,8},{13,9},{14,10},{15,11},{20,16},{21,... | collective-permute-start | bytes 55304 | tf_op jit(solution)/shard_map/ppermute | solution.py:15
  277.5 4.2 %collective-permute-start.6 = (f32[1,2,2,9,128]{4,3,2,1,0:T(8,128)S(1)}, f32[1,2,2,9,128]{4,3,2,1,0:T(8,128)S(1)}, u32[]{:S(2)}, u32[]{:S(2)}) collective-permute-start(f32[1,2,2,9,128]{4,3,2,1,0:T(8,128)S(1)} %get-tuple-element.127), channel_id=1, source_target_pairs={{8,0},{16,8},{24,16},{0,24},{9,1},{17,9},{25,17},{1,25},{10,2},{18... | collective-permute-start | bytes 55304 | tf_op jit(solution)/shard_map/ppermute | solution.py:21
  282.2 12.6 %copy-start.1 = (f32[2,2,2,81,128]{4,2,3,1,0:T(2,128)S(1)}, f32[2,2,2,81,128]{4,2,3,1,0:T(2,128)}, u32[]{:S(2)}) copy-start(f32[2,2,2,81,128]{4,2,3,1,0:T(2,128)} %param.5) | copy-start | bytes 995332
  282.9 9.1 %collective-permute-start.10 = (f32[2,1,2,9,128]{4,3,2,1,0:T(8,128)S(1)}, f32[2,1,2,9,128]{4,3,2,1,0:T(8,128)S(1)}, u32[]{:S(2)}, u32[]{:S(2)}) collective-permute-start(f32[2,1,2,9,128]{4,3,2,1,0:T(8,128)S(1)} %get-tuple-element.98), channel_id=1, source_target_pairs={{0,4},{1,5},{2,6},{3,7},{8,12},{9,13},{10,14},{11,15},{16,20},{17,... | collective-permute-start | bytes 55304 | tf_op jit(solution)/shard_map/ppermute | solution.py:15
  285.1 6.9 %collective-permute-start.11 = (f32[2,2,1,9,128]{4,3,2,1,0:T(8,128)S(1)}, f32[2,2,1,9,128]{4,3,2,1,0:T(8,128)S(1)}, u32[]{:S(2)}, u32[]{:S(2)}) collective-permute-start(f32[2,2,1,9,128]{4,3,2,1,0:T(8,128)S(1)} %get-tuple-element.100), channel_id=1, source_target_pairs={{0,1},{1,2},{2,3},{4,5},{5,6},{6,7},{8,9},{9,10},{10,11},{12,13},{... | collective-permute-start | bytes 55304 | tf_op jit(solution)/shard_map/ppermute | solution.py:15
  289.7 5.1 %collective-permute-start.9 = (f32[1,2,2,9,128]{4,3,2,1,0:T(8,128)S(1)}, f32[1,2,2,9,128]{4,3,2,1,0:T(8,128)S(1)}, u32[]{:S(2)}, u32[]{:S(2)}) collective-permute-start(f32[1,2,2,9,128]{4,3,2,1,0:T(8,128)S(1)} %get-tuple-element.96), channel_id=1, source_target_pairs={{24,0},{0,8},{8,16},{16,24},{25,1},{1,9},{9,17},{17,25},{26,2},{2,... | collective-permute-start | bytes 55304 | tf_op jit(solution)/shard_map/ppermute | solution.py:21
  295.0 5.6 %collective-permute-start.12 = (bf16[2,2,1,81,128]{4,3,2,1,0:T(8,128)(2,1)S(1)}, bf16[2,2,1,81,128]{4,3,2,1,0:T(8,128)(2,1)S(1)}, u32[]{:S(2)}, u32[]{:S(2)}) collective-permute-start(bf16[2,2,1,81,128]{4,3,2,1,0:T(8,128)(2,1)S(1)} %slice.703), channel_id=1, source_target_pairs={{0,1},{1,2},{2,3},{4,5},{5,6},{6,7},{8,9},{9,10},{10,11},{12,13},{... | collective-permute-start | bytes 248840 | tf_op jit(solution)/shard_map/ppermute | solution.py:15
  300.6 2.3 collective-permute-start.13
  303.6 8.2 %collective-permute-start.14 = (bf16[1,3,3,81,128]{4,3,2,1,0:T(8,128)(2,1)S(1)}, bf16[1,3,3,81,128]{4,3,2,1,0:T(8,128)(2,1)S(1)}, u32[]{:S(2)}, u32[]{:S(2)}) collective-permute-start(bf16[1,3,3,81,128]{4,3,2,1,0:T(8,128)(2,1)S(1)} %slice.706), channel_id=1, source_target_pairs={{24,0},{0,8},{8,16},{16,24},{25,1},{1,9},{9,17},{17,25},{26,2},{2,... | collective-permute-start | bytes 559880 | tf_op jit(solution)/shard_map/ppermute | solution.py:21
  330.6 10.8 %collective-permute-start.15 = (f32[1,3,3,81,128]{4,3,2,1,0:T(8,128)S(1)}, f32[1,3,3,81,128]{4,3,2,1,0:T(8,128)S(1)}, u32[]{:S(2)}, u32[]{:S(2)}) collective-permute-start(f32[1,3,3,81,128]{4,3,2,1,0:T(8,128)S(1)} %get-tuple-element.59), channel_id=1, source_target_pairs={{8,0},{16,8},{24,16},{0,24},{9,1},{17,9},{25,17},{1,25},{10,2},{18... | collective-permute-start | bytes 1119752 | tf_op jit(solution)/shard_map/ppermute | solution.py:21
  341.5 3.4 collective-permute-start.16
  345.0 9.1 %collective-permute-start.17 = (f32[2,2,1,81,128]{4,3,2,1,0:T(8,128)S(1)}, f32[2,2,1,81,128]{4,3,2,1,0:T(8,128)S(1)}, u32[]{:S(2)}, u32[]{:S(2)}) collective-permute-start(f32[2,2,1,81,128]{4,3,2,1,0:T(8,128)S(1)} %get-tuple-element.83), channel_id=1, source_target_pairs={{1,0},{2,1},{3,2},{5,4},{6,5},{7,6},{9,8},{10,9},{11,10},{13,12},{... | collective-permute-start | bytes 497672 | tf_op jit(solution)/shard_map/ppermute | solution.py:15
  354.4 5.8 %collective-permute-start.20 = (f32[2,2,1,9,128]{4,3,2,1,0:T(8,128)S(1)}, f32[2,2,1,9,128]{4,3,2,1,0:T(8,128)S(1)}, u32[]{:S(2)}, u32[]{:S(2)}) collective-permute-start(f32[2,2,1,9,128]{4,3,2,1,0:T(8,128)S(1)} %get-tuple-element.113), channel_id=1, source_target_pairs={{1,0},{2,1},{3,2},{5,4},{6,5},{7,6},{9,8},{10,9},{11,10},{13,12},{... | collective-permute-start | bytes 55304 | tf_op jit(solution)/shard_map/ppermute | solution.py:15
  355.7 4.5 %collective-permute-start.19 = (f32[2,1,2,9,128]{4,3,2,1,0:T(8,128)S(1)}, f32[2,1,2,9,128]{4,3,2,1,0:T(8,128)S(1)}, u32[]{:S(2)}, u32[]{:S(2)}) collective-permute-start(f32[2,1,2,9,128]{4,3,2,1,0:T(8,128)S(1)} %get-tuple-element.117), channel_id=1, source_target_pairs={{4,0},{5,1},{6,2},{7,3},{12,8},{13,9},{14,10},{15,11},{20,16},{21,... | collective-permute-start | bytes 55304 | tf_op jit(solution)/shard_map/ppermute | solution.py:15
  357.0 4.2 %collective-permute-start.18 = (f32[1,2,2,9,128]{4,3,2,1,0:T(8,128)S(1)}, f32[1,2,2,9,128]{4,3,2,1,0:T(8,128)S(1)}, u32[]{:S(2)}, u32[]{:S(2)}) collective-permute-start(f32[1,2,2,9,128]{4,3,2,1,0:T(8,128)S(1)} %get-tuple-element.119), channel_id=1, source_target_pairs={{8,0},{16,8},{24,16},{0,24},{9,1},{17,9},{25,17},{1,25},{10,2},{18... | collective-permute-start | bytes 55304 | tf_op jit(solution)/shard_map/ppermute | solution.py:21
  362.4 8.2 %collective-permute-start.21 = (f32[1,2,2,9,128]{4,3,2,1,0:T(8,128)S(1)}, f32[1,2,2,9,128]{4,3,2,1,0:T(8,128)S(1)}, u32[]{:S(2)}, u32[]{:S(2)}) collective-permute-start(f32[1,2,2,9,128]{4,3,2,1,0:T(8,128)S(1)} %get-tuple-element.86), channel_id=1, source_target_pairs={{24,0},{0,8},{8,16},{16,24},{25,1},{1,9},{9,17},{17,25},{26,2},{2,... | collective-permute-start | bytes 55304 | tf_op jit(solution)/shard_map/ppermute | solution.py:21
  364.3 6.4 %collective-permute-start.22 = (f32[2,1,2,9,128]{4,3,2,1,0:T(8,128)S(1)}, f32[2,1,2,9,128]{4,3,2,1,0:T(8,128)S(1)}, u32[]{:S(2)}, u32[]{:S(2)}) collective-permute-start(f32[2,1,2,9,128]{4,3,2,1,0:T(8,128)S(1)} %get-tuple-element.88), channel_id=1, source_target_pairs={{0,4},{1,5},{2,6},{3,7},{8,12},{9,13},{10,14},{11,15},{16,20},{17,... | collective-permute-start | bytes 55304 | tf_op jit(solution)/shard_map/ppermute | solution.py:15
  366.0 6.1 %collective-permute-start.23 = (f32[2,2,1,9,128]{4,3,2,1,0:T(8,128)S(1)}, f32[2,2,1,9,128]{4,3,2,1,0:T(8,128)S(1)}, u32[]{:S(2)}, u32[]{:S(2)}) collective-permute-start(f32[2,2,1,9,128]{4,3,2,1,0:T(8,128)S(1)} %get-tuple-element.90), channel_id=1, source_target_pairs={{0,1},{1,2},{2,3},{4,5},{5,6},{6,7},{8,9},{9,10},{10,11},{12,13},{... | collective-permute-start | bytes 55304 | tf_op jit(solution)/shard_map/ppermute | solution.py:15
where the time goes:
time: 377 us; the launch traced here: 373 us
  local copies, waits for them, and re-layouts  232 us (62%)
  waiting for transfers between devices  53.9 us (14%)
  starting transfers between devices  49 us (13%)
  other arithmetic  27.3 us (7%)
  matrix products  9.6 us (3%)
    gather x4, local copies, waits for them, and re-layouts, body(): inverses = jnp.take_along_axis(inverses, back[:, :, None], axis=1)  84.2 us
    gather x3, local copies, waits for them, and re-layouts, body(): inverses = jnp.take_along_axis(inverses, back[:, None, :], axis=2)  84 us
    ppermute x16, starting transfers between devices, passed_along(): lax.ppermute(value, axis, [(source, source + steps) for source in range(i...  35 us
    ppermute x8, waiting for transfers between devices, from_behind(): return lax.ppermute(block, axis, route)  30.9 us
    ppermute x16, waiting for transfers between devices, passed_along(): lax.ppermute(value, axis, [(source, source + steps) for source in range(i...  23 us
    concatenate x2, local copies, waits for them, and re-layouts, star_vectors(): return jnp.concatenate(pieces, axis=3)  15.3 us
    ppermute x8, starting transfers between devices, from_behind(): return lax.ppermute(block, axis, route)  14 us
    reshape x1, local copies, waits for them, and re-layouts, body(): inverses = patch_inverse.reshape(-1, PATCH, PATCH)  12.2 us
  transfers between devices with their start and end apart: 24, of which 16 were waited for; matrix products, arithmetic and copies ran while one was open for 63% of the time, Pallas kernels for 0%

commit v1 on v0

v1 whole, which is shorter than its diff:
```python
import functools
import itertools

import jax
import jax.numpy as jnp
import numpy as np
from jax import lax
from jax.experimental import pallas as pl
from jax.experimental.pallas import tpu as pltpu
from jax.sharding import PartitionSpec as P

INNER = 54
FACE = 9
OWN = INNER + 3 * FACE
LOCAL = INNER + 6 * FACE
SWEEPS = 2
PATCH = 540
SLOT = 96
WIDE = 8 * SLOT
AXES = ("gx", "gy", "gz")
CORNERS = tuple(itertools.product((0, 1), repeat=3))
X0, Y0, Z0 = INNER, INNER + FACE, INNER + 2 * FACE
f32, bf16 = jnp.float32, jnp.bfloat16
VMEM_LIMIT = 12 * 1024 * 1024


def wide_rows():
    rows = np.full((WIDE,), -1, np.int32)
    for a, b, c in CORNERS:
        m = 4 * a + 2 * b + c
        base = m * SLOT
        rows[base : base + INNER] = INNER * m + np.arange(INNER)
        starts = (2 * b + c, 4 + 2 * a + c, 8 + 2 * a + b)
        for d, face in enumerate(starts):
            low = base + INNER + d * FACE
            rows[low : low + FACE] = 8 * INNER + face * FACE + np.arange(FACE)
    return np.ascontiguousarray(np.broadcast_to(rows[:, None], (WIDE, 128)))


def prepare_kernel(inv, order, rows, mat, slot, wide, canon):
    hot = jnp.where(rows[:, :1] == order[0], 1.0, 0.0).astype(bf16)
    half = lax.dot_general(inv[0], hot, (((1,), (1,)), ((), ())), preferred_element_type=f32)
    wide[0] = jnp.dot(hot, half.astype(bf16), preferred_element_type=f32).astype(bf16)
    high = lax.Precision.HIGHEST
    index = lax.broadcasted_iota(jnp.int32, (LOCAL, LOCAL), 0)
    pick = jnp.where(index == slot[0], 1.0, 0.0).astype(f32)
    side = lax.dot_general(
        mat[0], pick, (((1,), (1,)), ((), ())), precision=high, preferred_element_type=f32
    )
    canon[0] = jnp.dot(pick, side, precision=high, preferred_element_type=f32)


def prepare(inverse, order, matrices, face_order):
    count = inverse.shape[0]
    offsets = (INNER + FACE * jnp.arange(6, dtype=jnp.int32))[:, None]
    slots = (face_order + offsets).reshape(count, 1, 6 * FACE)
    inner = jnp.broadcast_to(jnp.arange(INNER, dtype=jnp.int32), (count, 1, INNER))
    slots = jnp.concatenate([inner, slots], axis=2)
    flops = count * 2 * WIDE * PATCH * (PATCH + WIDE)
    one = lambda i: (i, 0, 0)
    return pl.pallas_call(
        prepare_kernel,
        grid=(count,),
        in_specs=[
            pl.BlockSpec((1, PATCH, PATCH), one),
            pl.BlockSpec((1, 1, PATCH), one),
            pl.BlockSpec((WIDE, 128), lambda i: (0, 0)),
            pl.BlockSpec((1, LOCAL, LOCAL), one),
            pl.BlockSpec((1, 1, LOCAL), one),
        ],
        out_specs=[
            pl.BlockSpec((1, WIDE, WIDE), one),
            pl.BlockSpec((1, LOCAL, LOCAL), one),
        ],
        out_shape=[
            jax.ShapeDtypeStruct((count, WIDE, WIDE), bf16),
            jax.ShapeDtypeStruct((count, LOCAL, LOCAL), f32),
        ],
        compiler_params=pltpu.CompilerParams(vmem_limit_bytes=VMEM_LIMIT),
        cost_estimate=pl.CostEstimate(
            flops=flops, bytes_accessed=count * 2 * (PATCH * PATCH + WIDE * WIDE), transcendentals=0
        ),
        name="prepare",
    )(inverse, order, jnp.asarray(wide_rows()), matrices, slots)


def call(kernel, operands, shapes, name):
    specs = [pl.BlockSpec(memory_space=pltpu.SMEM)]
    specs += [pl.BlockSpec(memory_space=pltpu.VMEM)] * (len(operands) - 1)
    return pl.pallas_call(
        kernel,
        in_specs=specs,
        out_specs=[pl.BlockSpec(memory_space=pltpu.VMEM)] * len(shapes),
        out_shape=[jax.ShapeDtypeStruct(s, t) for s, t in shapes],
        compiler_params=pltpu.CompilerParams(vmem_limit_bytes=VMEM_LIMIT),
        name=name,
    )(*operands)


def cat(*parts):
    return jnp.concatenate(parts, axis=0)


def zeros(rows, like):
    return jnp.zeros((rows, like.shape[-1]), f32)


def start_kernel(cells, flags, res, out, my):
    cx, cy, cz = cells
    for x, y, z in itertools.product(*map(range, cells)):
        e = (x * cy + y) * cz + z
        cur = res[e]
        if y == 0:
            cur = cat(cur[:Y0], cur[Y0:Z0] * flags[0], cur[Z0:])
        if z == 0:
            cur = cat(cur[:Z0], cur[Z0:] * flags[2])
        out[e] = cur
        if y == cy - 1:
            nine, rest = zeros(FACE, cur), zeros(112 - OWN, cur)
            my[x * cz + z] = cat(cur[:Y0], nine, cur[Z0:], rest).astype(bf16)


def spread_kernel(cells, terms, *refs):
    cx, cy, cz = cells
    if terms:
        flags, res, yr, tx, tz, out, mx, mz, mxz = refs
    else:
        flags, res, yr, out, mx, mz, mxz = refs
    for x, z in itertools.product(range(cx), range(cz)):
        lastx, lastz = x == cx - 1, z == cz - 1
        halo = yr[0, x * cz + z].astype(f32) * flags[0]
        nine = zeros(FACE, halo)
        if lastx:
            mx[z] = cat(halo[:X0], halo[81:90], nine, halo[Z0:OWN]).astype(bf16)
        if lastz:
            mz[x * (cy + 1)] = cat(halo[:Y0], nine, halo[90:99]).astype(bf16)
        if lastx and lastz:
            mxz[0] = cat(halo[:X0], halo[81:90], nine, halo[90:99]).astype(bf16)
        for y in range(cy):
            e = (x * cy + y) * cz + z
            cur = res[e]
            if y == 0 and terms:
                cur = cat(cur[:Y0], cur[Y0:Z0] + halo[Y0:Z0], cur[Z0:])
            out[e] = cur
            upx = tx[y * cz + z][:FACE] if terms and lastx else nine
            upz = tz[x * cy + y][:FACE] if terms and lastz else nine
            if lastx:
                mx[(y + 1) * cz + z] = cat(cur[:X0], upx, cur[Y0:]).astype(bf16)
            if lastz:
                mz[x * (cy + 1) + y + 1] = cat(cur[:Z0], upz).astype(bf16)
            if lastx and lastz:
                mxz[y + 1] = cat(cur[:X0], upx, cur[Y0:Z0], upz).astype(bf16)


def solve_kernel(cells, flags, wide, res, yr, hx, hz, hxz, c, ox, oz, oxz, stars, solved):
    cx, cy, cz = cells
    step = pl.program_id(0)

    @pl.when(step == 0)
    def _():
        found = {}
        for e in itertools.product(range(-1, cx), range(-1, cy), range(-1, cz)):
            x, y, z = e
            if x < 0 and z < 0:
                val = hxz[y + 1].astype(f32)
            elif x < 0:
                val = hx[(y + 1) * cz + z].astype(f32)
            elif z < 0:
                val = hz[x * (cy + 1) + y + 1].astype(f32)
            elif y < 0:
                val = yr[0, x * cz + z].astype(f32)[:OWN] * flags[0]
            else:
                val = res[(x * cy + y) * cz + z]
            found[e] = val
        for n, v in enumerate(itertools.product(*map(range, cells))):
            for a, b, g in CORNERS:
                x, y, z = v[0] - 1 + a, v[1] - 1 + b, v[2] - 1 + g
                val = found[(x, y, z)]
                nine = zeros(FACE, val)
                part = cat(
                    val[:X0],
                    val[X0:Y0] if a or x < 0 else nine,
                    val[Y0:Z0] if b else nine,
                    val[Z0:] if g or z < 0 else nine,
                    zeros(SLOT - OWN, val),
                )
                m = 4 * a + 2 * b + g
                stars[n, m * SLOT : (m + 1) * SLOT] = part.astype(bf16)

    solved[step] = jnp.dot(wide[0], stars[step], preferred_element_type=f32)

    @pl.when(step == pl.num_programs(0) - 1)
    def _():
        vertices = list(itertools.product(*map(range, cells)))
        for e in itertools.product(range(-1, cx), range(-1, cy), range(-1, cz)):
            parts = []
            for n, v in enumerate(vertices):
                m = tuple(e[d] - v[d] + 1 for d in range(3))
                if all(k in (0, 1) for k in m):
                    parts.append((n, m))

            def total(low, high, keep):
                acc = None
                for n, m in parts:
                    if keep(m):
                        base = (4 * m[0] + 2 * m[1] + m[2]) * SLOT
                        val = solved[n, base + low : base + high]
                        acc = val if acc is None else acc + val
                return acc

            pieces = [total(0, X0, lambda m: True)]
            for d in range(3):
                low = INNER + d * FACE
                pieces.append(total(low, low + FACE, lambda m: e[d] < 0 or m[d] == 1))
            val = cat(*pieces)
            x, y, z = e
            if x < 0 and z < 0:
                oxz[y + 1] = val.astype(bf16)
            elif x < 0:
                ox[(y + 1) * cz + z] = val.astype(bf16)
            elif z < 0:
                oz[x * (cy + 1) + y + 1] = val.astype(bf16)
            else:
                c[(x * (cy + 1) + y + 1) * cz + z] = val


def solve(cells, flags, wide, res, yr, hx, hz, hxz):
    cx, cy, cz = cells
    count, columns = wide.shape[0], res.shape[-1]
    whole = lambda a: pl.BlockSpec(a.shape, lambda i, n=a.ndim: (0,) * n)
    shapes = [
        jax.ShapeDtypeStruct((cx * (cy + 1) * cz, OWN, columns), f32),
        jax.ShapeDtypeStruct(hx.shape, bf16),
        jax.ShapeDtypeStruct(hz.shape, bf16),
        jax.ShapeDtypeStruct(hxz.shape, bf16),
    ]
    return pl.pallas_call(
        functools.partial(solve_kernel, cells),
        grid=(count,),
        in_specs=[
            pl.BlockSpec(memory_space=pltpu.SMEM),
            pl.BlockSpec((1, WIDE, WIDE), lambda i: (i, 0, 0)),
        ]
        + [whole(a) for a in (res, yr, hx, hz, hxz)],
        out_specs=[whole(s) for s in shapes],
        out_shape=shapes,
        scratch_shapes=[
            pltpu.VMEM((count, WIDE, columns), bf16),
            pltpu.VMEM((count, WIDE, columns), f32),
        ],
        compiler_params=pltpu.CompilerParams(vmem_limit_bytes=VMEM_LIMIT),
        name="solve",
    )(flags, wide, res, yr, hx, hz, hxz)


def add_received(val, x, y, z, cells, gx, gz, gxz):
    cx, cy, cz = cells
    nine = zeros(FACE, val)
    if x == cx - 1:
        got = gx[(y + 1) * cz + z].astype(f32)
        val = val + cat(got[:X0], nine, got[Y0:])
    if z == cz - 1:
        got = gz[x * (cy + 1) + y + 1].astype(f32)
        val = val + cat(got[:Z0], nine)
    if x == cx - 1 and z == cz - 1:
        got = gxz[y + 1].astype(f32)
        val = val + cat(got[:X0], nine, got[Y0:Z0], nine)
    return val


def upper_x(y, z, cells, gx, gxz):
    val = gx[(y + 1) * cells[2] + z].astype(f32)[X0:Y0]
    if z == cells[2] - 1:
        val = val + gxz[y + 1].astype(f32)[X0:Y0]
    return val


def upper_z(x, y, cells, gz, gxz):
    val = gz[x * (cells[1] + 1) + y + 1].astype(f32)[Z0:]
    if x == cells[0] - 1:
        val = val + gxz[y + 1].astype(f32)[Z0:]
    return val


def reduce_kernel(cells, flags, c, gx, gz, gxz, out):
    cx, cy, cz = cells
    for x, z in itertools.product(range(cx), range(cz)):
        val = add_received(c[x * (cy + 1) * cz + z], x, -1, z, cells, gx, gz, gxz)
        nine = zeros(FACE, val)
        upx = upper_x(-1, z, cells, gx, gxz) if x == cx - 1 else nine
        upz = upper_z(x, -1, cells, gz, gxz) if z == cz - 1 else nine
        out[x * cz + z] = cat(val, upx, upz, zeros(104 - OWN - 2 * FACE, val))


def element_kernel(cells, first, last, *refs):
    cx, cy, cz = cells
    flags, c, gx, gz, gxz, yr, mat, res, hx, hz = refs[:10]
    refs = refs[10:]
    if not first:
        prev, refs = refs[0], refs[1:]
    sol, out, tx, tz, my = refs
    peer = yr.shape[0] - 1
    own, images = {}, {}
    for e in itertools.product(*map(range, cells)):
        x, y, z = e
        n = (x * cy + y) * cz + z
        val = add_received(c[(x * (cy + 1) + y + 1) * cz + z], x, y, z, cells, gx, gz, gxz)
        if y == cy - 1:
            got = yr[peer, x * cz + z][:OWN] * flags[1]
            val = val + cat(got[:Y0], zeros(FACE, val), got[Z0:])
        if y == 0:
            val = cat(val[:Y0], val[Y0:Z0] * flags[0], val[Z0:])
        if z == 0:
            val = cat(val[:Z0], val[Z0:] * flags[2])
        own[e] = val
        sol[n] = val if first else prev[n] + val
    for e in itertools.product(*map(range, cells)):
        x, y, z = e
        if x < cx - 1:
            upx = own[(x + 1, y, z)][X0:Y0]
        else:
            upx = upper_x(y, z, cells, gx, gxz)
            if y == cy - 1:
                upx = upx + yr[peer, x * cz + z][81:90] * flags[1]
        if y < cy - 1:
            upy = own[(x, y + 1, z)][Y0:Z0]
        else:
            upy = yr[peer, x * cz + z][Y0:Z0] * flags[1]
        if z < cz - 1:
            upz = own[(x, y, z + 1)][Z0:]
        else:
            upz = upper_z(x, y, cells, gz, gxz)
            if y == cy - 1:
                upz = upz + yr[peer, x * cz + z][90:99] * flags[1]
        val = own[e]
        local = cat(val[:Y0], upx, val[Y0:Z0], upy, val[Z0:], upz)
        images[e] = jnp.dot(
            mat[(x * cy + y) * cz + z],
            local,
            precision=lax.Precision.HIGHEST,
            preferred_element_type=f32,
        )
    for e in itertools.product(*map(range, cells)):
        x, y, z = e
        n = (x * cy + y) * cz + z
        old, image = res[n], images[e]
        lowx = old[X0:Y0] - image[54:63]
        lowy = old[Y0:Z0] - image[72:81]
        lowz = old[Z0:] - image[90:99]
        if x > 0:
            lowx = lowx - images[(x - 1, y, z)][63:72]
        else:
            lowx = lowx + hx[(y + 1) * cz + z].astype(f32)[X0:Y0]
        if y > 0:
            lowy = lowy - images[(x, y - 1, z)][81:90]
        else:
            lowy = lowy * flags[0]
        if z > 0:
            lowz = lowz - images[(x, y, z - 1)][99:108]
        else:
            lowz = (lowz + hz[x * (cy + 1) + y + 1].astype(f32)[Z0:]) * flags[2]
        val = cat(old[:X0] - image[:X0], lowx, lowy, lowz)
        out[n] = val
        nine, seven = zeros(FACE, val), zeros(16 - FACE, val)
        upx, upy, upz = -image[63:72], -image[81:90], -image[99:108]
        if x == cx - 1:
            tx[y * cz + z] = cat(upx, seven)
        if z == cz - 1:
            tz[x * cy + y] = cat(upz, seven)
        if y == cy - 1 and last:
            my[x * cz + z] = cat(upy, seven)
        elif y == cy - 1:
            my[x * cz + z] = cat(
                val[:Y0],
                upy,
                val[Z0:],
                upx if x == cx - 1 else nine,
                upz if z == cz - 1 else nine,
                zeros(112 - OWN - 2 * FACE, val),
            ).astype(bf16)


def finish_kernel(cells, flags, res, fx, fy, fz, out):
    cx, cy, cz = cells
    for x, y, z in itertools.product(*map(range, cells)):
        n = (x * cy + y) * cz + z
        cur = res[n]
        lowx, lowy, lowz = cur[X0:Y0], cur[Y0:Z0], cur[Z0:]
        if x == 0:
            lowx = lowx + fx[y * cz + z][:FACE]
        if y == 0:
            lowy = lowy + fy[0, x * cz + z][:FACE] * flags[0]
        if z == 0:
            lowz = lowz + fz[x * cy + y][:FACE]
        out[n] = cat(cur[:X0], lowx, lowy, lowz)


def route(offset):
    sizes = [lax.axis_size(a) for a in AXES]
    flat = lambda c: (c[0] * sizes[1] + c[1]) * sizes[2] + c[2]
    pairs = []
    for spot in itertools.product(*map(range, sizes)):
        aim = [s + o for s, o in zip(spot, offset)]
        aim[0] %= sizes[0]
        if all(0 <= a < s for a, s in zip(aim, sizes)):
            pairs.append((flat(spot), flat(aim)))
    return pairs


def send_xz(mx, mz, mxz, sign):
    return (
        lax.ppermute(mx, AXES, route((sign, 0, 0))),
        lax.ppermute(mz, AXES, route((0, 0, sign))),
        lax.ppermute(mxz, AXES, route((sign, 0, sign))),
    )


def send_y(my, sign):
    if lax.axis_size("gy") == 2:
        return lax.all_gather(my, "gy")
    return lax.ppermute(my, AXES, route((0, sign, 0)))[None]


def body(residual_start, patch_inverse, patch_order, element_matrix, face_order):
    cells = cx, cy, cz = residual_start.shape[:3]
    if min(cells) < 2:
        raise ValueError(cells)
    columns = residual_start.shape[4]
    count = cx * cy * cz
    at_y, at_z = lax.axis_index("gy"), lax.axis_index("gz")
    flags = jnp.stack([at_y > 0, at_y < lax.axis_size("gy") - 1, at_z > 0]).astype(f32)
    bind = lambda kernel, *extra: functools.partial(kernel, cells, *extra)
    state = ((count, OWN, columns), f32)
    sent = (
        (((cy + 1) * cz, OWN, columns), bf16),
        ((cx * (cy + 1), OWN, columns), bf16),
        ((cy + 1, OWN, columns), bf16),
    )
    term_x, term_y, term_z = (((n, 16, columns), f32) for n in (cy * cz, cx * cz, cx * cy))
    rim = ((cx * cz, 112, columns), bf16)

    start = residual_start.reshape(count, OWN, columns)
    residual, my = call(bind(start_kernel), [flags, start], [state, rim], "start")
    wide, canon = prepare(
        patch_inverse.reshape(count, PATCH, PATCH),
        patch_order.reshape(count, 1, PATCH),
        element_matrix.reshape(count, LOCAL, LOCAL),
        face_order,
    )
    terms, solution = [], []
    for sweep in range(SWEEPS):
        first, last = sweep == 0, sweep == SWEEPS - 1
        yr = send_y(my, 1)
        residual, mx, mz, mxz = call(
            bind(spread_kernel, not first), [flags, residual, yr] + terms, [state, *sent], "spread"
        )
        hx, hz, hxz = send_xz(mx, mz, mxz, 1)
        c, ox, oz, oxz = solve(cells, flags, wide, residual, yr, hx, hz, hxz)
        gx, gz, gxz = send_xz(ox, oz, oxz, -1)
        (down,) = call(
            bind(reduce_kernel), [flags, c, gx, gz, gxz], [((cx * cz, 104, columns), f32)], "reduce"
        )
        back = send_y(down, -1)
        total, residual, tx, tz, my = call(
            bind(element_kernel, first, last),
            [flags, c, gx, gz, gxz, back, canon, residual, hx, hz] + solution,
            [state, state, term_x, term_z, term_y if last else rim],
            "element",
        )
        terms, solution = [tx, tz], [total]
    fx = lax.ppermute(tx, AXES, route((1, 0, 0)))
    fz = lax.ppermute(tz, AXES, route((0, 0, 1)))
    fy = send_y(my, 1)
    (residual,) = call(bind(finish_kernel), [flags, residual, fx, fy, fz], [state], "finish")
    shape = residual_start.shape
    return total.reshape(shape), residual.reshape(shape)


def solution(mesh):
    return jax.shard_map(
        body,
        mesh=mesh,
        in_specs=(
            P("gx", "gy", "gz", None, None),
            P("gx", "gy", "gz", None, None),
            P("gx", "gy", "gz", None),
            P("gx", "gy", "gz", None, None),
            P("gx", "gy", "gz", None, None),
        ),
        out_specs=(P("gx", "gy", "gz", None, None), P("gx", "gy", "gz", None, None)),
        check_vma=False,
    )
```

time: 377 us -> 105 us (0.28)
  local copies, waits for them, and re-layouts: 232 us -> 11.3 us
  waiting for transfers between devices: 53.9 us -> 14.5 us
  Pallas kernels: 0 us -> 32.1 us
  other arithmetic: 27.3 us -> 0.24 us
  starting transfers between devices: 49 us -> 35.7 us
  blocking collectives: 0 us -> 10.1 us
  matrix products: 9.6 us -> 0 us
    gather x14 -> x0, local copies, waits for them, and re-layouts: 190 us -> none  [the longest x4 84.2 us: body(): inverses = jnp.take_along_axis(inverses, back[:, :, None], axis=1)]
    ppermute x24 -> x14, waiting for transfers between devices: 53.9 us -> 14.5 us  [the longest x4 14.4 us: send_xz(): lax.ppermute(mxz, AXES, route((sign, 0, sign)))]
    pallas_call x0 -> x11, Pallas kernels: none -> 32.1 us  [the longest x1 16.7 us: prepare(): pl.pallas_call(prepare_kernel, grid=(count,), in_specs=[pl.BlockSpec((1,...]
    concatenate x6 -> x0, local copies, waits for them, and re-layouts: 16.7 us -> none  [the longest x2 15.3 us: star_vectors(): return jnp.concatenate(pieces, axis=3)]
    ppermute x24 -> x14, starting transfers between devices: 49 us -> 35.7 us  [the longest x4 11.4 us: send_xz(): lax.ppermute(mxz, AXES, route((sign, 0, sign)))]
    reshape x3 -> x2, local copies, waits for them, and re-layouts: 13 us -> 0.11 us  [the longest x1 0.08 us: prepare(): slots = (face_order + offsets).reshape(count, 1, 6 * FACE)]
    select_n x5 -> x0, other arithmetic: 11.5 us -> none  [the longest x1 5.59 us: body(): inverses = jnp.take_along_axis(inverses, back[:, None, :], axis=2)]
    all_gather x0 -> x5, blocking collectives: none -> 10.1 us  [send_y(): return lax.all_gather(my, 'gy')]
  transfers between devices with their start and end apart: 24 -> 14, of which waited for: 16 -> 3; matrix products, arithmetic and copies ran while one was open for 63% -> 7% of each run, Pallas kernels for 0% -> 16%
where the time goes in v1:
time: 105 us
  starting transfers between devices  35.7 us (34%)
  Pallas kernels  32.1 us (31%)
  waiting for transfers between devices  14.5 us (14%)
  local copies, waits for them, and re-layouts  11.3 us (11%)
  blocking collectives  10.1 us (10%)
    pallas_call x1, Pallas kernels, prepare(): pl.pallas_call(prepare_kernel, grid=(count,), in_specs=[pl.BlockSpec((1,...  16.7 us
    ppermute x4, waiting for transfers between devices, send_xz(): lax.ppermute(mxz, AXES, route((sign, 0, sign)))  14.4 us
    ppermute x4, starting transfers between devices, send_xz(): lax.ppermute(mxz, AXES, route((sign, 0, sign)))  11.4 us
    unnamed x15, local copies, waits for them, and re-layouts  11.2 us
    all_gather x5, blocking collectives, send_y(): return lax.all_gather(my, 'gy')  10.1 us
    ppermute x4, starting transfers between devices, send_xz(): lax.ppermute(mz, AXES, route((0, 0, sign)))  9.69 us
    pallas_call x2, Pallas kernels, solve(): pl.pallas_call(functools.partial(solve_kernel, cells), grid=(count,), in_...  9.61 us
    ppermute x4, starting transfers between devices, send_xz(): lax.ppermute(mx, AXES, route((sign, 0, 0)))  8.29 us
  transfers between devices with their start and end apart: 14, of which 3 were waited for; matrix products, arithmetic and copies ran while one was open for 7% of the time, Pallas kernels for 16%

profile of v1, /device:TPU:0, one launch (start us, length us, event | category | flops | bytes accessed | tf_op | source)
XLA Modules:
  0.0 104.9 jit_solution(3332276966566534084)
XLA Ops:
  0.6 1.0 copy.25
  2.3 2.1 %all-gather = bf16[8,112,128]{2,1,0:T(8,128)(2,1)S(1)} all-gather(bf16[4,112,128]{2,1,0:T(8,128)(2,1)S(1)} %get-tuple-element.34), channel_id=2, replica_groups=mesh['gx'=4,'gy'=2,'gz'=4] {'gy'}, dimensions={0}, use_global_device_ids=true | all-gather | bytes 344064 | tf_op jit(solution)/shard_map/all_gather | solution.py:420
  5.0 2.9 %collective-permute-start = (bf16[6,81,128]{2,1,0:T(8,128)(2,1)S(1)}, bf16[6,81,128]{2,1,0:T(8,128)(2,1)S(1)}, u32[]{:S(2)}, u32[]{:S(2)}) collective-permute-start(bf16[6,81,128]{2,1,0:T(8,128)(2,1)S(1)} %get-tuple-element.36), channel_id=1, source_target_pairs={{0,8},{1,9},{2,10},{3,11},{4,12},{5,13},{6,14},{7,15},{8,16},{9,17... | collective-permute-start | bytes 373256 | tf_op jit(solution)/shard_map/ppermute | solution.py:412
  7.9 3.5 %collective-permute-start.1 = (bf16[6,81,128]{2,1,0:T(8,128)(2,1)S(1)}, bf16[6,81,128]{2,1,0:T(8,128)(2,1)S(1)}, u32[]{:S(2)}, u32[]{:S(2)}) collective-permute-start(bf16[6,81,128]{2,1,0:T(8,128)(2,1)S(1)} %get-tuple-element.37), channel_id=1, source_target_pairs={{0,1},{1,2},{2,3},{4,5},{5,6},{6,7},{8,9},{9,10},{10,11},{12,13},{... | collective-permute-start | bytes 373256 | tf_op jit(solution)/shard_map/ppermute | solution.py:413
  11.4 4.4 %collective-permute-start.2 = (bf16[3,81,128]{2,1,0:T(8,128)(2,1)S(1)}, bf16[3,81,128]{2,1,0:T(8,128)(2,1)S(1)}, u32[]{:S(2)}, u32[]{:S(2)}) collective-permute-start(bf16[3,81,128]{2,1,0:T(8,128)(2,1)S(1)} %get-tuple-element.38), channel_id=1, source_target_pairs={{0,9},{1,10},{2,11},{4,13},{5,14},{6,15},{8,17},{9,18},{10,19},{12... | collective-permute-start | bytes 186632 | tf_op jit(solution)/shard_map/ppermute | solution.py:414
  15.9 5.8 %copy.21 = bf16[2,2,2,540,540]{4,3,2,1,0:T(8,128)(2,1)} copy(bf16[2,2,2,540,540]{4,2,3,1,0:T(2,128)(2,1)} %param.7) | data formatting | bytes 9331200 | tf_op args[1]
  22.0 2.6 %copy-done = bf16[2,2,2,540,540]{4,3,2,1,0:T(8,128)(2,1)S(1)} copy-done((bf16[2,2,2,540,540]{4,3,2,1,0:T(8,128)(2,1)S(1)}, bf16[2,2,2,540,540]{4,3,2,1,0:T(8,128)(2,1)}, u32[]{:S(2)}) %copy-start) | copy-done | bytes 4665624
  24.6 16.7 %prepare.1 = (bf16[8,768,768]{2,1,0:T(8,128)(2,1)S(1)}, f32[8,108,108]{2,1,0:T(8,128)S(1)}) custom-call(bf16[8,540,540]{2,1,0:T(8,128)(2,1)S(1)} %bitcast.14, s32[8,1,540]{2,1,0:T(1,128)S(1)} %reshape.31.order, s32[768,128]{1,0:T(8,128)S(1)} %copy-done.1, f32[8,108,108]{2,1,0:T(8,128)S(1)} %bitcast.23, s32[8,1,108]{2,1,0:T(1,128)S(1)} %pad_add_fusion.slot), custom_call_target="tpu_custom_call" | custom-call | flops 8679260160 | bytes 14102784 | tf_op jit(solution)/shard_map/prepare/pallas_call | solution.py:61
  41.4 4.8 %solve.2 = (f32[12,81,128]{2,1,0:T(8,128)S(1)}, bf16[6,81,128]{2,1,0:T(8,128)(2,1)S(1)}, bf16[6,81,128]{2,1,0:T(8,128)(2,1)S(1)}, bf16[3,81,128]{2,1,0:T(8,128)(2,1)S(1)}) custom-call(f32[3]{0:T(128)S(1)} %add_convert_fusion.flags.refs_0_, bf16[8,768,768]{2,1,0:T(8,128)(2,1)S(1)} %get-tuple-element.32.wide, f32[8,81,128]{2,1,0:T(8,128)S(1)} %get-tuple-element.35.res.refs_7_, ...), custom_call_target="tpu_custom_call" | custom-call | tf_op jit(solution)/shard_map/solve/pallas_call | solution.py:237
  46.2 1.5 %collective-permute-start.3 = (bf16[6,81,128]{2,1,0:T(8,128)(2,1)S(1)}, bf16[6,81,128]{2,1,0:T(8,128)(2,1)S(1)}, u32[]{:S(2)}, u32[]{:S(2)}) collective-permute-start(bf16[6,81,128]{2,1,0:T(8,128)(2,1)S(1)} %get-tuple-element.40), channel_id=1, source_target_pairs={{0,24},{1,25},{2,26},{3,27},{4,28},{5,29},{6,30},{7,31},{8,0},{9,1... | collective-permute-start | bytes 373256 | tf_op jit(solution)/shard_map/ppermute | solution.py:412
  47.7 1.3 %collective-permute-start.4 = (bf16[6,81,128]{2,1,0:T(8,128)(2,1)S(1)}, bf16[6,81,128]{2,1,0:T(8,128)(2,1)S(1)}, u32[]{:S(2)}, u32[]{:S(2)}) collective-permute-start(bf16[6,81,128]{2,1,0:T(8,128)(2,1)S(1)} %get-tuple-element.41), channel_id=1, source_target_pairs={{1,0},{2,1},{3,2},{5,4},{6,5},{7,6},{9,8},{10,9},{11,10},{13,12},{... | collective-permute-start | bytes 373256 | tf_op jit(solution)/shard_map/ppermute | solution.py:413
  49.0 1.3 %collective-permute-start.5 = (bf16[3,81,128]{2,1,0:T(8,128)(2,1)S(1)}, bf16[3,81,128]{2,1,0:T(8,128)(2,1)S(1)}, u32[]{:S(2)}, u32[]{:S(2)}) collective-permute-start(bf16[3,81,128]{2,1,0:T(8,128)(2,1)S(1)} %get-tuple-element.42), channel_id=1, source_target_pairs={{1,24},{2,25},{3,26},{5,28},{6,29},{7,30},{9,0},{10,1},{11,2},{13,... | collective-permute-start | bytes 186632 | tf_op jit(solution)/shard_map/ppermute | solution.py:414
  50.3 5.8 %collective-permute-done.5.gxz.refs_4_ = bf16[3,81,128]{2,1,0:T(8,128)(2,1)S(1)} collective-permute-done((bf16[3,81,128]{2,1,0:T(8,128)(2,1)S(1)}, bf16[3,81,128]{2,1,0:T(8,128)(2,1)S(1)}, u32[]{:S(2)}, u32[]{:S(2)}) %collective-permute-start.5) | collective-permute-done | bytes 62240 | tf_op jit(solution)/shard_map/ppermute | solution.py:414
  56.6 2.1 %all-gather.1 = f32[8,104,128]{2,1,0:T(8,128)S(1)} all-gather(f32[4,104,128]{2,1,0:T(8,128)S(1)} %reduce.2), channel_id=3, replica_groups=mesh['gx'=4,'gy'=2,'gz'=4] {'gy'}, dimensions={0}, use_global_device_ids=true | all-gather | bytes 638976 | tf_op jit(solution)/shard_map/all_gather | solution.py:420
  58.7 1.1 %element.2 = (f32[8,81,128]{2,1,0:T(8,128)S(1)}, f32[8,81,128]{2,1,0:T(8,128)S(1)}, f32[4,16,128]{2,1,0:T(8,128)S(1)}, f32[4,16,128]{2,1,0:T(8,128)S(1)}, bf16[4,112,128]{2,1,0:T(8,128)(2,1)S(1)}) custom-call(f32[3]{0:T(128)S(1)} %add_convert_fusion.flags.refs_0_, f32[12,81,128]{2,1,0:T(8,128)S(1)} %get-tuple-element.39.c.refs_1_, ...), custom_call_target="tpu_custom_call" | custom-call | tf_op jit(solution)/shard_map/element/pallas_call | solution.py:90
  59.9 2.0 %all-gather.2 = bf16[8,112,128]{2,1,0:T(8,128)(2,1)S(1)} all-gather(bf16[4,112,128]{2,1,0:T(8,128)(2,1)S(1)} %get-tuple-element.45), channel_id=4, replica_groups=mesh['gx'=4,'gy'=2,'gz'=4] {'gy'}, dimensions={0}, use_global_device_ids=true | all-gather | bytes 344064 | tf_op jit(solution)/shard_map/all_gather | solution.py:420
  62.5 2.4 %collective-permute-start.6 = (bf16[6,81,128]{2,1,0:T(8,128)(2,1)S(1)}, bf16[6,81,128]{2,1,0:T(8,128)(2,1)S(1)}, u32[]{:S(2)}, u32[]{:S(2)}) collective-permute-start(bf16[6,81,128]{2,1,0:T(8,128)(2,1)S(1)} %get-tuple-element.49), channel_id=1, source_target_pairs={{0,8},{1,9},{2,10},{3,11},{4,12},{5,13},{6,14},{7,15},{8,16},{9,17... | collective-permute-start | bytes 373256 | tf_op jit(solution)/shard_map/ppermute | solution.py:412
  64.9 3.7 %collective-permute-start.7 = (bf16[6,81,128]{2,1,0:T(8,128)(2,1)S(1)}, bf16[6,81,128]{2,1,0:T(8,128)(2,1)S(1)}, u32[]{:S(2)}, u32[]{:S(2)}) collective-permute-start(bf16[6,81,128]{2,1,0:T(8,128)(2,1)S(1)} %get-tuple-element.50), channel_id=1, source_target_pairs={{0,1},{1,2},{2,3},{4,5},{5,6},{6,7},{8,9},{9,10},{10,11},{12,13},{... | collective-permute-start | bytes 373256 | tf_op jit(solution)/shard_map/ppermute | solution.py:413
  68.5 4.4 %collective-permute-start.8 = (bf16[3,81,128]{2,1,0:T(8,128)(2,1)S(1)}, bf16[3,81,128]{2,1,0:T(8,128)(2,1)S(1)}, u32[]{:S(2)}, u32[]{:S(2)}) collective-permute-start(bf16[3,81,128]{2,1,0:T(8,128)(2,1)S(1)} %get-tuple-element.51), channel_id=1, source_target_pairs={{0,9},{1,10},{2,11},{4,13},{5,14},{6,15},{8,17},{9,18},{10,19},{12... | collective-permute-start | bytes 186632 | tf_op jit(solution)/shard_map/ppermute | solution.py:414
  73.0 1.9 %collective-permute-done.8.hxz = bf16[3,81,128]{2,1,0:T(8,128)(2,1)S(1)} collective-permute-done((bf16[3,81,128]{2,1,0:T(8,128)(2,1)S(1)}, bf16[3,81,128]{2,1,0:T(8,128)(2,1)S(1)}, u32[]{:S(2)}, u32[]{:S(2)}) %collective-permute-start.8) | collective-permute-done | bytes 62240 | tf_op jit(solution)/shard_map/ppermute | solution.py:414
  74.9 4.8 %solve.3 = (f32[12,81,128]{2,1,0:T(8,128)S(1)}, bf16[6,81,128]{2,1,0:T(8,128)(2,1)S(1)}, bf16[6,81,128]{2,1,0:T(8,128)(2,1)S(1)}, bf16[3,81,128]{2,1,0:T(8,128)(2,1)S(1)}) custom-call(f32[3]{0:T(128)S(1)} %add_convert_fusion.flags.refs_0_, bf16[8,768,768]{2,1,0:T(8,128)(2,1)S(1)} %get-tuple-element.32.wide, f32[8,81,128]{2,1,0:T(8,128)S(1)} %get-tuple-element.48.res.refs_7_, ...), custom_call_target="tpu_custom_call" | custom-call | tf_op jit(solution)/shard_map/solve/pallas_call | solution.py:237
  79.7 1.5 %collective-permute-start.9 = (bf16[6,81,128]{2,1,0:T(8,128)(2,1)S(1)}, bf16[6,81,128]{2,1,0:T(8,128)(2,1)S(1)}, u32[]{:S(2)}, u32[]{:S(2)}) collective-permute-start(bf16[6,81,128]{2,1,0:T(8,128)(2,1)S(1)} %get-tuple-element.53), channel_id=1, source_target_pairs={{0,24},{1,25},{2,26},{3,27},{4,28},{5,29},{6,30},{7,31},{8,0},{9,1... | collective-permute-start | bytes 373256 | tf_op jit(solution)/shard_map/ppermute | solution.py:412
  81.2 1.3 %collective-permute-start.10 = (bf16[6,81,128]{2,1,0:T(8,128)(2,1)S(1)}, bf16[6,81,128]{2,1,0:T(8,128)(2,1)S(1)}, u32[]{:S(2)}, u32[]{:S(2)}) collective-permute-start(bf16[6,81,128]{2,1,0:T(8,128)(2,1)S(1)} %get-tuple-element.54), channel_id=1, source_target_pairs={{1,0},{2,1},{3,2},{5,4},{6,5},{7,6},{9,8},{10,9},{11,10},{13,12},{... | collective-permute-start | bytes 373256 | tf_op jit(solution)/shard_map/ppermute | solution.py:413
  82.5 1.3 %collective-permute-start.11 = (bf16[3,81,128]{2,1,0:T(8,128)(2,1)S(1)}, bf16[3,81,128]{2,1,0:T(8,128)(2,1)S(1)}, u32[]{:S(2)}, u32[]{:S(2)}) collective-permute-start(bf16[3,81,128]{2,1,0:T(8,128)(2,1)S(1)} %get-tuple-element.55), channel_id=1, source_target_pairs={{1,24},{2,25},{3,26},{5,28},{6,29},{7,30},{9,0},{10,1},{11,2},{13,... | collective-permute-start | bytes 186632 | tf_op jit(solution)/shard_map/ppermute | solution.py:414
  83.8 6.8 %collective-permute-done.11.gxz.refs_4_ = bf16[3,81,128]{2,1,0:T(8,128)(2,1)S(1)} collective-permute-done((bf16[3,81,128]{2,1,0:T(8,128)(2,1)S(1)}, bf16[3,81,128]{2,1,0:T(8,128)(2,1)S(1)}, u32[]{:S(2)}, u32[]{:S(2)}) %collective-permute-start.11) | collective-permute-done | bytes 62240 | tf_op jit(solution)/shard_map/ppermute | solution.py:414
  91.1 2.1 %all-gather.3 = f32[8,104,128]{2,1,0:T(8,128)S(1)} all-gather(f32[4,104,128]{2,1,0:T(8,128)S(1)} %reduce.3), channel_id=5, replica_groups=mesh['gx'=4,'gy'=2,'gz'=4] {'gy'}, dimensions={0}, use_global_device_ids=true | all-gather | bytes 638976 | tf_op jit(solution)/shard_map/all_gather | solution.py:420
  93.2 1.2 %element.3 = (f32[8,81,128]{2,1,0:T(8,128)S(1)}, f32[8,81,128]{2,1,0:T(8,128)S(1)}, f32[4,16,128]{2,1,0:T(8,128)S(1)}, f32[4,16,128]{2,1,0:T(8,128)S(1)}, f32[4,16,128]{2,1,0:T(8,128)S(1)}) custom-call(f32[3]{0:T(128)S(1)} %add_convert_fusion.flags.refs_0_, f32[12,81,128]{2,1,0:T(8,128)S(1)} %get-tuple-element.52.c.refs_1_, ...), custom_call_target="tpu_custom_call" | custom-call | tf_op jit(solution)/shard_map/element/pallas_call | solution.py:90
  94.4 1.5 %collective-permute-start.12 = (f32[4,16,128]{2,1,0:T(8,128)S(1)}, f32[4,16,128]{2,1,0:T(8,128)S(1)}, u32[]{:S(2)}, u32[]{:S(2)}) collective-permute-start(f32[4,16,128]{2,1,0:T(8,128)S(1)} %get-tuple-element.59), channel_id=1, source_target_pairs={{0,8},{1,9},{2,10},{3,11},{4,12},{5,13},{6,14},{7,15},{8,16},{9,17... | collective-permute-start | bytes 98312 | tf_op jit(solution)/shard_map/ppermute | solution.py:471
  95.9 4.8 %collective-permute-start.13 = (f32[4,16,128]{2,1,0:T(8,128)S(1)}, f32[4,16,128]{2,1,0:T(8,128)S(1)}, u32[]{:S(2)}, u32[]{:S(2)}) collective-permute-start(f32[4,16,128]{2,1,0:T(8,128)S(1)} %get-tuple-element.61), channel_id=1, source_target_pairs={{0,1},{1,2},{2,3},{4,5},{5,6},{6,7},{8,9},{9,10},{10,11},{12,13},{... | collective-permute-start | bytes 98312 | tf_op jit(solution)/shard_map/ppermute | solution.py:472
  100.7 0.9 copy.26
  101.6 1.8 %all-gather.4 = f32[8,16,128]{2,1,0:T(8,128)S(1)} all-gather(f32[4,16,128]{2,1,0:T(8,128)S(1)} %get-tuple-element.60), channel_id=6, replica_groups=mesh['gx'=4,'gy'=2,'gz'=4] {'gy'}, dimensions={0}, use_global_device_ids=true | all-gather | bytes 98304 | tf_op jit(solution)/shard_map/all_gather | solution.py:420
  104.0 0.9 copy.27
  (35 shorter events, 3.9 us)
Async XLA Ops:
  5.0 16.6 %copy-start.4 = (s32[2,2,2,540]{3,2,1,0:T(2,128)S(1)}, s32[2,2,2,540]{3,2,1,0:T(2,128)}, u32[]{:S(2)}) copy-start(s32[2,2,2,540]{3,2,1,0:T(2,128)} %param.8) | copy-start | bytes 51844
  5.0 36.3 %collective-permute-start = (bf16[6,81,128]{2,1,0:T(8,128)(2,1)S(1)}, bf16[6,81,128]{2,1,0:T(8,128)(2,1)S(1)}, u32[]{:S(2)}, u32[]{:S(2)}) collective-permute-start(bf16[6,81,128]{2,1,0:T(8,128)(2,1)S(1)} %get-tuple-element.36), channel_id=1, source_target_pairs={{0,8},{1,9},{2,10},{3,11},{4,12},{5,13},{6,14},{7,15},{8,16},{9,17... | collective-permute-start | bytes 373256 | tf_op jit(solution)/shard_map/ppermute | solution.py:412
  7.9 33.5 %collective-permute-start.1 = (bf16[6,81,128]{2,1,0:T(8,128)(2,1)S(1)}, bf16[6,81,128]{2,1,0:T(8,128)(2,1)S(1)}, u32[]{:S(2)}, u32[]{:S(2)}) collective-permute-start(bf16[6,81,128]{2,1,0:T(8,128)(2,1)S(1)} %get-tuple-element.37), channel_id=1, source_target_pairs={{0,1},{1,2},{2,3},{4,5},{5,6},{6,7},{8,9},{9,10},{10,11},{12,13},{... | collective-permute-start | bytes 373256 | tf_op jit(solution)/shard_map/ppermute | solution.py:413
  11.4 29.9 %collective-permute-start.2 = (bf16[3,81,128]{2,1,0:T(8,128)(2,1)S(1)}, bf16[3,81,128]{2,1,0:T(8,128)(2,1)S(1)}, u32[]{:S(2)}, u32[]{:S(2)}) collective-permute-start(bf16[3,81,128]{2,1,0:T(8,128)(2,1)S(1)} %get-tuple-element.38), channel_id=1, source_target_pairs={{0,9},{1,10},{2,11},{4,13},{5,14},{6,15},{8,17},{9,18},{10,19},{12... | collective-permute-start | bytes 186632 | tf_op jit(solution)/shard_map/ppermute | solution.py:414
  15.8 5.9 %copy-start.2 = (f32[2,2,2,108,108]{4,2,3,1,0:T(2,128)S(1)}, f32[2,2,2,108,108]{4,2,3,1,0:T(2,128)}, u32[]{:S(2)}) copy-start(f32[2,2,2,108,108]{4,2,3,1,0:T(2,128)} %param.9) | copy-start | bytes 1119748
  15.8 5.9 %copy-start.3 = (s32[2,2,2,6,9]{4,2,3,1,0:T(2,128)S(1)}, s32[2,2,2,6,9]{4,2,3,1,0:T(2,128)}, u32[]{:S(2)}) copy-start(s32[2,2,2,6,9]{4,2,3,1,0:T(2,128)} %param.10) | copy-start | bytes 5188
  15.8 6.2 %copy-start.1 = (s32[768,128]{1,0:T(8,128)S(1)}, s32[768,128]{1,0:T(8,128)}, u32[]{:S(2)}) copy-start(s32[768,128]{1,0:T(8,128)} %constant.19.clone.rows) | copy-start | bytes 1179652
  22.0 2.6 %copy-start = (bf16[2,2,2,540,540]{4,3,2,1,0:T(8,128)(2,1)S(1)}, bf16[2,2,2,540,540]{4,3,2,1,0:T(8,128)(2,1)}, u32[]{:S(2)}) copy-start(bf16[2,2,2,540,540]{4,3,2,1,0:T(8,128)(2,1)} %copy.21) | copy-start | bytes 13996804
  46.2 9.9 %collective-permute-start.3 = (bf16[6,81,128]{2,1,0:T(8,128)(2,1)S(1)}, bf16[6,81,128]{2,1,0:T(8,128)(2,1)S(1)}, u32[]{:S(2)}, u32[]{:S(2)}) collective-permute-start(bf16[6,81,128]{2,1,0:T(8,128)(2,1)S(1)} %get-tuple-element.40), channel_id=1, source_target_pairs={{0,24},{1,25},{2,26},{3,27},{4,28},{5,29},{6,30},{7,31},{8,0},{9,1... | collective-permute-start | bytes 373256 | tf_op jit(solution)/shard_map/ppermute | solution.py:412
  47.7 8.4 %collective-permute-start.4 = (bf16[6,81,128]{2,1,0:T(8,128)(2,1)S(1)}, bf16[6,81,128]{2,1,0:T(8,128)(2,1)S(1)}, u32[]{:S(2)}, u32[]{:S(2)}) collective-permute-start(bf16[6,81,128]{2,1,0:T(8,128)(2,1)S(1)} %get-tuple-element.41), channel_id=1, source_target_pairs={{1,0},{2,1},{3,2},{5,4},{6,5},{7,6},{9,8},{10,9},{11,10},{13,12},{... | collective-permute-start | bytes 373256 | tf_op jit(solution)/shard_map/ppermute | solution.py:413
  49.0 7.1 %collective-permute-start.5 = (bf16[3,81,128]{2,1,0:T(8,128)(2,1)S(1)}, bf16[3,81,128]{2,1,0:T(8,128)(2,1)S(1)}, u32[]{:S(2)}, u32[]{:S(2)}) collective-permute-start(bf16[3,81,128]{2,1,0:T(8,128)(2,1)S(1)} %get-tuple-element.42), channel_id=1, source_target_pairs={{1,24},{2,25},{3,26},{5,28},{6,29},{7,30},{9,0},{10,1},{11,2},{13,... | collective-permute-start | bytes 186632 | tf_op jit(solution)/shard_map/ppermute | solution.py:414
  62.5 12.4 %collective-permute-start.6 = (bf16[6,81,128]{2,1,0:T(8,128)(2,1)S(1)}, bf16[6,81,128]{2,1,0:T(8,128)(2,1)S(1)}, u32[]{:S(2)}, u32[]{:S(2)}) collective-permute-start(bf16[6,81,128]{2,1,0:T(8,128)(2,1)S(1)} %get-tuple-element.49), channel_id=1, source_target_pairs={{0,8},{1,9},{2,10},{3,11},{4,12},{5,13},{6,14},{7,15},{8,16},{9,17... | collective-permute-start | bytes 373256 | tf_op jit(solution)/shard_map/ppermute | solution.py:412
  64.9 10.0 %collective-permute-start.7 = (bf16[6,81,128]{2,1,0:T(8,128)(2,1)S(1)}, bf16[6,81,128]{2,1,0:T(8,128)(2,1)S(1)}, u32[]{:S(2)}, u32[]{:S(2)}) collective-permute-start(bf16[6,81,128]{2,1,0:T(8,128)(2,1)S(1)} %get-tuple-element.50), channel_id=1, source_target_pairs={{0,1},{1,2},{2,3},{4,5},{5,6},{6,7},{8,9},{9,10},{10,11},{12,13},{... | collective-permute-start | bytes 373256 | tf_op jit(solution)/shard_map/ppermute | solution.py:413
  68.5 6.3 %collective-permute-start.8 = (bf16[3,81,128]{2,1,0:T(8,128)(2,1)S(1)}, bf16[3,81,128]{2,1,0:T(8,128)(2,1)S(1)}, u32[]{:S(2)}, u32[]{:S(2)}) collective-permute-start(bf16[3,81,128]{2,1,0:T(8,128)(2,1)S(1)} %get-tuple-element.51), channel_id=1, source_target_pairs={{0,9},{1,10},{2,11},{4,13},{5,14},{6,15},{8,17},{9,18},{10,19},{12... | collective-permute-start | bytes 186632 | tf_op jit(solution)/shard_map/ppermute | solution.py:414
  79.7 10.8 %collective-permute-start.9 = (bf16[6,81,128]{2,1,0:T(8,128)(2,1)S(1)}, bf16[6,81,128]{2,1,0:T(8,128)(2,1)S(1)}, u32[]{:S(2)}, u32[]{:S(2)}) collective-permute-start(bf16[6,81,128]{2,1,0:T(8,128)(2,1)S(1)} %get-tuple-element.53), channel_id=1, source_target_pairs={{0,24},{1,25},{2,26},{3,27},{4,28},{5,29},{6,30},{7,31},{8,0},{9,1... | collective-permute-start | bytes 373256 | tf_op jit(solution)/shard_map/ppermute | solution.py:412
  81.2 9.3 %collective-permute-start.10 = (bf16[6,81,128]{2,1,0:T(8,128)(2,1)S(1)}, bf16[6,81,128]{2,1,0:T(8,128)(2,1)S(1)}, u32[]{:S(2)}, u32[]{:S(2)}) collective-permute-start(bf16[6,81,128]{2,1,0:T(8,128)(2,1)S(1)} %get-tuple-element.54), channel_id=1, source_target_pairs={{1,0},{2,1},{3,2},{5,4},{6,5},{7,6},{9,8},{10,9},{11,10},{13,12},{... | collective-permute-start | bytes 373256 | tf_op jit(solution)/shard_map/ppermute | solution.py:413
  82.5 8.1 %collective-permute-start.11 = (bf16[3,81,128]{2,1,0:T(8,128)(2,1)S(1)}, bf16[3,81,128]{2,1,0:T(8,128)(2,1)S(1)}, u32[]{:S(2)}, u32[]{:S(2)}) collective-permute-start(bf16[3,81,128]{2,1,0:T(8,128)(2,1)S(1)} %get-tuple-element.55), channel_id=1, source_target_pairs={{1,24},{2,25},{3,26},{5,28},{6,29},{7,30},{9,0},{10,1},{11,2},{13,... | collective-permute-start | bytes 186632 | tf_op jit(solution)/shard_map/ppermute | solution.py:414
  94.4 9.1 %collective-permute-start.12 = (f32[4,16,128]{2,1,0:T(8,128)S(1)}, f32[4,16,128]{2,1,0:T(8,128)S(1)}, u32[]{:S(2)}, u32[]{:S(2)}) collective-permute-start(f32[4,16,128]{2,1,0:T(8,128)S(1)} %get-tuple-element.59), channel_id=1, source_target_pairs={{0,8},{1,9},{2,10},{3,11},{4,12},{5,13},{6,14},{7,15},{8,16},{9,17... | collective-permute-start | bytes 98312 | tf_op jit(solution)/shard_map/ppermute | solution.py:471
  95.9 7.5 %collective-permute-start.13 = (f32[4,16,128]{2,1,0:T(8,128)S(1)}, f32[4,16,128]{2,1,0:T(8,128)S(1)}, u32[]{:S(2)}, u32[]{:S(2)}) collective-permute-start(f32[4,16,128]{2,1,0:T(8,128)S(1)} %get-tuple-element.61), channel_id=1, source_target_pairs={{0,1},{1,2},{2,3},{4,5},{5,6},{6,7},{8,9},{9,10},{10,11},{12,13},{... | collective-permute-start | bytes 98312 | tf_op jit(solution)/shard_map/ppermute | solution.py:472

commit v2 on v1

v2 whole, which is shorter than its diff:
```python
import functools
import itertools

import jax
import jax.numpy as jnp
from jax import lax
from jax.experimental import pallas as pl
from jax.experimental.pallas import tpu as pltpu
from jax.sharding import PartitionSpec as P

INNER = 54
FACE = 9
OWN = INNER + 3 * FACE
LOCAL = INNER + 6 * FACE
SWEEPS = 2
PATCH = 540
SLOT = 96
WIDE = 8 * SLOT
AXES = ("gx", "gy", "gz")
CORNERS = tuple(itertools.product((0, 1), repeat=3))
X0, Y0, Z0 = INNER, INNER + FACE, INNER + 2 * FACE
f32, bf16 = jnp.float32, jnp.bfloat16
VMEM_LIMIT = 12 * 1024 * 1024


def canonical_rows(q):
    m = (q * 683) >> 16
    r = q - SLOT * m
    d = ((r - INNER) * 57) >> 9
    a, b, c = m >> 2, (m >> 1) & 1, m & 1
    face = jnp.where(d == 0, 2 * b + c, jnp.where(d == 1, 4 + 2 * a + c, 8 + 2 * a + b))
    on_face = 8 * INNER + FACE * face + r - INNER - FACE * d
    row = jnp.where(r < INNER, INNER * m + r, jnp.where(r < OWN, on_face, -1))
    return row.astype(f32)


def tables_kernel(cells, inv, order, matrix, pick, back, loaded, sems):
    cx, cy, cz = cells
    copies = [
        pltpu.make_async_copy(inv.at[n // cy, n % cy], loaded.at[n], sems.at[n])
        for n in range(cx * cy)
    ]
    for copy in copies:
        copy.start()
    across = canonical_rows(lax.broadcasted_iota(jnp.int32, (1, WIDE), 1))
    down = canonical_rows(lax.broadcasted_iota(jnp.int32, (WIDE, 1), 0))
    for n, copy in enumerate(copies):
        for z in range(cz):
            line = order[n // cy, n % cy, z : z + 1, :].astype(f32)
            spread = jnp.broadcast_to(line, (128, PATCH)).T
            spread = jnp.concatenate([spread] * (WIDE // 128), axis=1)
            pick[n * cz + z] = jnp.where(spread == across, 1.0, 0.0).astype(bf16)
            back[n * cz + z] = jnp.where(down == line, 1.0, 0.0).astype(bf16)
        copy.wait()
        matrix[n] = loaded[n].reshape(cz * PATCH, PATCH)


def tables(cells, inverse, order):
    cx, cy, cz = cells
    count = cx * cy * cz
    vmem = pl.BlockSpec(memory_space=pltpu.VMEM)
    return pl.pallas_call(
        functools.partial(tables_kernel, cells),
        in_specs=[pl.BlockSpec(memory_space=pltpu.HBM), vmem],
        out_specs=[vmem] * 3,
        out_shape=[
            jax.ShapeDtypeStruct((cx * cy, cz * PATCH, PATCH), bf16),
            jax.ShapeDtypeStruct((count, PATCH, WIDE), bf16),
            jax.ShapeDtypeStruct((count, WIDE, PATCH), bf16),
        ],
        scratch_shapes=[
            pltpu.VMEM((cx * cy, PATCH, cz, PATCH), bf16),
            pltpu.SemaphoreType.DMA((cx * cy,)),
        ],
        compiler_params=pltpu.CompilerParams(vmem_limit_bytes=VMEM_LIMIT),
        cost_estimate=pl.CostEstimate(
            flops=count * 16 * WIDE * PATCH * 128,
            bytes_accessed=count * 2 * PATCH * PATCH,
            transcendentals=0,
        ),
        name="tables",
    )(inverse, order)


def exact_parts(value):
    high = value.astype(bf16)
    rest = value - high.astype(f32)
    middle = rest.astype(bf16)
    return high, middle, (rest - middle.astype(f32)).astype(bf16)


def matrices_kernel(depth, mat, slot, canon, both):
    both[...] = mat[0, 0].reshape(depth * LOCAL, LOCAL)
    index = lax.broadcasted_iota(jnp.int32, (LOCAL, LOCAL), 0)
    dims = (((1,), (1,)), ((), ()))
    for z in range(depth):
        pick = jnp.where(index == slot[z], 1.0, 0.0).astype(bf16)
        parts = exact_parts(both[pl.ds(z, LOCAL, stride=depth), :])
        side = sum(lax.dot_general(p, pick, dims, preferred_element_type=f32) for p in parts)
        parts = exact_parts(side)
        canon[z] = sum(jnp.dot(pick, p, preferred_element_type=f32) for p in parts)


def canonical_matrices(cells, matrices, face_order):
    cx, cy, cz = cells
    count = cx * cy * cz
    offsets = (INNER + FACE * jnp.arange(6, dtype=jnp.int32))[:, None]
    slots = (face_order + offsets).reshape(count, 1, 6 * FACE)
    inner = jnp.broadcast_to(jnp.arange(INNER, dtype=jnp.int32), (count, 1, INNER))
    slots = jnp.concatenate([inner, slots], axis=2)
    return pl.pallas_call(
        functools.partial(matrices_kernel, cz),
        grid=(cx * cy,),
        in_specs=[
            pl.BlockSpec((1, 1, LOCAL, cz, LOCAL), lambda i: (i // cy, i % cy, 0, 0, 0)),
            pl.BlockSpec((cz, 1, LOCAL), lambda i: (i, 0, 0)),
        ],
        out_specs=pl.BlockSpec((cz, LOCAL, LOCAL), lambda i: (i, 0, 0)),
        out_shape=jax.ShapeDtypeStruct((count, LOCAL, LOCAL), f32),
        scratch_shapes=[pltpu.VMEM((cz * LOCAL, LOCAL), f32)],
        compiler_params=pltpu.CompilerParams(vmem_limit_bytes=VMEM_LIMIT),
        cost_estimate=pl.CostEstimate(
            flops=count * 24 * LOCAL**3, bytes_accessed=count * 8 * LOCAL**2, transcendentals=0
        ),
        name="matrices",
    )(jnp.transpose(matrices, (0, 1, 3, 2, 4)), slots)


def call(kernel, operands, shapes, name):
    specs = [pl.BlockSpec(memory_space=pltpu.SMEM)]
    specs += [pl.BlockSpec(memory_space=pltpu.VMEM)] * (len(operands) - 1)
    return pl.pallas_call(
        kernel,
        in_specs=specs,
        out_specs=[pl.BlockSpec(memory_space=pltpu.VMEM)] * len(shapes),
        out_shape=[jax.ShapeDtypeStruct(s, t) for s, t in shapes],
        compiler_params=pltpu.CompilerParams(vmem_limit_bytes=VMEM_LIMIT),
        name=name,
    )(*operands)


def cat(*parts):
    return jnp.concatenate(parts, axis=0)


def zeros(rows, like):
    return jnp.zeros((rows, like.shape[-1]), f32)


def mixed(x, y, z, cells):
    return pl.ds((x * cells[1] + y) * OWN * cells[2] + z, OWN, stride=cells[2])


def start_kernel(cells, flags, res, out, my):
    cx, cy, cz = cells
    for x, y, z in itertools.product(*map(range, cells)):
        e = (x * cy + y) * cz + z
        cur = res[mixed(x, y, z, cells)]
        if y == 0:
            cur = cat(cur[:Y0], cur[Y0:Z0] * flags[0], cur[Z0:])
        if z == 0:
            cur = cat(cur[:Z0], cur[Z0:] * flags[2])
        out[e] = cur
        if y == cy - 1:
            nine, rest = zeros(FACE, cur), zeros(112 - OWN, cur)
            my[x * cz + z] = cat(cur[:Y0], nine, cur[Z0:], rest).astype(bf16)


def spread_kernel(cells, terms, *refs):
    cx, cy, cz = cells
    if terms:
        flags, res, yr, tx, tz, out, mx, mz, mxz = refs
    else:
        flags, res, yr, out, mx, mz, mxz = refs
    for x, z in itertools.product(range(cx), range(cz)):
        lastx, lastz = x == cx - 1, z == cz - 1
        halo = yr[0, x * cz + z].astype(f32) * flags[0]
        nine = zeros(FACE, halo)
        if lastx:
            mx[z] = cat(halo[:X0], halo[81:90], nine, halo[Z0:OWN]).astype(bf16)
        if lastz:
            mz[x * (cy + 1)] = cat(halo[:Y0], nine, halo[90:99]).astype(bf16)
        if lastx and lastz:
            mxz[0] = cat(halo[:X0], halo[81:90], nine, halo[90:99]).astype(bf16)
        for y in range(cy):
            e = (x * cy + y) * cz + z
            cur = res[e]
            if y == 0 and terms:
                cur = cat(cur[:Y0], cur[Y0:Z0] + halo[Y0:Z0], cur[Z0:])
            out[e] = cur
            upx = tx[y * cz + z][:FACE] if terms and lastx else nine
            upz = tz[x * cy + y][:FACE] if terms and lastz else nine
            if lastx:
                mx[(y + 1) * cz + z] = cat(cur[:X0], upx, cur[Y0:]).astype(bf16)
            if lastz:
                mz[x * (cy + 1) + y + 1] = cat(cur[:Z0], upz).astype(bf16)
            if lastx and lastz:
                mxz[y + 1] = cat(cur[:X0], upx, cur[Y0:Z0], upz).astype(bf16)


def solve_kernel(cells, *refs):
    flags, matrix, pick, back, res, yr, hx, hz, hxz = refs[:9]
    c, ox, oz, oxz, stars, solved, both = refs[9:]
    cx, cy, cz = cells
    columns = res.shape[-1]

    found = {}
    for e in itertools.product(range(-1, cx), range(-1, cy), range(-1, cz)):
        x, y, z = e
        if x < 0 and z < 0:
            val = hxz[y + 1].astype(f32) * flags[2]
        elif x < 0:
            val = hx[(y + 1) * cz + z].astype(f32)
        elif z < 0:
            val = hz[x * (cy + 1) + y + 1].astype(f32) * flags[2]
        elif y < 0:
            val = yr[0, x * cz + z].astype(f32)[:OWN] * flags[0]
        else:
            val = res[(x * cy + y) * cz + z]
        found[e] = val
    for n, v in enumerate(itertools.product(*map(range, cells))):
        for a, b, g in CORNERS:
            x, y, z = v[0] - 1 + a, v[1] - 1 + b, v[2] - 1 + g
            val = found[(x, y, z)]
            nine = zeros(FACE, val)
            part = cat(
                val[:X0],
                val[X0:Y0] if a or x < 0 else nine,
                val[Y0:Z0] if b else nine,
                val[Z0:] if g or z < 0 else nine,
                zeros(SLOT - OWN, val),
            )
            m = 4 * a + 2 * b + g
            stars[n, m * SLOT : (m + 1) * SLOT] = part.astype(bf16)

    @pl.loop(0, cx * cy)
    def _(step):
        listed = []
        for z in range(cz):
            n = step * cz + z
            got = jnp.dot(pick[n], stars[n], preferred_element_type=f32)
            listed.append(got.astype(bf16))
        listed = jnp.concatenate(listed, axis=1)
        answer = jnp.dot(matrix[step], listed, preferred_element_type=f32)
        for z in range(cz):
            both[z] = answer[:, z * columns : (z + 1) * columns]
        for z in range(cz):
            n = step * cz + z
            value = both[z, pl.ds(z, PATCH, stride=cz), :].astype(bf16)
            solved[n] = jnp.dot(back[n], value, preferred_element_type=f32)

    vertices = list(itertools.product(*map(range, cells)))
    for e in itertools.product(range(-1, cx), range(-1, cy), range(-1, cz)):
        parts = []
        for n, v in enumerate(vertices):
            m = tuple(e[d] - v[d] + 1 for d in range(3))
            if all(k in (0, 1) for k in m):
                parts.append((n, m))

        def total(low, high, keep):
            acc = None
            for n, m in parts:
                if keep(m):
                    base = (4 * m[0] + 2 * m[1] + m[2]) * SLOT
                    val = solved[n, base + low : base + high]
                    acc = val if acc is None else acc + val
            return acc

        pieces = [total(0, X0, lambda m: True)]
        for d in range(3):
            low = INNER + d * FACE
            pieces.append(total(low, low + FACE, lambda m: e[d] < 0 or m[d] == 1))
        val = cat(*pieces)
        x, y, z = e
        if x < 0 and z < 0:
            oxz[y + 1] = val.astype(bf16)
        elif x < 0:
            ox[(y + 1) * cz + z] = val.astype(bf16)
        elif z < 0:
            oz[x * (cy + 1) + y + 1] = val.astype(bf16)
        else:
            c[(x * (cy + 1) + y + 1) * cz + z] = val


def solve(cells, operands):
    cx, cy, cz = cells
    count, columns = cx * cy * cz, operands[4].shape[-1]
    vmem = pl.BlockSpec(memory_space=pltpu.VMEM)
    halos = operands[-3:]
    return pl.pallas_call(
        functools.partial(solve_kernel, cells),
        in_specs=[pl.BlockSpec(memory_space=pltpu.SMEM)] + [vmem] * (len(operands) - 1),
        out_specs=[vmem] * 4,
        out_shape=[jax.ShapeDtypeStruct((cx * (cy + 1) * cz, OWN, columns), f32)]
        + [jax.ShapeDtypeStruct(h.shape, bf16) for h in halos],
        scratch_shapes=[
            pltpu.VMEM((count, WIDE, columns), bf16),
            pltpu.VMEM((count, WIDE, columns), f32),
            pltpu.VMEM((cz, cz * PATCH, columns), f32),
        ],
        compiler_params=pltpu.CompilerParams(vmem_limit_bytes=VMEM_LIMIT),
        name="solve",
    )(*operands)


def add_received(val, x, y, z, cells, last, gx, gz, gxz):
    cx, cy, cz = cells
    nine = zeros(FACE, val)
    if x == cx - 1:
        got = gx[(y + 1) * cz + z].astype(f32)
        val = val + cat(got[:X0], nine, got[Y0:])
    if z == cz - 1:
        got = gz[x * (cy + 1) + y + 1].astype(f32) * last
        val = val + cat(got[:Z0], nine)
    if x == cx - 1 and z == cz - 1:
        got = gxz[y + 1].astype(f32) * last
        val = val + cat(got[:X0], nine, got[Y0:Z0], nine)
    return val


def upper_x(y, z, cells, last, gx, gxz):
    val = gx[(y + 1) * cells[2] + z].astype(f32)[X0:Y0]
    if z == cells[2] - 1:
        val = val + gxz[y + 1].astype(f32)[X0:Y0] * last
    return val


def upper_z(x, y, cells, last, gz, gxz):
    val = gz[x * (cells[1] + 1) + y + 1].astype(f32)[Z0:]
    if x == cells[0] - 1:
        val = val + gxz[y + 1].astype(f32)[Z0:]
    return val * last


def reduce_kernel(cells, flags, c, gx, gz, gxz, out):
    cx, cy, cz = cells
    for x, z in itertools.product(range(cx), range(cz)):
        val = add_received(c[x * (cy + 1) * cz + z], x, -1, z, cells, flags[3], gx, gz, gxz)
        nine = zeros(FACE, val)
        upx = upper_x(-1, z, cells, flags[3], gx, gxz) if x == cx - 1 else nine
        upz = upper_z(x, -1, cells, flags[3], gz, gxz) if z == cz - 1 else nine
        out[x * cz + z] = cat(val, upx, upz, zeros(104 - OWN - 2 * FACE, val))


def element_kernel(cells, first, last, *refs):
    cx, cy, cz = cells
    flags, c, gx, gz, gxz, yr, mat, res, hx, hz = refs[:10]
    refs = refs[10:]
    if not first:
        prev, refs = refs[0], refs[1:]
    sol, out, tx, tz, my = refs
    peer = yr.shape[0] - 1
    own, images = {}, {}
    for e in itertools.product(*map(range, cells)):
        x, y, z = e
        n = (x * cy + y) * cz + z
        val = add_received(c[(x * (cy + 1) + y + 1) * cz + z], x, y, z, cells, flags[3], gx, gz, gxz)
        if y == cy - 1:
            got = yr[peer, x * cz + z][:OWN] * flags[1]
            val = val + cat(got[:Y0], zeros(FACE, val), got[Z0:])
        if y == 0:
            val = cat(val[:Y0], val[Y0:Z0] * flags[0], val[Z0:])
        if z == 0:
            val = cat(val[:Z0], val[Z0:] * flags[2])
        own[e] = val
        total = val if first else prev[n] + val
        if last:
            sol[mixed(x, y, z, cells)] = total
        else:
            sol[n] = total
    for e in itertools.product(*map(range, cells)):
        x, y, z = e
        if x < cx - 1:
            upx = own[(x + 1, y, z)][X0:Y0]
        else:
            upx = upper_x(y, z, cells, flags[3], gx, gxz)
            if y == cy - 1:
                upx = upx + yr[peer, x * cz + z][81:90] * flags[1]
        if y < cy - 1:
            upy = own[(x, y + 1, z)][Y0:Z0]
        else:
            upy = yr[peer, x * cz + z][Y0:Z0] * flags[1]
        if z < cz - 1:
            upz = own[(x, y, z + 1)][Z0:]
        else:
            upz = upper_z(x, y, cells, flags[3], gz, gxz)
            if y == cy - 1:
                upz = upz + yr[peer, x * cz + z][90:99] * flags[1]
        val = own[e]
        local = cat(val[:Y0], upx, val[Y0:Z0], upy, val[Z0:], upz)
        images[e] = jnp.dot(
            mat[(x * cy + y) * cz + z],
            local,
            precision=lax.Precision.HIGHEST,
            preferred_element_type=f32,
        )
    for e in itertools.product(*map(range, cells)):
        x, y, z = e
        n = (x * cy + y) * cz + z
        old, image = res[n], images[e]
        lowx = old[X0:Y0] - image[54:63]
        lowy = old[Y0:Z0] - image[72:81]
        lowz = old[Z0:] - image[90:99]
        if x > 0:
            lowx = lowx - images[(x - 1, y, z)][63:72]
        else:
            lowx = lowx + hx[(y + 1) * cz + z].astype(f32)[X0:Y0]
        if y > 0:
            lowy = lowy - images[(x, y - 1, z)][81:90]
        else:
            lowy = lowy * flags[0]
        if z > 0:
            lowz = lowz - images[(x, y, z - 1)][99:108]
        else:
            lowz = (lowz + hz[x * (cy + 1) + y + 1].astype(f32)[Z0:]) * flags[2]
        val = cat(old[:X0] - image[:X0], lowx, lowy, lowz)
        out[n] = val
        nine, seven = zeros(FACE, val), zeros(16 - FACE, val)
        upx, upy, upz = -image[63:72], -image[81:90], -image[99:108]
        if x == cx - 1:
            tx[y * cz + z] = cat(upx, seven)
        if z == cz - 1:
            tz[x * cy + y] = cat(upz, seven)
        if y == cy - 1 and last:
            my[x * cz + z] = cat(upy, seven)
        elif y == cy - 1:
            my[x * cz + z] = cat(
                val[:Y0],
                upy,
                val[Z0:],
                upx if x == cx - 1 else nine,
                upz if z == cz - 1 else nine,
                zeros(112 - OWN - 2 * FACE, val),
            ).astype(bf16)


def finish_kernel(cells, flags, res, fx, fy, fz, out):
    cx, cy, cz = cells
    for x, y, z in itertools.product(*map(range, cells)):
        n = (x * cy + y) * cz + z
        cur = res[n]
        lowx, lowy, lowz = cur[X0:Y0], cur[Y0:Z0], cur[Z0:]
        if x == 0:
            lowx = lowx + fx[y * cz + z][:FACE]
        if y == 0:
            lowy = lowy + fy[0, x * cz + z][:FACE] * flags[0]
        if z == 0:
            lowz = lowz + fz[x * cy + y][:FACE] * flags[2]
        out[mixed(x, y, z, cells)] = cat(cur[:X0], lowx, lowy, lowz)


def route(offset):
    sizes = [lax.axis_size(a) for a in AXES]
    flat = lambda c: (c[0] * sizes[1] + c[1]) * sizes[2] + c[2]
    pairs = []
    for spot in itertools.product(*map(range, sizes)):
        aim = [s + o for s, o in zip(spot, offset)]
        aim[0] %= sizes[0]
        aim[2] %= sizes[2]
        if all(0 <= a < s for a, s in zip(aim, sizes)):
            pairs.append((flat(spot), flat(aim)))
    return pairs


def send_xz(mx, mz, mxz, sign):
    return (
        lax.ppermute(mx, AXES, route((sign, 0, 0))),
        lax.ppermute(mz, AXES, route((0, 0, sign))),
        lax.ppermute(mxz, AXES, route((sign, 0, sign))),
    )


def send_y(my, sign):
    if lax.axis_size("gy") == 2:
        return lax.all_gather(my, "gy")
    return lax.ppermute(my, AXES, route((0, sign, 0)))[None]


def body(residual_start, patch_inverse, patch_order, element_matrix, face_order):
    cells = cx, cy, cz = residual_start.shape[:3]
    if min(cells) < 2:
        raise ValueError(cells)
    columns = residual_start.shape[4]
    count = cx * cy * cz
    at_y, at_z = lax.axis_index("gy"), lax.axis_index("gz")
    flags = jnp.stack(
        [
            at_y > 0,
            at_y < lax.axis_size("gy") - 1,
            at_z > 0,
            at_z < lax.axis_size("gz") - 1,
        ]
    ).astype(f32)
    bind = lambda kernel, *extra: functools.partial(kernel, cells, *extra)
    state = ((count, OWN, columns), f32)
    sent = (
        (((cy + 1) * cz, OWN, columns), bf16),
        ((cx * (cy + 1), OWN, columns), bf16),
        ((cy + 1, OWN, columns), bf16),
    )
    term_x, term_y, term_z = (((n, 16, columns), f32) for n in (cy * cz, cx * cz, cx * cy))
    rim = ((cx * cz, 112, columns), bf16)

    swap = lambda a: jnp.transpose(a, (0, 1, 3, 2, 4))
    flat = ((count * OWN, columns), f32)
    start = swap(residual_start).reshape(count * OWN, columns)
    residual, my = call(bind(start_kernel), [flags, start], [state, rim], "start")
    inverse = swap(patch_inverse)
    inverse = pltpu.with_memory_space_constraint(swap(patch_inverse), pltpu.HBM)
    order = patch_order
    terms, solution = [], []
    for sweep in range(SWEEPS):
        first, last = sweep == 0, sweep == SWEEPS - 1
        yr = send_y(my, 1)
        residual, mx, mz, mxz = call(
            bind(spread_kernel, not first), [flags, residual, yr] + terms, [state, *sent], "spread"
        )
        order, mx, mz, mxz = lax.optimization_barrier((order, mx, mz, mxz))
        hx, hz, hxz = send_xz(mx, mz, mxz, 1)
        matrix, pick, place = tables(cells, inverse, order)
        c, ox, oz, oxz = solve(cells, [flags, matrix, pick, place, residual, yr, hx, hz, hxz])
        if first:
            face_order, ox = lax.optimization_barrier((face_order, ox))
            canon = canonical_matrices(cells, element_matrix, face_order)
        gx, gz, gxz = send_xz(ox, oz, oxz, -1)
        (down,) = call(
            bind(reduce_kernel), [flags, c, gx, gz, gxz], [((cx * cz, 104, columns), f32)], "reduce"
        )
        back = send_y(down, -1)
        total, residual, tx, tz, my = call(
            bind(element_kernel, first, last),
            [flags, c, gx, gz, gxz, back, canon, residual, hx, hz] + solution,
            [flat if last else state, state, term_x, term_z, term_y if last else rim],
            "element",
        )
        terms, solution = [tx, tz], [total]
    fx = lax.ppermute(tx, AXES, route((1, 0, 0)))
    fz = lax.ppermute(tz, AXES, route((0, 0, 1)))
    fy = send_y(my, 1)
    (residual,) = call(bind(finish_kernel), [flags, residual, fx, fy, fz], [flat], "finish")
    shape = (cx, cy, OWN, cz, columns)
    return swap(total.reshape(shape)), swap(residual.reshape(shape))


def solution(mesh):
    return jax.shard_map(
        body,
        mesh=mesh,
        in_specs=(
            P("gx", "gy", "gz", None, None),
            P("gx", "gy", "gz", None, None),
            P("gx", "gy", "gz", None),
            P("gx", "gy", "gz", None, None),
            P("gx", "gy", "gz", None, None),
        ),
        out_specs=(P("gx", "gy", "gz", None, None), P("gx", "gy", "gz", None, None)),
        check_vma=False,
    )
```

time: 105 us -> 86.5 us (0.82)
  starting transfers between devices: 35.7 us -> 22.2 us
  local copies, waits for them, and re-layouts: 11.3 us -> 1.81 us
  Pallas kernels: 32.1 us -> 41.3 us
  waiting for transfers between devices: 14.5 us -> 9.8 us
    ppermute x4, waiting for transfers between devices: 14.4 us -> 3.37 us  [send_xz(): lax.ppermute(mxz, AXES, route((sign, 0, sign)))]
    unnamed x15 -> x10, local copies, waits for them, and re-layouts: 11.2 us -> 1.72 us
    pallas_call x3 -> x5, Pallas kernels: 26.4 us -> 34.3 us  [the longest x2 21.8 us: solve(): pl.pallas_call(functools.partial(solve_kernel, cells), in_specs=[pl.Block...]
    ppermute x4, starting transfers between devices: 9.69 us -> 4.65 us  [send_xz(): lax.ppermute(mz, AXES, route((0, 0, sign)))]
    ppermute x1, starting transfers between devices: 4.78 us -> 0.16 us  [body(): fz = lax.ppermute(tz, AXES, route((0, 0, 1)))]
    ppermute x1, waiting for transfers between devices: 0.01 us -> 3.18 us  [body(): fz = lax.ppermute(tz, AXES, route((0, 0, 1)))]
    ppermute x4, starting transfers between devices: 8.29 us -> 5.2 us  [send_xz(): lax.ppermute(mx, AXES, route((sign, 0, 0)))]
    ppermute x4, waiting for transfers between devices: 0.01 us -> 1.74 us  [send_xz(): lax.ppermute(mz, AXES, route((0, 0, sign)))]
  transfers between devices with their start and end apart: 14 -> 14, of which waited for: 3 -> 7; matrix products, arithmetic and copies ran while one was open for 7% -> 0% of each run, Pallas kernels for 16% -> 14%
where the time goes in v2:
time: 86.5 us; the launch traced here: 86.3 us
  Pallas kernels  41.3 us (48%)
  starting transfers between devices  22.2 us (26%)
  blocking collectives  10.1 us (12%)
  waiting for transfers between devices  9.8 us (11%)
  local copies, waits for them, and re-layouts  1.81 us (2%)
    pallas_call x2, Pallas kernels, solve(): pl.pallas_call(functools.partial(solve_kernel, cells), in_specs=[pl.Block...  21.8 us
    all_gather x5, blocking collectives, send_y(): return lax.all_gather(my, 'gy')  10.1 us
    ppermute x4, starting transfers between devices, send_xz(): lax.ppermute(mxz, AXES, route((sign, 0, sign)))  9.9 us
    pallas_call x2, Pallas kernels, tables(): pl.pallas_call(functools.partial(tables_kernel, cells), in_specs=[pl.Bloc...  9.45 us
    pallas_call x8, Pallas kernels, call(): pl.pallas_call(kernel, in_specs=specs, out_specs=[pl.BlockSpec(memory_spa...  7.04 us
    ppermute x4, starting transfers between devices, send_xz(): lax.ppermute(mx, AXES, route((sign, 0, 0)))  5.2 us
    ppermute x4, starting transfers between devices, send_xz(): lax.ppermute(mz, AXES, route((0, 0, sign)))  4.65 us
    ppermute x4, waiting for transfers between devices, send_xz(): lax.ppermute(mxz, AXES, route((sign, 0, sign)))  3.37 us
  transfers between devices with their start and end apart: 14, of which 7 were waited for; matrix products, arithmetic and copies ran while one was open for 0% of the time, Pallas kernels for 14%

profile of v2, /device:TPU:0, one launch (start us, length us, event | category | flops | bytes accessed | tf_op | source)
XLA Modules:
  0.0 86.3 jit_solution(14602182589631372612)
XLA Ops:
  0.7 1.0 %copy-done.1 = f32[2,2,2,81,128]{4,2,3,1,0:T(2,128)S(1)} copy-done((f32[2,2,2,81,128]{4,2,3,1,0:T(2,128)S(1)}, f32[2,2,2,81,128]{4,2,3,1,0:T(2,128)}, u32[]{:S(2)}) %copy-start.1) | copy-done | bytes 331800
  2.3 2.1 %all-gather = bf16[8,112,128]{2,1,0:T(8,128)(2,1)S(1)} all-gather(bf16[4,112,128]{2,1,0:T(8,128)(2,1)S(1)} %get-tuple-element.47), channel_id=2, replica_groups=mesh['gx'=4,'gy'=2,'gz'=4] {'gy'}, dimensions={0}, use_global_device_ids=true | all-gather | bytes 344064 | tf_op jit(solution)/shard_map/all_gather | solution.py:475
  5.0 3.9 %collective-permute-start.2 = (bf16[3,81,128]{2,1,0:T(8,128)(2,1)S(1)}, bf16[3,81,128]{2,1,0:T(8,128)(2,1)S(1)}, u32[]{:S(2)}, u32[]{:S(2)}) collective-permute-start(bf16[3,81,128]{2,1,0:T(8,128)(2,1)S(1)} %get-tuple-element.58), channel_id=1, source_target_pairs={{0,9},{1,10},{2,11},{3,8},{4,13},{5,14},{6,15},{7,12},{8,17},{9,18... | collective-permute-start | bytes 186632 | tf_op jit(solution)/shard_map/ppermute | solution.py:469
  8.9 1.5 %collective-permute-start = (bf16[6,81,128]{2,1,0:T(8,128)(2,1)S(1)}, bf16[6,81,128]{2,1,0:T(8,128)(2,1)S(1)}, u32[]{:S(2)}, u32[]{:S(2)}) collective-permute-start(bf16[6,81,128]{2,1,0:T(8,128)(2,1)S(1)} %get-tuple-element.56), channel_id=1, source_target_pairs={{0,8},{1,9},{2,10},{3,11},{4,12},{5,13},{6,14},{7,15},{8,16},{9,17... | collective-permute-start | bytes 373256 | tf_op jit(solution)/shard_map/ppermute | solution.py:467
  10.4 1.6 %collective-permute-start.1 = (bf16[6,81,128]{2,1,0:T(8,128)(2,1)S(1)}, bf16[6,81,128]{2,1,0:T(8,128)(2,1)S(1)}, u32[]{:S(2)}, u32[]{:S(2)}) collective-permute-start(bf16[6,81,128]{2,1,0:T(8,128)(2,1)S(1)} %get-tuple-element.57), channel_id=1, source_target_pairs={{0,1},{1,2},{2,3},{3,0},{4,5},{5,6},{6,7},{7,4},{8,9},{9,10},{10,1... | collective-permute-start | bytes 373256 | tf_op jit(solution)/shard_map/ppermute | solution.py:468
  11.9 0.7 copy-done.2
  12.7 4.7 %tables.2 = (bf16[4,1080,540]{2,1,0:T(8,128)(2,1)S(1)}, bf16[8,540,768]{2,1,0:T(8,128)(2,1)S(1)}, bf16[8,768,540]{2,1,0:T(8,128)(2,1)S(1)}) custom-call(bf16[2,2,540,2,540]{4,3,2,1,0:T(2,128)(2,1)} %bitcast.32, s32[2,2,2,540]{3,2,1,0:T(2,128)S(1)} %copy-done.2), custom_call_target="tpu_custom_call" | custom-call | flops 6794772480 | bytes 4665600 | tf_op jit(solution)/shard_map/tables/pallas_call | solution.py:62
  17.5 10.9 %solve.2 = (f32[12,81,128]{2,1,0:T(8,128)S(1)}, bf16[6,81,128]{2,1,0:T(8,128)(2,1)S(1)}, bf16[6,81,128]{2,1,0:T(8,128)(2,1)S(1)}, bf16[3,81,128]{2,1,0:T(8,128)(2,1)S(1)}) custom-call(f32[4]{0:T(128)S(1)} %add_convert_fusion.flags.refs_0_, bf16[4,1080,540]{2,1,0:T(8,128)(2,1)S(1)} %get-tuple-element.52.refs_1_, ...), custom_call_target="tpu_custom_call" | custom-call | tf_op jit(solution)/shard_map/solve/pallas_call | solution.py:290
  28.6 3.1 %collective-permute-start.5 = (bf16[3,81,128]{2,1,0:T(8,128)(2,1)S(1)}, bf16[3,81,128]{2,1,0:T(8,128)(2,1)S(1)}, u32[]{:S(2)}, u32[]{:S(2)}) collective-permute-start(bf16[3,81,128]{2,1,0:T(8,128)(2,1)S(1)} %get-tuple-element.63), channel_id=1, source_target_pairs={{0,27},{1,24},{2,25},{3,26},{4,31},{5,28},{6,29},{7,30},{8,3},{9,0... | collective-permute-start | bytes 186632 | tf_op jit(solution)/shard_map/ppermute | solution.py:469
  31.7 0.7 collective-permute-start.3
  33.0 3.0 %matrices.1.refs_6_ = f32[8,108,108]{2,1,0:T(8,128)S(1)} custom-call(f32[2,2,108,2,108]{4,3,2,1,0:T(2,128)S(1)} %bitcast.27, s32[8,1,108]{2,1,0:T(1,128)S(1)} %pad_add_fusion.slot), custom_call_target="tpu_custom_call" | custom-call | flops 241864704 | bytes 746496 | tf_op jit(solution)/shard_map/matrices/pallas_call | solution.py:111
  36.0 0.7 collective-permute-done.3.gx.refs_2_
  36.7 0.7 collective-permute-done.4.gz.refs_3_
  37.9 2.1 %all-gather.1 = f32[8,104,128]{2,1,0:T(8,128)S(1)} all-gather(f32[4,104,128]{2,1,0:T(8,128)S(1)} %reduce.2), channel_id=3, replica_groups=mesh['gx'=4,'gy'=2,'gz'=4] {'gy'}, dimensions={0}, use_global_device_ids=true | all-gather | bytes 638976 | tf_op jit(solution)/shard_map/all_gather | solution.py:475
  40.0 1.1 %element.2 = (f32[8,81,128]{2,1,0:T(8,128)S(1)}, f32[8,81,128]{2,1,0:T(8,128)S(1)}, f32[4,16,128]{2,1,0:T(8,128)S(1)}, f32[4,16,128]{2,1,0:T(8,128)S(1)}, bf16[4,112,128]{2,1,0:T(8,128)(2,1)S(1)}) custom-call(f32[4]{0:T(128)S(1)} %add_convert_fusion.flags.refs_0_, f32[12,81,128]{2,1,0:T(8,128)S(1)} %get-tuple-element.59.c.refs_1_, ...), custom_call_target="tpu_custom_call" | custom-call | tf_op jit(solution)/shard_map/element/pallas_call | solution.py:132
  41.2 2.0 %all-gather.2 = bf16[8,112,128]{2,1,0:T(8,128)(2,1)S(1)} all-gather(bf16[4,112,128]{2,1,0:T(8,128)(2,1)S(1)} %get-tuple-element.66), channel_id=4, replica_groups=mesh['gx'=4,'gy'=2,'gz'=4] {'gy'}, dimensions={0}, use_global_device_ids=true | all-gather | bytes 344064 | tf_op jit(solution)/shard_map/all_gather | solution.py:475
  43.8 1.1 %collective-permute-start.8 = (bf16[3,81,128]{2,1,0:T(8,128)(2,1)S(1)}, bf16[3,81,128]{2,1,0:T(8,128)(2,1)S(1)}, u32[]{:S(2)}, u32[]{:S(2)}) collective-permute-start(bf16[3,81,128]{2,1,0:T(8,128)(2,1)S(1)} %get-tuple-element.79), channel_id=1, source_target_pairs={{0,9},{1,10},{2,11},{3,8},{4,13},{5,14},{6,15},{7,12},{8,17},{9,18... | collective-permute-start | bytes 186632 | tf_op jit(solution)/shard_map/ppermute | solution.py:469
  44.8 1.4 %collective-permute-start.6 = (bf16[6,81,128]{2,1,0:T(8,128)(2,1)S(1)}, bf16[6,81,128]{2,1,0:T(8,128)(2,1)S(1)}, u32[]{:S(2)}, u32[]{:S(2)}) collective-permute-start(bf16[6,81,128]{2,1,0:T(8,128)(2,1)S(1)} %get-tuple-element.77), channel_id=1, source_target_pairs={{0,8},{1,9},{2,10},{3,11},{4,12},{5,13},{6,14},{7,15},{8,16},{9,17... | collective-permute-start | bytes 373256 | tf_op jit(solution)/shard_map/ppermute | solution.py:467
  46.2 1.2 %collective-permute-start.7 = (bf16[6,81,128]{2,1,0:T(8,128)(2,1)S(1)}, bf16[6,81,128]{2,1,0:T(8,128)(2,1)S(1)}, u32[]{:S(2)}, u32[]{:S(2)}) collective-permute-start(bf16[6,81,128]{2,1,0:T(8,128)(2,1)S(1)} %get-tuple-element.78), channel_id=1, source_target_pairs={{0,1},{1,2},{2,3},{3,0},{4,5},{5,6},{6,7},{7,4},{8,9},{9,10},{10,1... | collective-permute-start | bytes 373256 | tf_op jit(solution)/shard_map/ppermute | solution.py:468
  47.5 4.7 %tables.3 = (bf16[4,1080,540]{2,1,0:T(8,128)(2,1)S(1)}, bf16[8,540,768]{2,1,0:T(8,128)(2,1)S(1)}, bf16[8,768,540]{2,1,0:T(8,128)(2,1)S(1)}) custom-call(bf16[2,2,540,2,540]{4,3,2,1,0:T(2,128)(2,1)} %bitcast.33, s32[2,2,2,540]{3,2,1,0:T(2,128)S(1)} %copy-done.3), custom_call_target="tpu_custom_call" | custom-call | flops 6794772480 | bytes 4665600 | tf_op jit(solution)/shard_map/tables/pallas_call | solution.py:62
  52.5 1.1 %collective-permute-done.7.refs_7_.refs_9_ = bf16[6,81,128]{2,1,0:T(8,128)(2,1)S(1)} collective-permute-done((bf16[6,81,128]{2,1,0:T(8,128)(2,1)S(1)}, bf16[6,81,128]{2,1,0:T(8,128)(2,1)S(1)}, u32[]{:S(2)}, u32[]{:S(2)}) %collective-permute-start.7) | collective-permute-done | bytes 124448 | tf_op jit(solution)/shard_map/ppermute | solution.py:468
  53.6 10.9 %solve.3 = (f32[12,81,128]{2,1,0:T(8,128)S(1)}, bf16[6,81,128]{2,1,0:T(8,128)(2,1)S(1)}, bf16[6,81,128]{2,1,0:T(8,128)(2,1)S(1)}, bf16[3,81,128]{2,1,0:T(8,128)(2,1)S(1)}) custom-call(f32[4]{0:T(128)S(1)} %add_convert_fusion.flags.refs_0_, bf16[4,1080,540]{2,1,0:T(8,128)(2,1)S(1)} %get-tuple-element.73.refs_1_, ...), custom_call_target="tpu_custom_call" | custom-call | tf_op jit(solution)/shard_map/solve/pallas_call | solution.py:290
  64.5 1.6 %collective-permute-start.9 = (bf16[6,81,128]{2,1,0:T(8,128)(2,1)S(1)}, bf16[6,81,128]{2,1,0:T(8,128)(2,1)S(1)}, u32[]{:S(2)}, u32[]{:S(2)}) collective-permute-start(bf16[6,81,128]{2,1,0:T(8,128)(2,1)S(1)} %get-tuple-element.81), channel_id=1, source_target_pairs={{0,24},{1,25},{2,26},{3,27},{4,28},{5,29},{6,30},{7,31},{8,0},{9,1... | collective-permute-start | bytes 373256 | tf_op jit(solution)/shard_map/ppermute | solution.py:467
  66.1 1.3 %collective-permute-start.10 = (bf16[6,81,128]{2,1,0:T(8,128)(2,1)S(1)}, bf16[6,81,128]{2,1,0:T(8,128)(2,1)S(1)}, u32[]{:S(2)}, u32[]{:S(2)}) collective-permute-start(bf16[6,81,128]{2,1,0:T(8,128)(2,1)S(1)} %get-tuple-element.82), channel_id=1, source_target_pairs={{0,3},{1,0},{2,1},{3,2},{4,7},{5,4},{6,5},{7,6},{8,11},{9,8},{10,9... | collective-permute-start | bytes 373256 | tf_op jit(solution)/shard_map/ppermute | solution.py:468
  67.4 1.8 %collective-permute-start.11 = (bf16[3,81,128]{2,1,0:T(8,128)(2,1)S(1)}, bf16[3,81,128]{2,1,0:T(8,128)(2,1)S(1)}, u32[]{:S(2)}, u32[]{:S(2)}) collective-permute-start(bf16[3,81,128]{2,1,0:T(8,128)(2,1)S(1)} %get-tuple-element.83), channel_id=1, source_target_pairs={{0,27},{1,24},{2,25},{3,26},{4,31},{5,28},{6,29},{7,30},{8,3},{9,0... | collective-permute-start | bytes 186632 | tf_op jit(solution)/shard_map/ppermute | solution.py:469
  69.2 3.4 %collective-permute-done.11.gxz.refs_4_ = bf16[3,81,128]{2,1,0:T(8,128)(2,1)S(1)} collective-permute-done((bf16[3,81,128]{2,1,0:T(8,128)(2,1)S(1)}, bf16[3,81,128]{2,1,0:T(8,128)(2,1)S(1)}, u32[]{:S(2)}, u32[]{:S(2)}) %collective-permute-start.11) | collective-permute-done | bytes 62240 | tf_op jit(solution)/shard_map/ppermute | solution.py:469
  73.2 2.1 %all-gather.3 = f32[8,104,128]{2,1,0:T(8,128)S(1)} all-gather(f32[4,104,128]{2,1,0:T(8,128)S(1)} %reduce.3), channel_id=5, replica_groups=mesh['gx'=4,'gy'=2,'gz'=4] {'gy'}, dimensions={0}, use_global_device_ids=true | all-gather | bytes 638976 | tf_op jit(solution)/shard_map/all_gather | solution.py:475
  75.3 1.7 %element.3 = (f32[648,128]{1,0:T(8,128)}, f32[8,81,128]{2,1,0:T(8,128)S(1)}, f32[4,16,128]{2,1,0:T(8,128)S(1)}, f32[4,16,128]{2,1,0:T(8,128)S(1)}, f32[4,16,128]{2,1,0:T(8,128)S(1)}) custom-call(f32[4]{0:T(128)S(1)} %add_convert_fusion.flags.refs_0_, f32[12,81,128]{2,1,0:T(8,128)S(1)} %get-tuple-element.80.c.refs_1_, ...), custom_call_target="tpu_custom_call" | custom-call | tf_op jit(solution)/shard_map/element/pallas_call | solution.py:132
  77.0 2.3 %collective-permute-start.12 = (f32[4,16,128]{2,1,0:T(8,128)S(1)}, f32[4,16,128]{2,1,0:T(8,128)S(1)}, u32[]{:S(2)}, u32[]{:S(2)}) collective-permute-start(f32[4,16,128]{2,1,0:T(8,128)S(1)} %get-tuple-element.87), channel_id=1, source_target_pairs={{0,8},{1,9},{2,10},{3,11},{4,12},{5,13},{6,14},{7,15},{8,16},{9,17... | collective-permute-start | bytes 98312 | tf_op jit(solution)/shard_map/ppermute | solution.py:537
  79.4 1.8 %all-gather.4 = f32[8,16,128]{2,1,0:T(8,128)S(1)} all-gather(f32[4,16,128]{2,1,0:T(8,128)S(1)} %get-tuple-element.88), channel_id=6, replica_groups=mesh['gx'=4,'gy'=2,'gz'=4] {'gy'}, dimensions={0}, use_global_device_ids=true | all-gather | bytes 98304 | tf_op jit(solution)/shard_map/all_gather | solution.py:475
  81.8 3.2 %collective-permute-done.13.fz = f32[4,16,128]{2,1,0:T(8,128)S(1)} collective-permute-done((f32[4,16,128]{2,1,0:T(8,128)S(1)}, f32[4,16,128]{2,1,0:T(8,128)S(1)}, u32[]{:S(2)}, u32[]{:S(2)}) %collective-permute-start.13) | collective-permute-done | bytes 32800 | tf_op jit(solution)/shard_map/ppermute | solution.py:538
  85.0 1.3 %finish.1 = f32[648,128]{1,0:T(8,128)} custom-call(f32[4]{0:T(128)S(1)} %add_convert_fusion.flags.refs_0_, f32[8,81,128]{2,1,0:T(8,128)S(1)} %get-tuple-element.86.res, f32[4,16,128]{2,1,0:T(8,128)S(1)} %collective-permute-done.12.fx, f32[2,4,16,128]{3,2,1,0:T(8,128)S(1)} %bitcast.29, f32[4,16,128]{2,1,0:T(8,128)S(1)} %collective-permute-done.13.fz), custom_call_target="tpu_custom_call" | custom-call | tf_op jit(solution)/shard_map/finish/pallas_call | solution.py:132
  (31 shorter events, 4.9 us)
Async XLA Ops:
  0.7 1.0 %copy-start.1 = (f32[2,2,2,81,128]{4,2,3,1,0:T(2,128)S(1)}, f32[2,2,2,81,128]{4,2,3,1,0:T(2,128)}, u32[]{:S(2)}) copy-start(f32[2,2,2,81,128]{4,2,3,1,0:T(2,128)} %param.5) | copy-start | bytes 995332
  5.0 12.4 %collective-permute-start.2 = (bf16[3,81,128]{2,1,0:T(8,128)(2,1)S(1)}, bf16[3,81,128]{2,1,0:T(8,128)(2,1)S(1)}, u32[]{:S(2)}, u32[]{:S(2)}) collective-permute-start(bf16[3,81,128]{2,1,0:T(8,128)(2,1)S(1)} %get-tuple-element.58), channel_id=1, source_target_pairs={{0,9},{1,10},{2,11},{3,8},{4,13},{5,14},{6,15},{7,12},{8,17},{9,18... | collective-permute-start | bytes 186632 | tf_op jit(solution)/shard_map/ppermute | solution.py:469
  8.9 8.6 %collective-permute-start = (bf16[6,81,128]{2,1,0:T(8,128)(2,1)S(1)}, bf16[6,81,128]{2,1,0:T(8,128)(2,1)S(1)}, u32[]{:S(2)}, u32[]{:S(2)}) collective-permute-start(bf16[6,81,128]{2,1,0:T(8,128)(2,1)S(1)} %get-tuple-element.56), channel_id=1, source_target_pairs={{0,8},{1,9},{2,10},{3,11},{4,12},{5,13},{6,14},{7,15},{8,16},{9,17... | collective-permute-start | bytes 373256 | tf_op jit(solution)/shard_map/ppermute | solution.py:467
  10.4 7.1 %collective-permute-start.1 = (bf16[6,81,128]{2,1,0:T(8,128)(2,1)S(1)}, bf16[6,81,128]{2,1,0:T(8,128)(2,1)S(1)}, u32[]{:S(2)}, u32[]{:S(2)}) collective-permute-start(bf16[6,81,128]{2,1,0:T(8,128)(2,1)S(1)} %get-tuple-element.57), channel_id=1, source_target_pairs={{0,1},{1,2},{2,3},{3,0},{4,5},{5,6},{6,7},{7,4},{8,9},{9,10},{10,1... | collective-permute-start | bytes 373256 | tf_op jit(solution)/shard_map/ppermute | solution.py:468
  11.9 0.7 copy-start.2
  17.4 10.9 %copy-start.4 = (s32[2,2,2,6,9]{4,2,3,1,0:T(2,128)S(1)}, s32[2,2,2,6,9]{4,2,3,1,0:T(2,128)}, u32[]{:S(2)}) copy-start(s32[2,2,2,6,9]{4,2,3,1,0:T(2,128)} %param.9) | copy-start | bytes 5188
  17.5 15.6 %copy-start = (f32[2,2,2,108,108]{4,2,3,1,0:T(2,128)S(1)}, f32[2,2,2,108,108]{4,2,3,1,0:T(2,128)}, u32[]{:S(2)}) copy-start(f32[2,2,2,108,108]{4,2,3,1,0:T(2,128)} %param.8) | copy-start | bytes 1119748
  17.5 30.0 %copy-start.3 = (s32[2,2,2,540]{3,2,1,0:T(2,128)S(1)}, s32[2,2,2,540]{3,2,1,0:T(2,128)}, u32[]{:S(2)}) copy-start(s32[2,2,2,540]{3,2,1,0:T(2,128)} %order.1) | copy-start | bytes 51844
  28.6 7.5 %collective-permute-start.5 = (bf16[3,81,128]{2,1,0:T(8,128)(2,1)S(1)}, bf16[3,81,128]{2,1,0:T(8,128)(2,1)S(1)}, u32[]{:S(2)}, u32[]{:S(2)}) collective-permute-start(bf16[3,81,128]{2,1,0:T(8,128)(2,1)S(1)} %get-tuple-element.63), channel_id=1, source_target_pairs={{0,27},{1,24},{2,25},{3,26},{4,31},{5,28},{6,29},{7,30},{8,3},{9,0... | collective-permute-start | bytes 186632 | tf_op jit(solution)/shard_map/ppermute | solution.py:469
  31.7 5.0 %collective-permute-start.3 = (bf16[6,81,128]{2,1,0:T(8,128)(2,1)S(1)}, bf16[6,81,128]{2,1,0:T(8,128)(2,1)S(1)}, u32[]{:S(2)}, u32[]{:S(2)}) collective-permute-start(bf16[6,81,128]{2,1,0:T(8,128)(2,1)S(1)} %get-tuple-element.61), channel_id=1, source_target_pairs={{0,24},{1,25},{2,26},{3,27},{4,28},{5,29},{6,30},{7,31},{8,0},{9,1... | collective-permute-start | bytes 373256 | tf_op jit(solution)/shard_map/ppermute | solution.py:467
  32.3 5.0 %collective-permute-start.4 = (bf16[6,81,128]{2,1,0:T(8,128)(2,1)S(1)}, bf16[6,81,128]{2,1,0:T(8,128)(2,1)S(1)}, u32[]{:S(2)}, u32[]{:S(2)}) collective-permute-start(bf16[6,81,128]{2,1,0:T(8,128)(2,1)S(1)} %get-tuple-element.62), channel_id=1, source_target_pairs={{0,3},{1,0},{2,1},{3,2},{4,7},{5,4},{6,5},{7,6},{8,11},{9,8},{10,9... | collective-permute-start | bytes 373256 | tf_op jit(solution)/shard_map/ppermute | solution.py:468
  43.8 8.4 %collective-permute-start.8 = (bf16[3,81,128]{2,1,0:T(8,128)(2,1)S(1)}, bf16[3,81,128]{2,1,0:T(8,128)(2,1)S(1)}, u32[]{:S(2)}, u32[]{:S(2)}) collective-permute-start(bf16[3,81,128]{2,1,0:T(8,128)(2,1)S(1)} %get-tuple-element.79), channel_id=1, source_target_pairs={{0,9},{1,10},{2,11},{3,8},{4,13},{5,14},{6,15},{7,12},{8,17},{9,18... | collective-permute-start | bytes 186632 | tf_op jit(solution)/shard_map/ppermute | solution.py:469
  44.8 7.7 %collective-permute-start.6 = (bf16[6,81,128]{2,1,0:T(8,128)(2,1)S(1)}, bf16[6,81,128]{2,1,0:T(8,128)(2,1)S(1)}, u32[]{:S(2)}, u32[]{:S(2)}) collective-permute-start(bf16[6,81,128]{2,1,0:T(8,128)(2,1)S(1)} %get-tuple-element.77), channel_id=1, source_target_pairs={{0,8},{1,9},{2,10},{3,11},{4,12},{5,13},{6,14},{7,15},{8,16},{9,17... | collective-permute-start | bytes 373256 | tf_op jit(solution)/shard_map/ppermute | solution.py:467
  46.2 7.3 %collective-permute-start.7 = (bf16[6,81,128]{2,1,0:T(8,128)(2,1)S(1)}, bf16[6,81,128]{2,1,0:T(8,128)(2,1)S(1)}, u32[]{:S(2)}, u32[]{:S(2)}) collective-permute-start(bf16[6,81,128]{2,1,0:T(8,128)(2,1)S(1)} %get-tuple-element.78), channel_id=1, source_target_pairs={{0,1},{1,2},{2,3},{3,0},{4,5},{5,6},{6,7},{7,4},{8,9},{9,10},{10,1... | collective-permute-start | bytes 373256 | tf_op jit(solution)/shard_map/ppermute | solution.py:468
  64.5 8.1 %collective-permute-start.9 = (bf16[6,81,128]{2,1,0:T(8,128)(2,1)S(1)}, bf16[6,81,128]{2,1,0:T(8,128)(2,1)S(1)}, u32[]{:S(2)}, u32[]{:S(2)}) collective-permute-start(bf16[6,81,128]{2,1,0:T(8,128)(2,1)S(1)} %get-tuple-element.81), channel_id=1, source_target_pairs={{0,24},{1,25},{2,26},{3,27},{4,28},{5,29},{6,30},{7,31},{8,0},{9,1... | collective-permute-start | bytes 373256 | tf_op jit(solution)/shard_map/ppermute | solution.py:467
  66.1 6.5 %collective-permute-start.10 = (bf16[6,81,128]{2,1,0:T(8,128)(2,1)S(1)}, bf16[6,81,128]{2,1,0:T(8,128)(2,1)S(1)}, u32[]{:S(2)}, u32[]{:S(2)}) collective-permute-start(bf16[6,81,128]{2,1,0:T(8,128)(2,1)S(1)} %get-tuple-element.82), channel_id=1, source_target_pairs={{0,3},{1,0},{2,1},{3,2},{4,7},{5,4},{6,5},{7,6},{8,11},{9,8},{10,9... | collective-permute-start | bytes 373256 | tf_op jit(solution)/shard_map/ppermute | solution.py:468
  67.4 5.2 %collective-permute-start.11 = (bf16[3,81,128]{2,1,0:T(8,128)(2,1)S(1)}, bf16[3,81,128]{2,1,0:T(8,128)(2,1)S(1)}, u32[]{:S(2)}, u32[]{:S(2)}) collective-permute-start(bf16[3,81,128]{2,1,0:T(8,128)(2,1)S(1)} %get-tuple-element.83), channel_id=1, source_target_pairs={{0,27},{1,24},{2,25},{3,26},{4,31},{5,28},{6,29},{7,30},{8,3},{9,0... | collective-permute-start | bytes 186632 | tf_op jit(solution)/shard_map/ppermute | solution.py:469
  77.0 4.8 %collective-permute-start.12 = (f32[4,16,128]{2,1,0:T(8,128)S(1)}, f32[4,16,128]{2,1,0:T(8,128)S(1)}, u32[]{:S(2)}, u32[]{:S(2)}) collective-permute-start(f32[4,16,128]{2,1,0:T(8,128)S(1)} %get-tuple-element.87), channel_id=1, source_target_pairs={{0,8},{1,9},{2,10},{3,11},{4,12},{5,13},{6,14},{7,15},{8,16},{9,17... | collective-permute-start | bytes 98312 | tf_op jit(solution)/shard_map/ppermute | solution.py:537
  79.3 5.7 %collective-permute-start.13 = (f32[4,16,128]{2,1,0:T(8,128)S(1)}, f32[4,16,128]{2,1,0:T(8,128)S(1)}, u32[]{:S(2)}, u32[]{:S(2)}) collective-permute-start(f32[4,16,128]{2,1,0:T(8,128)S(1)} %get-tuple-element.89), channel_id=1, source_target_pairs={{0,1},{1,2},{2,3},{3,0},{4,5},{5,6},{6,7},{7,4},{8,9},{9,10},{10,1... | collective-permute-start | bytes 98312 | tf_op jit(solution)/shard_map/ppermute | solution.py:538

commit v3 on v2

--- a/solution.py
+++ b/solution.py
@@ -23,6 +23,13 @@
 VMEM_LIMIT = 12 * 1024 * 1024
 
 
+FACE_ROWS = (
+    lambda a, b, g: 8 * INNER + FACE * (2 * b + g),
+    lambda a, b, g: 8 * INNER + FACE * (4 + 2 * a + g),
+    lambda a, b, g: 8 * INNER + FACE * (8 + 2 * a + b),
+)
+
+
 def canonical_rows(q):
     m = (q * 683) >> 16
     r = q - SLOT * m
@@ -43,7 +50,7 @@
     for copy in copies:
         copy.start()
     across = canonical_rows(lax.broadcasted_iota(jnp.int32, (1, WIDE), 1))
-    down = canonical_rows(lax.broadcasted_iota(jnp.int32, (WIDE, 1), 0))
+    down = lax.broadcasted_iota(jnp.int32, (PATCH, PATCH), 0).astype(f32)
     for n, copy in enumerate(copies):
         for z in range(cz):
             line = order[n // cy, n % cy, z : z + 1, :].astype(f32)
@@ -66,7 +73,7 @@
         out_shape=[
             jax.ShapeDtypeStruct((cx * cy, cz * PATCH, PATCH), bf16),
             jax.ShapeDtypeStruct((count, PATCH, WIDE), bf16),
-            jax.ShapeDtypeStruct((count, WIDE, PATCH), bf16),
+            jax.ShapeDtypeStruct((count, PATCH, PATCH), bf16),
         ],
         scratch_shapes=[
             pltpu.VMEM((cx * cy, PATCH, cz, PATCH), bf16),
@@ -233,21 +240,18 @@
             m = 4 * a + 2 * b + g
             stars[n, m * SLOT : (m + 1) * SLOT] = part.astype(bf16)
 
-    @pl.loop(0, cx * cy)
-    def _(step):
-        listed = []
+    listed = []
+    for n in range(cx * cy * cz):
+        got = jnp.dot(pick[n], stars[n], preferred_element_type=f32)
+        listed.append(got.astype(bf16))
+    for step in range(cx * cy):
+        pair = jnp.concatenate(listed[step * cz : (step + 1) * cz], axis=1)
+        answer = jnp.dot(matrix[step], pair, preferred_element_type=f32)
         for z in range(cz):
-            n = step * cz + z
-            got = jnp.dot(pick[n], stars[n], preferred_element_type=f32)
-            listed.append(got.astype(bf16))
-        listed = jnp.concatenate(listed, axis=1)
-        answer = jnp.dot(matrix[step], listed, preferred_element_type=f32)
-        for z in range(cz):
-            both[z] = answer[:, z * columns : (z + 1) * columns]
-        for z in range(cz):
-            n = step * cz + z
-            value = both[z, pl.ds(z, PATCH, stride=cz), :].astype(bf16)
-            solved[n] = jnp.dot(back[n], value, preferred_element_type=f32)
+            both[step * cz + z] = answer[:, z * columns : (z + 1) * columns]
+    for n in range(cx * cy * cz):
+        value = both[n, pl.ds(n % cz, PATCH, stride=cz), :].astype(bf16)
+        solved[n] = jnp.dot(back[n], value, preferred_element_type=f32)
 
     vertices = list(itertools.product(*map(range, cells)))
     for e in itertools.product(range(-1, cx), range(-1, cy), range(-1, cz)):
@@ -257,19 +261,18 @@
             if all(k in (0, 1) for k in m):
                 parts.append((n, m))
 
-        def total(low, high, keep):
+        def total(rows, base, keep):
             acc = None
             for n, m in parts:
                 if keep(m):
-                    base = (4 * m[0] + 2 * m[1] + m[2]) * SLOT
-                    val = solved[n, base + low : base + high]
+                    low = base(*m)
+                    val = solved[n, low : low + rows]
                     acc = val if acc is None else acc + val
             return acc
 
-        pieces = [total(0, X0, lambda m: True)]
-        for d in range(3):
-            low = INNER + d * FACE
-            pieces.append(total(low, low + FACE, lambda m: e[d] < 0 or m[d] == 1))
+        pieces = [total(INNER, lambda a, b, g: INNER * (4 * a + 2 * b + g), lambda m: True)]
+        for d, base in enumerate(FACE_ROWS):
+            pieces.append(total(FACE, base, lambda m: e[d] < 0 or m[d] == 1))
         val = cat(*pieces)
         x, y, z = e
         if x < 0 and z < 0:
@@ -295,8 +298,8 @@
         + [jax.ShapeDtypeStruct(h.shape, bf16) for h in halos],
         scratch_shapes=[
             pltpu.VMEM((count, WIDE, columns), bf16),
-            pltpu.VMEM((count, WIDE, columns), f32),
-            pltpu.VMEM((cz, cz * PATCH, columns), f32),
+            pltpu.VMEM((count, PATCH, columns), f32),
+            pltpu.VMEM((count, cz * PATCH, columns), f32),
         ],
         compiler_params=pltpu.CompilerParams(vmem_limit_bytes=VMEM_LIMIT),
         name="solve",

time: 86.5 us -> 76.1 us (0.88)
  Pallas kernels: 41.3 us -> 30.1 us
  waiting for transfers between devices: 9.8 us -> 11.3 us
    pallas_call x2, Pallas kernels: 21.8 us -> 11.8 us  [solve(): pl.pallas_call(functools.partial(solve_kernel, cells), in_specs=[pl.Block...]
    ppermute x4, waiting for transfers between devices: 3.37 us -> 5.06 us  [send_xz(): lax.ppermute(mxz, AXES, route((sign, 0, sign)))]
    pallas_call x2, Pallas kernels: 9.45 us -> 8.21 us  [tables(): pl.pallas_call(functools.partial(tables_kernel, cells), in_specs=[pl.Bloc...]
    ppermute x4, starting transfers between devices: 9.9 us -> 8.82 us  [send_xz(): lax.ppermute(mxz, AXES, route((sign, 0, sign)))]
    ppermute x4, starting transfers between devices: 5.2 us -> 6.1 us  [send_xz(): lax.ppermute(mx, AXES, route((sign, 0, 0)))]
  transfers between devices with their start and end apart: 14 -> 14, of which waited for: 7 -> 8; matrix products, arithmetic and copies ran while one was open for 0% -> 0% of each run, Pallas kernels for 14% -> 15%
where the time goes in v3:
time: 76.1 us; the launch traced here: 75.9 us
  Pallas kernels  30.1 us (40%)
  starting transfers between devices  21.5 us (28%)
  waiting for transfers between devices  11.3 us (15%)
  blocking collectives  10.1 us (13%)
  local copies, waits for them, and re-layouts  1.81 us (2%)
  between operations  0.78 us (1%)
    pallas_call x2, Pallas kernels, solve(): pl.pallas_call(functools.partial(solve_kernel, cells), in_specs=[pl.Block...  11.8 us
    all_gather x5, blocking collectives, send_y(): return lax.all_gather(my, 'gy')  10.1 us
    ppermute x4, starting transfers between devices, send_xz(): lax.ppermute(mxz, AXES, route((sign, 0, sign)))  8.82 us
    pallas_call x2, Pallas kernels, tables(): pl.pallas_call(functools.partial(tables_kernel, cells), in_specs=[pl.Bloc...  8.21 us
    pallas_call x8, Pallas kernels, call(): pl.pallas_call(kernel, in_specs=specs, out_specs=[pl.BlockSpec(memory_spa...  7.04 us
    ppermute x4, starting transfers between devices, send_xz(): lax.ppermute(mx, AXES, route((sign, 0, 0)))  6.1 us
    ppermute x4, waiting for transfers between devices, send_xz(): lax.ppermute(mxz, AXES, route((sign, 0, sign)))  5.06 us
    ppermute x4, starting transfers between devices, send_xz(): lax.ppermute(mz, AXES, route((0, 0, sign)))  4.33 us
  transfers between devices with their start and end apart: 14, of which 8 were waited for; matrix products, arithmetic and copies ran while one was open for 0% of the time, Pallas kernels for 15%

profile of v3, /device:TPU:0, one launch (start us, length us, event | category | flops | bytes accessed | tf_op | source)
XLA Modules:
  0.0 75.9 jit_solution(4371102247504530063)
XLA Ops:
  0.7 1.0 %copy-done.1 = f32[2,2,2,81,128]{4,2,3,1,0:T(2,128)S(1)} copy-done((f32[2,2,2,81,128]{4,2,3,1,0:T(2,128)S(1)}, f32[2,2,2,81,128]{4,2,3,1,0:T(2,128)}, u32[]{:S(2)}) %copy-start.1) | copy-done | bytes 331800
  2.3 2.1 %all-gather = bf16[8,112,128]{2,1,0:T(8,128)(2,1)S(1)} all-gather(bf16[4,112,128]{2,1,0:T(8,128)(2,1)S(1)} %get-tuple-element.47), channel_id=2, replica_groups=mesh['gx'=4,'gy'=2,'gz'=4] {'gy'}, dimensions={0}, use_global_device_ids=true | all-gather | bytes 344064 | tf_op jit(solution)/shard_map/all_gather | solution.py:478
  5.0 3.9 %collective-permute-start.2 = (bf16[3,81,128]{2,1,0:T(8,128)(2,1)S(1)}, bf16[3,81,128]{2,1,0:T(8,128)(2,1)S(1)}, u32[]{:S(2)}, u32[]{:S(2)}) collective-permute-start(bf16[3,81,128]{2,1,0:T(8,128)(2,1)S(1)} %get-tuple-element.58), channel_id=1, source_target_pairs={{0,9},{1,10},{2,11},{3,8},{4,13},{5,14},{6,15},{7,12},{8,17},{9,18... | collective-permute-start | bytes 186632 | tf_op jit(solution)/shard_map/ppermute | solution.py:472
  8.9 1.5 %collective-permute-start = (bf16[6,81,128]{2,1,0:T(8,128)(2,1)S(1)}, bf16[6,81,128]{2,1,0:T(8,128)(2,1)S(1)}, u32[]{:S(2)}, u32[]{:S(2)}) collective-permute-start(bf16[6,81,128]{2,1,0:T(8,128)(2,1)S(1)} %get-tuple-element.56), channel_id=1, source_target_pairs={{0,8},{1,9},{2,10},{3,11},{4,12},{5,13},{6,14},{7,15},{8,16},{9,17... | collective-permute-start | bytes 373256 | tf_op jit(solution)/shard_map/ppermute | solution.py:470
  10.4 1.6 %collective-permute-start.1 = (bf16[6,81,128]{2,1,0:T(8,128)(2,1)S(1)}, bf16[6,81,128]{2,1,0:T(8,128)(2,1)S(1)}, u32[]{:S(2)}, u32[]{:S(2)}) collective-permute-start(bf16[6,81,128]{2,1,0:T(8,128)(2,1)S(1)} %get-tuple-element.57), channel_id=1, source_target_pairs={{0,1},{1,2},{2,3},{3,0},{4,5},{5,6},{6,7},{7,4},{8,9},{9,10},{10,1... | collective-permute-start | bytes 373256 | tf_op jit(solution)/shard_map/ppermute | solution.py:471
  11.9 0.7 copy-done.2
  12.7 4.1 %tables.2 = (bf16[4,1080,540]{2,1,0:T(8,128)(2,1)S(1)}, bf16[8,540,768]{2,1,0:T(8,128)(2,1)S(1)}, bf16[8,540,540]{2,1,0:T(8,128)(2,1)S(1)}) custom-call(bf16[2,2,540,2,540]{4,3,2,1,0:T(2,128)(2,1)} %bitcast.32, s32[2,2,2,540]{3,2,1,0:T(2,128)S(1)} %copy-done.2), custom_call_target="tpu_custom_call" | custom-call | flops 6794772480 | bytes 4665600 | tf_op jit(solution)/shard_map/tables/pallas_call | solution.py:69
  17.2 5.9 %solve.2 = (f32[12,81,128]{2,1,0:T(8,128)S(1)}, bf16[6,81,128]{2,1,0:T(8,128)(2,1)S(1)}, bf16[6,81,128]{2,1,0:T(8,128)(2,1)S(1)}, bf16[3,81,128]{2,1,0:T(8,128)(2,1)S(1)}) custom-call(f32[4]{0:T(128)S(1)} %add_convert_fusion.flags.refs_0_, bf16[4,1080,540]{2,1,0:T(8,128)(2,1)S(1)} %get-tuple-element.52.refs_1_, ...), custom_call_target="tpu_custom_call" | custom-call | tf_op jit(solution)/shard_map/solve/pallas_call | solution.py:293
  23.3 2.7 %collective-permute-start.5 = (bf16[3,81,128]{2,1,0:T(8,128)(2,1)S(1)}, bf16[3,81,128]{2,1,0:T(8,128)(2,1)S(1)}, u32[]{:S(2)}, u32[]{:S(2)}) collective-permute-start(bf16[3,81,128]{2,1,0:T(8,128)(2,1)S(1)} %get-tuple-element.63), channel_id=1, source_target_pairs={{0,27},{1,24},{2,25},{3,26},{4,31},{5,28},{6,29},{7,30},{8,3},{9,0... | collective-permute-start | bytes 186632 | tf_op jit(solution)/shard_map/ppermute | solution.py:472
  26.1 1.3 %collective-permute-start.3 = (bf16[6,81,128]{2,1,0:T(8,128)(2,1)S(1)}, bf16[6,81,128]{2,1,0:T(8,128)(2,1)S(1)}, u32[]{:S(2)}, u32[]{:S(2)}) collective-permute-start(bf16[6,81,128]{2,1,0:T(8,128)(2,1)S(1)} %get-tuple-element.61), channel_id=1, source_target_pairs={{0,24},{1,25},{2,26},{3,27},{4,28},{5,29},{6,30},{7,31},{8,0},{9,1... | collective-permute-start | bytes 373256 | tf_op jit(solution)/shard_map/ppermute | solution.py:470
  28.0 3.0 %matrices.1.refs_6_ = f32[8,108,108]{2,1,0:T(8,128)S(1)} custom-call(f32[2,2,108,2,108]{4,3,2,1,0:T(2,128)S(1)} %bitcast.27, s32[8,1,108]{2,1,0:T(1,128)S(1)} %pad_add_fusion.slot), custom_call_target="tpu_custom_call" | custom-call | flops 241864704 | bytes 746496 | tf_op jit(solution)/shard_map/matrices/pallas_call | solution.py:118
  31.3 1.1 %collective-permute-done.4.gz.refs_3_ = bf16[6,81,128]{2,1,0:T(8,128)(2,1)S(1)} collective-permute-done((bf16[6,81,128]{2,1,0:T(8,128)(2,1)S(1)}, bf16[6,81,128]{2,1,0:T(8,128)(2,1)S(1)}, u32[]{:S(2)}, u32[]{:S(2)}) %collective-permute-start.4) | collective-permute-done | bytes 124448 | tf_op jit(solution)/shard_map/ppermute | solution.py:471
  32.9 2.1 %all-gather.1 = f32[8,104,128]{2,1,0:T(8,128)S(1)} all-gather(f32[4,104,128]{2,1,0:T(8,128)S(1)} %reduce.2), channel_id=3, replica_groups=mesh['gx'=4,'gy'=2,'gz'=4] {'gy'}, dimensions={0}, use_global_device_ids=true | all-gather | bytes 638976 | tf_op jit(solution)/shard_map/all_gather | solution.py:478
  35.1 1.1 %element.2 = (f32[8,81,128]{2,1,0:T(8,128)S(1)}, f32[8,81,128]{2,1,0:T(8,128)S(1)}, f32[4,16,128]{2,1,0:T(8,128)S(1)}, f32[4,16,128]{2,1,0:T(8,128)S(1)}, bf16[4,112,128]{2,1,0:T(8,128)(2,1)S(1)}) custom-call(f32[4]{0:T(128)S(1)} %add_convert_fusion.flags.refs_0_, f32[12,81,128]{2,1,0:T(8,128)S(1)} %get-tuple-element.59.c.refs_1_, ...), custom_call_target="tpu_custom_call" | custom-call | tf_op jit(solution)/shard_map/element/pallas_call | solution.py:139
  36.2 2.0 %all-gather.2 = bf16[8,112,128]{2,1,0:T(8,128)(2,1)S(1)} all-gather(bf16[4,112,128]{2,1,0:T(8,128)(2,1)S(1)} %get-tuple-element.66), channel_id=4, replica_groups=mesh['gx'=4,'gy'=2,'gz'=4] {'gy'}, dimensions={0}, use_global_device_ids=true | all-gather | bytes 344064 | tf_op jit(solution)/shard_map/all_gather | solution.py:478
  39.4 1.3 %collective-permute-start.6 = (bf16[6,81,128]{2,1,0:T(8,128)(2,1)S(1)}, bf16[6,81,128]{2,1,0:T(8,128)(2,1)S(1)}, u32[]{:S(2)}, u32[]{:S(2)}) collective-permute-start(bf16[6,81,128]{2,1,0:T(8,128)(2,1)S(1)} %get-tuple-element.77), channel_id=1, source_target_pairs={{0,8},{1,9},{2,10},{3,11},{4,12},{5,13},{6,14},{7,15},{8,16},{9,17... | collective-permute-start | bytes 373256 | tf_op jit(solution)/shard_map/ppermute | solution.py:470
  40.7 1.2 %collective-permute-start.7 = (bf16[6,81,128]{2,1,0:T(8,128)(2,1)S(1)}, bf16[6,81,128]{2,1,0:T(8,128)(2,1)S(1)}, u32[]{:S(2)}, u32[]{:S(2)}) collective-permute-start(bf16[6,81,128]{2,1,0:T(8,128)(2,1)S(1)} %get-tuple-element.78), channel_id=1, source_target_pairs={{0,1},{1,2},{2,3},{3,0},{4,5},{5,6},{6,7},{7,4},{8,9},{9,10},{10,1... | collective-permute-start | bytes 373256 | tf_op jit(solution)/shard_map/ppermute | solution.py:471
  41.8 4.1 %tables.3 = (bf16[4,1080,540]{2,1,0:T(8,128)(2,1)S(1)}, bf16[8,540,768]{2,1,0:T(8,128)(2,1)S(1)}, bf16[8,540,540]{2,1,0:T(8,128)(2,1)S(1)}) custom-call(bf16[2,2,540,2,540]{4,3,2,1,0:T(2,128)(2,1)} %bitcast.33, s32[2,2,2,540]{3,2,1,0:T(2,128)S(1)} %copy-done.3), custom_call_target="tpu_custom_call" | custom-call | flops 6794772480 | bytes 4665600 | tf_op jit(solution)/shard_map/tables/pallas_call | solution.py:69
  46.0 1.5 %collective-permute-done.8.refs_8_ = bf16[3,81,128]{2,1,0:T(8,128)(2,1)S(1)} collective-permute-done((bf16[3,81,128]{2,1,0:T(8,128)(2,1)S(1)}, bf16[3,81,128]{2,1,0:T(8,128)(2,1)S(1)}, u32[]{:S(2)}, u32[]{:S(2)}) %collective-permute-start.8) | collective-permute-done | bytes 62240 | tf_op jit(solution)/shard_map/ppermute | solution.py:472
  47.4 0.7 collective-permute-done.7.refs_7_.refs_9_
  48.1 5.9 %solve.3 = (f32[12,81,128]{2,1,0:T(8,128)S(1)}, bf16[6,81,128]{2,1,0:T(8,128)(2,1)S(1)}, bf16[6,81,128]{2,1,0:T(8,128)(2,1)S(1)}, bf16[3,81,128]{2,1,0:T(8,128)(2,1)S(1)}) custom-call(f32[4]{0:T(128)S(1)} %add_convert_fusion.flags.refs_0_, bf16[4,1080,540]{2,1,0:T(8,128)(2,1)S(1)} %get-tuple-element.73.refs_1_, ...), custom_call_target="tpu_custom_call" | custom-call | tf_op jit(solution)/shard_map/solve/pallas_call | solution.py:293
  54.0 2.0 %collective-permute-start.9 = (bf16[6,81,128]{2,1,0:T(8,128)(2,1)S(1)}, bf16[6,81,128]{2,1,0:T(8,128)(2,1)S(1)}, u32[]{:S(2)}, u32[]{:S(2)}) collective-permute-start(bf16[6,81,128]{2,1,0:T(8,128)(2,1)S(1)} %get-tuple-element.81), channel_id=1, source_target_pairs={{0,24},{1,25},{2,26},{3,27},{4,28},{5,29},{6,30},{7,31},{8,0},{9,1... | collective-permute-start | bytes 373256 | tf_op jit(solution)/shard_map/ppermute | solution.py:470
  56.0 1.0 %collective-permute-start.10 = (bf16[6,81,128]{2,1,0:T(8,128)(2,1)S(1)}, bf16[6,81,128]{2,1,0:T(8,128)(2,1)S(1)}, u32[]{:S(2)}, u32[]{:S(2)}) collective-permute-start(bf16[6,81,128]{2,1,0:T(8,128)(2,1)S(1)} %get-tuple-element.82), channel_id=1, source_target_pairs={{0,3},{1,0},{2,1},{3,2},{4,7},{5,4},{6,5},{7,6},{8,11},{9,8},{10,9... | collective-permute-start | bytes 373256 | tf_op jit(solution)/shard_map/ppermute | solution.py:471
  57.0 1.6 %collective-permute-start.11 = (bf16[3,81,128]{2,1,0:T(8,128)(2,1)S(1)}, bf16[3,81,128]{2,1,0:T(8,128)(2,1)S(1)}, u32[]{:S(2)}, u32[]{:S(2)}) collective-permute-start(bf16[3,81,128]{2,1,0:T(8,128)(2,1)S(1)} %get-tuple-element.83), channel_id=1, source_target_pairs={{0,27},{1,24},{2,25},{3,26},{4,31},{5,28},{6,29},{7,30},{8,3},{9,0... | collective-permute-start | bytes 186632 | tf_op jit(solution)/shard_map/ppermute | solution.py:472
  58.6 3.6 %collective-permute-done.11.gxz.refs_4_ = bf16[3,81,128]{2,1,0:T(8,128)(2,1)S(1)} collective-permute-done((bf16[3,81,128]{2,1,0:T(8,128)(2,1)S(1)}, bf16[3,81,128]{2,1,0:T(8,128)(2,1)S(1)}, u32[]{:S(2)}, u32[]{:S(2)}) %collective-permute-start.11) | collective-permute-done | bytes 62240 | tf_op jit(solution)/shard_map/ppermute | solution.py:472
  62.8 2.1 %all-gather.3 = f32[8,104,128]{2,1,0:T(8,128)S(1)} all-gather(f32[4,104,128]{2,1,0:T(8,128)S(1)} %reduce.3), channel_id=5, replica_groups=mesh['gx'=4,'gy'=2,'gz'=4] {'gy'}, dimensions={0}, use_global_device_ids=true | all-gather | bytes 638976 | tf_op jit(solution)/shard_map/all_gather | solution.py:478
  64.9 1.7 %element.3 = (f32[648,128]{1,0:T(8,128)}, f32[8,81,128]{2,1,0:T(8,128)S(1)}, f32[4,16,128]{2,1,0:T(8,128)S(1)}, f32[4,16,128]{2,1,0:T(8,128)S(1)}, f32[4,16,128]{2,1,0:T(8,128)S(1)}) custom-call(f32[4]{0:T(128)S(1)} %add_convert_fusion.flags.refs_0_, f32[12,81,128]{2,1,0:T(8,128)S(1)} %get-tuple-element.80.c.refs_1_, ...), custom_call_target="tpu_custom_call" | custom-call | tf_op jit(solution)/shard_map/element/pallas_call | solution.py:139
  66.6 2.3 %collective-permute-start.12 = (f32[4,16,128]{2,1,0:T(8,128)S(1)}, f32[4,16,128]{2,1,0:T(8,128)S(1)}, u32[]{:S(2)}, u32[]{:S(2)}) collective-permute-start(f32[4,16,128]{2,1,0:T(8,128)S(1)} %get-tuple-element.87), channel_id=1, source_target_pairs={{0,8},{1,9},{2,10},{3,11},{4,12},{5,13},{6,14},{7,15},{8,16},{9,17... | collective-permute-start | bytes 98312 | tf_op jit(solution)/shard_map/ppermute | solution.py:540
  68.9 1.8 %all-gather.4 = f32[8,16,128]{2,1,0:T(8,128)S(1)} all-gather(f32[4,16,128]{2,1,0:T(8,128)S(1)} %get-tuple-element.88), channel_id=6, replica_groups=mesh['gx'=4,'gy'=2,'gz'=4] {'gy'}, dimensions={0}, use_global_device_ids=true | all-gather | bytes 98304 | tf_op jit(solution)/shard_map/all_gather | solution.py:478
  70.7 0.7 collective-permute-done.12.fx
  71.4 3.2 %collective-permute-done.13.fz = f32[4,16,128]{2,1,0:T(8,128)S(1)} collective-permute-done((f32[4,16,128]{2,1,0:T(8,128)S(1)}, f32[4,16,128]{2,1,0:T(8,128)S(1)}, u32[]{:S(2)}, u32[]{:S(2)}) %collective-permute-start.13) | collective-permute-done | bytes 32800 | tf_op jit(solution)/shard_map/ppermute | solution.py:541
  74.6 1.3 %finish.1 = f32[648,128]{1,0:T(8,128)} custom-call(f32[4]{0:T(128)S(1)} %add_convert_fusion.flags.refs_0_, f32[8,81,128]{2,1,0:T(8,128)S(1)} %get-tuple-element.86.res, f32[4,16,128]{2,1,0:T(8,128)S(1)} %collective-permute-done.12.fx, f32[2,4,16,128]{3,2,1,0:T(8,128)S(1)} %bitcast.29, f32[4,16,128]{2,1,0:T(8,128)S(1)} %collective-permute-done.13.fz), custom_call_target="tpu_custom_call" | custom-call | tf_op jit(solution)/shard_map/finish/pallas_call | solution.py:139
  (31 shorter events, 5.1 us)
Async XLA Ops:
  0.7 1.0 %copy-start.1 = (f32[2,2,2,81,128]{4,2,3,1,0:T(2,128)S(1)}, f32[2,2,2,81,128]{4,2,3,1,0:T(2,128)}, u32[]{:S(2)}) copy-start(f32[2,2,2,81,128]{4,2,3,1,0:T(2,128)} %param.5) | copy-start | bytes 995332
  5.0 11.8 %collective-permute-start.2 = (bf16[3,81,128]{2,1,0:T(8,128)(2,1)S(1)}, bf16[3,81,128]{2,1,0:T(8,128)(2,1)S(1)}, u32[]{:S(2)}, u32[]{:S(2)}) collective-permute-start(bf16[3,81,128]{2,1,0:T(8,128)(2,1)S(1)} %get-tuple-element.58), channel_id=1, source_target_pairs={{0,9},{1,10},{2,11},{3,8},{4,13},{5,14},{6,15},{7,12},{8,17},{9,18... | collective-permute-start | bytes 186632 | tf_op jit(solution)/shard_map/ppermute | solution.py:472
  8.9 7.9 %collective-permute-start = (bf16[6,81,128]{2,1,0:T(8,128)(2,1)S(1)}, bf16[6,81,128]{2,1,0:T(8,128)(2,1)S(1)}, u32[]{:S(2)}, u32[]{:S(2)}) collective-permute-start(bf16[6,81,128]{2,1,0:T(8,128)(2,1)S(1)} %get-tuple-element.56), channel_id=1, source_target_pairs={{0,8},{1,9},{2,10},{3,11},{4,12},{5,13},{6,14},{7,15},{8,16},{9,17... | collective-permute-start | bytes 373256 | tf_op jit(solution)/shard_map/ppermute | solution.py:470
  10.4 6.9 %collective-permute-start.1 = (bf16[6,81,128]{2,1,0:T(8,128)(2,1)S(1)}, bf16[6,81,128]{2,1,0:T(8,128)(2,1)S(1)}, u32[]{:S(2)}, u32[]{:S(2)}) collective-permute-start(bf16[6,81,128]{2,1,0:T(8,128)(2,1)S(1)} %get-tuple-element.57), channel_id=1, source_target_pairs={{0,1},{1,2},{2,3},{3,0},{4,5},{5,6},{6,7},{7,4},{8,9},{9,10},{10,1... | collective-permute-start | bytes 373256 | tf_op jit(solution)/shard_map/ppermute | solution.py:471
  11.9 0.7 copy-start.2
  17.2 5.9 %copy-start.4 = (s32[2,2,2,6,9]{4,2,3,1,0:T(2,128)S(1)}, s32[2,2,2,6,9]{4,2,3,1,0:T(2,128)}, u32[]{:S(2)}) copy-start(s32[2,2,2,6,9]{4,2,3,1,0:T(2,128)} %param.9) | copy-start | bytes 5188
  17.2 10.8 %copy-start = (f32[2,2,2,108,108]{4,2,3,1,0:T(2,128)S(1)}, f32[2,2,2,108,108]{4,2,3,1,0:T(2,128)}, u32[]{:S(2)}) copy-start(f32[2,2,2,108,108]{4,2,3,1,0:T(2,128)} %param.8) | copy-start | bytes 1119748
  23.2 18.7 %copy-start.3 = (s32[2,2,2,540]{3,2,1,0:T(2,128)S(1)}, s32[2,2,2,540]{3,2,1,0:T(2,128)}, u32[]{:S(2)}) copy-start(s32[2,2,2,540]{3,2,1,0:T(2,128)} %order.1) | copy-start | bytes 51844
  23.3 7.7 %collective-permute-start.5 = (bf16[3,81,128]{2,1,0:T(8,128)(2,1)S(1)}, bf16[3,81,128]{2,1,0:T(8,128)(2,1)S(1)}, u32[]{:S(2)}, u32[]{:S(2)}) collective-permute-start(bf16[3,81,128]{2,1,0:T(8,128)(2,1)S(1)} %get-tuple-element.63), channel_id=1, source_target_pairs={{0,27},{1,24},{2,25},{3,26},{4,31},{5,28},{6,29},{7,30},{8,3},{9,0... | collective-permute-start | bytes 186632 | tf_op jit(solution)/shard_map/ppermute | solution.py:472
  26.1 5.2 %collective-permute-start.3 = (bf16[6,81,128]{2,1,0:T(8,128)(2,1)S(1)}, bf16[6,81,128]{2,1,0:T(8,128)(2,1)S(1)}, u32[]{:S(2)}, u32[]{:S(2)}) collective-permute-start(bf16[6,81,128]{2,1,0:T(8,128)(2,1)S(1)} %get-tuple-element.61), channel_id=1, source_target_pairs={{0,24},{1,25},{2,26},{3,27},{4,28},{5,29},{6,30},{7,31},{8,0},{9,1... | collective-permute-start | bytes 373256 | tf_op jit(solution)/shard_map/ppermute | solution.py:470
  27.4 5.0 %collective-permute-start.4 = (bf16[6,81,128]{2,1,0:T(8,128)(2,1)S(1)}, bf16[6,81,128]{2,1,0:T(8,128)(2,1)S(1)}, u32[]{:S(2)}, u32[]{:S(2)}) collective-permute-start(bf16[6,81,128]{2,1,0:T(8,128)(2,1)S(1)} %get-tuple-element.62), channel_id=1, source_target_pairs={{0,3},{1,0},{2,1},{3,2},{4,7},{5,4},{6,5},{7,6},{8,11},{9,8},{10,9... | collective-permute-start | bytes 373256 | tf_op jit(solution)/shard_map/ppermute | solution.py:471
  38.8 8.7 %collective-permute-start.8 = (bf16[3,81,128]{2,1,0:T(8,128)(2,1)S(1)}, bf16[3,81,128]{2,1,0:T(8,128)(2,1)S(1)}, u32[]{:S(2)}, u32[]{:S(2)}) collective-permute-start(bf16[3,81,128]{2,1,0:T(8,128)(2,1)S(1)} %get-tuple-element.79), channel_id=1, source_target_pairs={{0,9},{1,10},{2,11},{3,8},{4,13},{5,14},{6,15},{7,12},{8,17},{9,18... | collective-permute-start | bytes 186632 | tf_op jit(solution)/shard_map/ppermute | solution.py:472
  39.4 8.1 %collective-permute-start.6 = (bf16[6,81,128]{2,1,0:T(8,128)(2,1)S(1)}, bf16[6,81,128]{2,1,0:T(8,128)(2,1)S(1)}, u32[]{:S(2)}, u32[]{:S(2)}) collective-permute-start(bf16[6,81,128]{2,1,0:T(8,128)(2,1)S(1)} %get-tuple-element.77), channel_id=1, source_target_pairs={{0,8},{1,9},{2,10},{3,11},{4,12},{5,13},{6,14},{7,15},{8,16},{9,17... | collective-permute-start | bytes 373256 | tf_op jit(solution)/shard_map/ppermute | solution.py:470
  40.7 7.4 %collective-permute-start.7 = (bf16[6,81,128]{2,1,0:T(8,128)(2,1)S(1)}, bf16[6,81,128]{2,1,0:T(8,128)(2,1)S(1)}, u32[]{:S(2)}, u32[]{:S(2)}) collective-permute-start(bf16[6,81,128]{2,1,0:T(8,128)(2,1)S(1)} %get-tuple-element.78), channel_id=1, source_target_pairs={{0,1},{1,2},{2,3},{3,0},{4,5},{5,6},{6,7},{7,4},{8,9},{9,10},{10,1... | collective-permute-start | bytes 373256 | tf_op jit(solution)/shard_map/ppermute | solution.py:471
  54.0 8.2 %collective-permute-start.9 = (bf16[6,81,128]{2,1,0:T(8,128)(2,1)S(1)}, bf16[6,81,128]{2,1,0:T(8,128)(2,1)S(1)}, u32[]{:S(2)}, u32[]{:S(2)}) collective-permute-start(bf16[6,81,128]{2,1,0:T(8,128)(2,1)S(1)} %get-tuple-element.81), channel_id=1, source_target_pairs={{0,24},{1,25},{2,26},{3,27},{4,28},{5,29},{6,30},{7,31},{8,0},{9,1... | collective-permute-start | bytes 373256 | tf_op jit(solution)/shard_map/ppermute | solution.py:470
  56.0 6.2 %collective-permute-start.10 = (bf16[6,81,128]{2,1,0:T(8,128)(2,1)S(1)}, bf16[6,81,128]{2,1,0:T(8,128)(2,1)S(1)}, u32[]{:S(2)}, u32[]{:S(2)}) collective-permute-start(bf16[6,81,128]{2,1,0:T(8,128)(2,1)S(1)} %get-tuple-element.82), channel_id=1, source_target_pairs={{0,3},{1,0},{2,1},{3,2},{4,7},{5,4},{6,5},{7,6},{8,11},{9,8},{10,9... | collective-permute-start | bytes 373256 | tf_op jit(solution)/shard_map/ppermute | solution.py:471
  57.0 5.2 %collective-permute-start.11 = (bf16[3,81,128]{2,1,0:T(8,128)(2,1)S(1)}, bf16[3,81,128]{2,1,0:T(8,128)(2,1)S(1)}, u32[]{:S(2)}, u32[]{:S(2)}) collective-permute-start(bf16[3,81,128]{2,1,0:T(8,128)(2,1)S(1)} %get-tuple-element.83), channel_id=1, source_target_pairs={{0,27},{1,24},{2,25},{3,26},{4,31},{5,28},{6,29},{7,30},{8,3},{9,0... | collective-permute-start | bytes 186632 | tf_op jit(solution)/shard_map/ppermute | solution.py:472
  66.6 4.8 %collective-permute-start.12 = (f32[4,16,128]{2,1,0:T(8,128)S(1)}, f32[4,16,128]{2,1,0:T(8,128)S(1)}, u32[]{:S(2)}, u32[]{:S(2)}) collective-permute-start(f32[4,16,128]{2,1,0:T(8,128)S(1)} %get-tuple-element.87), channel_id=1, source_target_pairs={{0,8},{1,9},{2,10},{3,11},{4,12},{5,13},{6,14},{7,15},{8,16},{9,17... | collective-permute-start | bytes 98312 | tf_op jit(solution)/shard_map/ppermute | solution.py:540
  68.9 5.7 %collective-permute-start.13 = (f32[4,16,128]{2,1,0:T(8,128)S(1)}, f32[4,16,128]{2,1,0:T(8,128)S(1)}, u32[]{:S(2)}, u32[]{:S(2)}) collective-permute-start(f32[4,16,128]{2,1,0:T(8,128)S(1)} %get-tuple-element.89), channel_id=1, source_target_pairs={{0,1},{1,2},{2,3},{3,0},{4,5},{5,6},{6,7},{7,4},{8,9},{9,10},{10,1... | collective-permute-start | bytes 98312 | tf_op jit(solution)/shard_map/ppermute | solution.py:541

commit v4 on v3

--- a/solution.py
+++ b/solution.py
@@ -391,12 +391,11 @@
                 upz = upz + yr[peer, x * cz + z][90:99] * flags[1]
         val = own[e]
         local = cat(val[:Y0], upx, val[Y0:Z0], upy, val[Z0:], upz)
-        images[e] = jnp.dot(
-            mat[(x * cy + y) * cz + z],
-            local,
-            precision=lax.Precision.HIGHEST,
-            preferred_element_type=f32,
-        )
+        high, low, _ = exact_parts(mat[(x * cy + y) * cz + z])
+        top, rest, _ = exact_parts(local)
+        image = jnp.dot(high, top, preferred_element_type=f32)
+        image = image + jnp.dot(high, rest, preferred_element_type=f32)
+        images[e] = image + jnp.dot(low, top, preferred_element_type=f32)
     for e in itertools.product(*map(range, cells)):
         x, y, z = e
         n = (x * cy + y) * cz + z

time: 76.1 us -> 76 us (level)
  no operation moved by 1% of the time
where the time goes in v4:
time: 76 us; the launch traced here: 75.7 us
  Pallas kernels  29.9 us (39%)
  starting transfers between devices  21.5 us (28%)
  waiting for transfers between devices  11.3 us (15%)
  blocking collectives  10.1 us (13%)
  local copies, waits for them, and re-layouts  1.81 us (2%)
  between operations  0.78 us (1%)
    pallas_call x2, Pallas kernels, solve(): pl.pallas_call(functools.partial(solve_kernel, cells), in_specs=[pl.Block...  11.8 us
    all_gather x5, blocking collectives, send_y(): return lax.all_gather(my, 'gy')  10.1 us
    ppermute x4, starting transfers between devices, send_xz(): lax.ppermute(mxz, AXES, route((sign, 0, sign)))  8.82 us
    pallas_call x2, Pallas kernels, tables(): pl.pallas_call(functools.partial(tables_kernel, cells), in_specs=[pl.Bloc...  8.21 us
    pallas_call x8, Pallas kernels, call(): pl.pallas_call(kernel, in_specs=specs, out_specs=[pl.BlockSpec(memory_spa...  6.84 us
    ppermute x4, starting transfers between devices, send_xz(): lax.ppermute(mx, AXES, route((sign, 0, 0)))  6.1 us
    ppermute x4, waiting for transfers between devices, send_xz(): lax.ppermute(mxz, AXES, route((sign, 0, sign)))  5.06 us
    ppermute x4, starting transfers between devices, send_xz(): lax.ppermute(mz, AXES, route((0, 0, sign)))  4.33 us
  transfers between devices with their start and end apart: 14, of which 8 were waited for; matrix products, arithmetic and copies ran while one was open for 0% of the time, Pallas kernels for 15%

profile of v4, /device:TPU:0, one launch (start us, length us, event | category | flops | bytes accessed | tf_op | source)
XLA Modules:
  0.0 75.7 jit_solution(1300180145159518634)
XLA Ops:
  0.7 1.0 %copy-done.1 = f32[2,2,2,81,128]{4,2,3,1,0:T(2,128)S(1)} copy-done((f32[2,2,2,81,128]{4,2,3,1,0:T(2,128)S(1)}, f32[2,2,2,81,128]{4,2,3,1,0:T(2,128)}, u32[]{:S(2)}) %copy-start.1) | copy-done | bytes 331800
  2.3 2.1 %all-gather = bf16[8,112,128]{2,1,0:T(8,128)(2,1)S(1)} all-gather(bf16[4,112,128]{2,1,0:T(8,128)(2,1)S(1)} %get-tuple-element.47), channel_id=2, replica_groups=mesh['gx'=4,'gy'=2,'gz'=4] {'gy'}, dimensions={0}, use_global_device_ids=true | all-gather | bytes 344064 | tf_op jit(solution)/shard_map/all_gather | solution.py:477
  5.0 3.9 %collective-permute-start.2 = (bf16[3,81,128]{2,1,0:T(8,128)(2,1)S(1)}, bf16[3,81,128]{2,1,0:T(8,128)(2,1)S(1)}, u32[]{:S(2)}, u32[]{:S(2)}) collective-permute-start(bf16[3,81,128]{2,1,0:T(8,128)(2,1)S(1)} %get-tuple-element.58), channel_id=1, source_target_pairs={{0,9},{1,10},{2,11},{3,8},{4,13},{5,14},{6,15},{7,12},{8,17},{9,18... | collective-permute-start | bytes 186632 | tf_op jit(solution)/shard_map/ppermute | solution.py:471
  8.9 1.5 %collective-permute-start = (bf16[6,81,128]{2,1,0:T(8,128)(2,1)S(1)}, bf16[6,81,128]{2,1,0:T(8,128)(2,1)S(1)}, u32[]{:S(2)}, u32[]{:S(2)}) collective-permute-start(bf16[6,81,128]{2,1,0:T(8,128)(2,1)S(1)} %get-tuple-element.56), channel_id=1, source_target_pairs={{0,8},{1,9},{2,10},{3,11},{4,12},{5,13},{6,14},{7,15},{8,16},{9,17... | collective-permute-start | bytes 373256 | tf_op jit(solution)/shard_map/ppermute | solution.py:469
  10.4 1.6 %collective-permute-start.1 = (bf16[6,81,128]{2,1,0:T(8,128)(2,1)S(1)}, bf16[6,81,128]{2,1,0:T(8,128)(2,1)S(1)}, u32[]{:S(2)}, u32[]{:S(2)}) collective-permute-start(bf16[6,81,128]{2,1,0:T(8,128)(2,1)S(1)} %get-tuple-element.57), channel_id=1, source_target_pairs={{0,1},{1,2},{2,3},{3,0},{4,5},{5,6},{6,7},{7,4},{8,9},{9,10},{10,1... | collective-permute-start | bytes 373256 | tf_op jit(solution)/shard_map/ppermute | solution.py:470
  11.9 0.7 copy-done.2
  12.7 4.1 %tables.2 = (bf16[4,1080,540]{2,1,0:T(8,128)(2,1)S(1)}, bf16[8,540,768]{2,1,0:T(8,128)(2,1)S(1)}, bf16[8,540,540]{2,1,0:T(8,128)(2,1)S(1)}) custom-call(bf16[2,2,540,2,540]{4,3,2,1,0:T(2,128)(2,1)} %bitcast.32, s32[2,2,2,540]{3,2,1,0:T(2,128)S(1)} %copy-done.2), custom_call_target="tpu_custom_call" | custom-call | flops 6794772480 | bytes 4665600 | tf_op jit(solution)/shard_map/tables/pallas_call | solution.py:69
  17.2 5.9 %solve.2 = (f32[12,81,128]{2,1,0:T(8,128)S(1)}, bf16[6,81,128]{2,1,0:T(8,128)(2,1)S(1)}, bf16[6,81,128]{2,1,0:T(8,128)(2,1)S(1)}, bf16[3,81,128]{2,1,0:T(8,128)(2,1)S(1)}) custom-call(f32[4]{0:T(128)S(1)} %add_convert_fusion.flags.refs_0_, bf16[4,1080,540]{2,1,0:T(8,128)(2,1)S(1)} %get-tuple-element.52.refs_1_, ...), custom_call_target="tpu_custom_call" | custom-call | tf_op jit(solution)/shard_map/solve/pallas_call | solution.py:293
  23.3 2.7 %collective-permute-start.5 = (bf16[3,81,128]{2,1,0:T(8,128)(2,1)S(1)}, bf16[3,81,128]{2,1,0:T(8,128)(2,1)S(1)}, u32[]{:S(2)}, u32[]{:S(2)}) collective-permute-start(bf16[3,81,128]{2,1,0:T(8,128)(2,1)S(1)} %get-tuple-element.63), channel_id=1, source_target_pairs={{0,27},{1,24},{2,25},{3,26},{4,31},{5,28},{6,29},{7,30},{8,3},{9,0... | collective-permute-start | bytes 186632 | tf_op jit(solution)/shard_map/ppermute | solution.py:471
  26.1 1.3 %collective-permute-start.3 = (bf16[6,81,128]{2,1,0:T(8,128)(2,1)S(1)}, bf16[6,81,128]{2,1,0:T(8,128)(2,1)S(1)}, u32[]{:S(2)}, u32[]{:S(2)}) collective-permute-start(bf16[6,81,128]{2,1,0:T(8,128)(2,1)S(1)} %get-tuple-element.61), channel_id=1, source_target_pairs={{0,24},{1,25},{2,26},{3,27},{4,28},{5,29},{6,30},{7,31},{8,0},{9,1... | collective-permute-start | bytes 373256 | tf_op jit(solution)/shard_map/ppermute | solution.py:469
  28.0 3.0 %matrices.1.refs_6_ = f32[8,108,108]{2,1,0:T(8,128)S(1)} custom-call(f32[2,2,108,2,108]{4,3,2,1,0:T(2,128)S(1)} %bitcast.27, s32[8,1,108]{2,1,0:T(1,128)S(1)} %pad_add_fusion.slot), custom_call_target="tpu_custom_call" | custom-call | flops 241864704 | bytes 746496 | tf_op jit(solution)/shard_map/matrices/pallas_call | solution.py:118
  31.3 1.1 %collective-permute-done.4.gz.refs_3_ = bf16[6,81,128]{2,1,0:T(8,128)(2,1)S(1)} collective-permute-done((bf16[6,81,128]{2,1,0:T(8,128)(2,1)S(1)}, bf16[6,81,128]{2,1,0:T(8,128)(2,1)S(1)}, u32[]{:S(2)}, u32[]{:S(2)}) %collective-permute-start.4) | collective-permute-done | bytes 124448 | tf_op jit(solution)/shard_map/ppermute | solution.py:470
  32.9 2.1 %all-gather.1 = f32[8,104,128]{2,1,0:T(8,128)S(1)} all-gather(f32[4,104,128]{2,1,0:T(8,128)S(1)} %reduce.2), channel_id=3, replica_groups=mesh['gx'=4,'gy'=2,'gz'=4] {'gy'}, dimensions={0}, use_global_device_ids=true | all-gather | bytes 638976 | tf_op jit(solution)/shard_map/all_gather | solution.py:477
  35.1 1.1 %element.2 = (f32[8,81,128]{2,1,0:T(8,128)S(1)}, f32[8,81,128]{2,1,0:T(8,128)S(1)}, f32[4,16,128]{2,1,0:T(8,128)S(1)}, f32[4,16,128]{2,1,0:T(8,128)S(1)}, bf16[4,112,128]{2,1,0:T(8,128)(2,1)S(1)}) custom-call(f32[4]{0:T(128)S(1)} %add_convert_fusion.flags.refs_0_, f32[12,81,128]{2,1,0:T(8,128)S(1)} %get-tuple-element.59.c.refs_1_, ...), custom_call_target="tpu_custom_call" | custom-call | tf_op jit(solution)/shard_map/element/pallas_call | solution.py:139
  36.1 2.0 %all-gather.2 = bf16[8,112,128]{2,1,0:T(8,128)(2,1)S(1)} all-gather(bf16[4,112,128]{2,1,0:T(8,128)(2,1)S(1)} %get-tuple-element.66), channel_id=4, replica_groups=mesh['gx'=4,'gy'=2,'gz'=4] {'gy'}, dimensions={0}, use_global_device_ids=true | all-gather | bytes 344064 | tf_op jit(solution)/shard_map/all_gather | solution.py:477
  39.3 1.3 %collective-permute-start.6 = (bf16[6,81,128]{2,1,0:T(8,128)(2,1)S(1)}, bf16[6,81,128]{2,1,0:T(8,128)(2,1)S(1)}, u32[]{:S(2)}, u32[]{:S(2)}) collective-permute-start(bf16[6,81,128]{2,1,0:T(8,128)(2,1)S(1)} %get-tuple-element.77), channel_id=1, source_target_pairs={{0,8},{1,9},{2,10},{3,11},{4,12},{5,13},{6,14},{7,15},{8,16},{9,17... | collective-permute-start | bytes 373256 | tf_op jit(solution)/shard_map/ppermute | solution.py:469
  40.6 1.2 %collective-permute-start.7 = (bf16[6,81,128]{2,1,0:T(8,128)(2,1)S(1)}, bf16[6,81,128]{2,1,0:T(8,128)(2,1)S(1)}, u32[]{:S(2)}, u32[]{:S(2)}) collective-permute-start(bf16[6,81,128]{2,1,0:T(8,128)(2,1)S(1)} %get-tuple-element.78), channel_id=1, source_target_pairs={{0,1},{1,2},{2,3},{3,0},{4,5},{5,6},{6,7},{7,4},{8,9},{9,10},{10,1... | collective-permute-start | bytes 373256 | tf_op jit(solution)/shard_map/ppermute | solution.py:470
  41.8 4.1 %tables.3 = (bf16[4,1080,540]{2,1,0:T(8,128)(2,1)S(1)}, bf16[8,540,768]{2,1,0:T(8,128)(2,1)S(1)}, bf16[8,540,540]{2,1,0:T(8,128)(2,1)S(1)}) custom-call(bf16[2,2,540,2,540]{4,3,2,1,0:T(2,128)(2,1)} %bitcast.33, s32[2,2,2,540]{3,2,1,0:T(2,128)S(1)} %copy-done.3), custom_call_target="tpu_custom_call" | custom-call | flops 6794772480 | bytes 4665600 | tf_op jit(solution)/shard_map/tables/pallas_call | solution.py:69
  45.9 1.5 %collective-permute-done.8.refs_8_ = bf16[3,81,128]{2,1,0:T(8,128)(2,1)S(1)} collective-permute-done((bf16[3,81,128]{2,1,0:T(8,128)(2,1)S(1)}, bf16[3,81,128]{2,1,0:T(8,128)(2,1)S(1)}, u32[]{:S(2)}, u32[]{:S(2)}) %collective-permute-start.8) | collective-permute-done | bytes 62240 | tf_op jit(solution)/shard_map/ppermute | solution.py:471
  47.4 0.7 collective-permute-done.7.refs_7_.refs_9_
  48.0 5.9 %solve.3 = (f32[12,81,128]{2,1,0:T(8,128)S(1)}, bf16[6,81,128]{2,1,0:T(8,128)(2,1)S(1)}, bf16[6,81,128]{2,1,0:T(8,128)(2,1)S(1)}, bf16[3,81,128]{2,1,0:T(8,128)(2,1)S(1)}) custom-call(f32[4]{0:T(128)S(1)} %add_convert_fusion.flags.refs_0_, bf16[4,1080,540]{2,1,0:T(8,128)(2,1)S(1)} %get-tuple-element.73.refs_1_, ...), custom_call_target="tpu_custom_call" | custom-call | tf_op jit(solution)/shard_map/solve/pallas_call | solution.py:293
  54.0 2.0 %collective-permute-start.9 = (bf16[6,81,128]{2,1,0:T(8,128)(2,1)S(1)}, bf16[6,81,128]{2,1,0:T(8,128)(2,1)S(1)}, u32[]{:S(2)}, u32[]{:S(2)}) collective-permute-start(bf16[6,81,128]{2,1,0:T(8,128)(2,1)S(1)} %get-tuple-element.81), channel_id=1, source_target_pairs={{0,24},{1,25},{2,26},{3,27},{4,28},{5,29},{6,30},{7,31},{8,0},{9,1... | collective-permute-start | bytes 373256 | tf_op jit(solution)/shard_map/ppermute | solution.py:469
  56.0 1.0 %collective-permute-start.10 = (bf16[6,81,128]{2,1,0:T(8,128)(2,1)S(1)}, bf16[6,81,128]{2,1,0:T(8,128)(2,1)S(1)}, u32[]{:S(2)}, u32[]{:S(2)}) collective-permute-start(bf16[6,81,128]{2,1,0:T(8,128)(2,1)S(1)} %get-tuple-element.82), channel_id=1, source_target_pairs={{0,3},{1,0},{2,1},{3,2},{4,7},{5,4},{6,5},{7,6},{8,11},{9,8},{10,9... | collective-permute-start | bytes 373256 | tf_op jit(solution)/shard_map/ppermute | solution.py:470
  57.0 1.6 %collective-permute-start.11 = (bf16[3,81,128]{2,1,0:T(8,128)(2,1)S(1)}, bf16[3,81,128]{2,1,0:T(8,128)(2,1)S(1)}, u32[]{:S(2)}, u32[]{:S(2)}) collective-permute-start(bf16[3,81,128]{2,1,0:T(8,128)(2,1)S(1)} %get-tuple-element.83), channel_id=1, source_target_pairs={{0,27},{1,24},{2,25},{3,26},{4,31},{5,28},{6,29},{7,30},{8,3},{9,0... | collective-permute-start | bytes 186632 | tf_op jit(solution)/shard_map/ppermute | solution.py:471
  58.6 3.6 %collective-permute-done.11.gxz.refs_4_ = bf16[3,81,128]{2,1,0:T(8,128)(2,1)S(1)} collective-permute-done((bf16[3,81,128]{2,1,0:T(8,128)(2,1)S(1)}, bf16[3,81,128]{2,1,0:T(8,128)(2,1)S(1)}, u32[]{:S(2)}, u32[]{:S(2)}) %collective-permute-start.11) | collective-permute-done | bytes 62240 | tf_op jit(solution)/shard_map/ppermute | solution.py:471
  62.7 2.1 %all-gather.3 = f32[8,104,128]{2,1,0:T(8,128)S(1)} all-gather(f32[4,104,128]{2,1,0:T(8,128)S(1)} %reduce.3), channel_id=5, replica_groups=mesh['gx'=4,'gy'=2,'gz'=4] {'gy'}, dimensions={0}, use_global_device_ids=true | all-gather | bytes 638976 | tf_op jit(solution)/shard_map/all_gather | solution.py:477
  64.9 1.6 %element.3 = (f32[648,128]{1,0:T(8,128)}, f32[8,81,128]{2,1,0:T(8,128)S(1)}, f32[4,16,128]{2,1,0:T(8,128)S(1)}, f32[4,16,128]{2,1,0:T(8,128)S(1)}, f32[4,16,128]{2,1,0:T(8,128)S(1)}) custom-call(f32[4]{0:T(128)S(1)} %add_convert_fusion.flags.refs_0_, f32[12,81,128]{2,1,0:T(8,128)S(1)} %get-tuple-element.80.c.refs_1_, ...), custom_call_target="tpu_custom_call" | custom-call | tf_op jit(solution)/shard_map/element/pallas_call | solution.py:139
  66.4 2.3 %collective-permute-start.12 = (f32[4,16,128]{2,1,0:T(8,128)S(1)}, f32[4,16,128]{2,1,0:T(8,128)S(1)}, u32[]{:S(2)}, u32[]{:S(2)}) collective-permute-start(f32[4,16,128]{2,1,0:T(8,128)S(1)} %get-tuple-element.87), channel_id=1, source_target_pairs={{0,8},{1,9},{2,10},{3,11},{4,12},{5,13},{6,14},{7,15},{8,16},{9,17... | collective-permute-start | bytes 98312 | tf_op jit(solution)/shard_map/ppermute | solution.py:539
  68.7 1.8 %all-gather.4 = f32[8,16,128]{2,1,0:T(8,128)S(1)} all-gather(f32[4,16,128]{2,1,0:T(8,128)S(1)} %get-tuple-element.88), channel_id=6, replica_groups=mesh['gx'=4,'gy'=2,'gz'=4] {'gy'}, dimensions={0}, use_global_device_ids=true | all-gather | bytes 98304 | tf_op jit(solution)/shard_map/all_gather | solution.py:477
  70.5 0.7 collective-permute-done.12.fx
  71.2 3.2 %collective-permute-done.13.fz = f32[4,16,128]{2,1,0:T(8,128)S(1)} collective-permute-done((f32[4,16,128]{2,1,0:T(8,128)S(1)}, f32[4,16,128]{2,1,0:T(8,128)S(1)}, u32[]{:S(2)}, u32[]{:S(2)}) %collective-permute-start.13) | collective-permute-done | bytes 32800 | tf_op jit(solution)/shard_map/ppermute | solution.py:540
  74.4 1.3 %finish.1 = f32[648,128]{1,0:T(8,128)} custom-call(f32[4]{0:T(128)S(1)} %add_convert_fusion.flags.refs_0_, f32[8,81,128]{2,1,0:T(8,128)S(1)} %get-tuple-element.86.res, f32[4,16,128]{2,1,0:T(8,128)S(1)} %collective-permute-done.12.fx, f32[2,4,16,128]{3,2,1,0:T(8,128)S(1)} %bitcast.29, f32[4,16,128]{2,1,0:T(8,128)S(1)} %collective-permute-done.13.fz), custom_call_target="tpu_custom_call" | custom-call | tf_op jit(solution)/shard_map/finish/pallas_call | solution.py:139
  (31 shorter events, 5.1 us)
Async XLA Ops:
  0.7 1.0 %copy-start.1 = (f32[2,2,2,81,128]{4,2,3,1,0:T(2,128)S(1)}, f32[2,2,2,81,128]{4,2,3,1,0:T(2,128)}, u32[]{:S(2)}) copy-start(f32[2,2,2,81,128]{4,2,3,1,0:T(2,128)} %param.5) | copy-start | bytes 995332
  5.0 11.8 %collective-permute-start.2 = (bf16[3,81,128]{2,1,0:T(8,128)(2,1)S(1)}, bf16[3,81,128]{2,1,0:T(8,128)(2,1)S(1)}, u32[]{:S(2)}, u32[]{:S(2)}) collective-permute-start(bf16[3,81,128]{2,1,0:T(8,128)(2,1)S(1)} %get-tuple-element.58), channel_id=1, source_target_pairs={{0,9},{1,10},{2,11},{3,8},{4,13},{5,14},{6,15},{7,12},{8,17},{9,18... | collective-permute-start | bytes 186632 | tf_op jit(solution)/shard_map/ppermute | solution.py:471
  8.9 7.9 %collective-permute-start = (bf16[6,81,128]{2,1,0:T(8,128)(2,1)S(1)}, bf16[6,81,128]{2,1,0:T(8,128)(2,1)S(1)}, u32[]{:S(2)}, u32[]{:S(2)}) collective-permute-start(bf16[6,81,128]{2,1,0:T(8,128)(2,1)S(1)} %get-tuple-element.56), channel_id=1, source_target_pairs={{0,8},{1,9},{2,10},{3,11},{4,12},{5,13},{6,14},{7,15},{8,16},{9,17... | collective-permute-start | bytes 373256 | tf_op jit(solution)/shard_map/ppermute | solution.py:469
  10.4 6.9 %collective-permute-start.1 = (bf16[6,81,128]{2,1,0:T(8,128)(2,1)S(1)}, bf16[6,81,128]{2,1,0:T(8,128)(2,1)S(1)}, u32[]{:S(2)}, u32[]{:S(2)}) collective-permute-start(bf16[6,81,128]{2,1,0:T(8,128)(2,1)S(1)} %get-tuple-element.57), channel_id=1, source_target_pairs={{0,1},{1,2},{2,3},{3,0},{4,5},{5,6},{6,7},{7,4},{8,9},{9,10},{10,1... | collective-permute-start | bytes 373256 | tf_op jit(solution)/shard_map/ppermute | solution.py:470
  11.9 0.7 copy-start.2
  17.2 5.9 %copy-start.4 = (s32[2,2,2,6,9]{4,2,3,1,0:T(2,128)S(1)}, s32[2,2,2,6,9]{4,2,3,1,0:T(2,128)}, u32[]{:S(2)}) copy-start(s32[2,2,2,6,9]{4,2,3,1,0:T(2,128)} %param.9) | copy-start | bytes 5188
  17.2 10.8 %copy-start = (f32[2,2,2,108,108]{4,2,3,1,0:T(2,128)S(1)}, f32[2,2,2,108,108]{4,2,3,1,0:T(2,128)}, u32[]{:S(2)}) copy-start(f32[2,2,2,108,108]{4,2,3,1,0:T(2,128)} %param.8) | copy-start | bytes 1119748
  23.2 18.6 %copy-start.3 = (s32[2,2,2,540]{3,2,1,0:T(2,128)S(1)}, s32[2,2,2,540]{3,2,1,0:T(2,128)}, u32[]{:S(2)}) copy-start(s32[2,2,2,540]{3,2,1,0:T(2,128)} %order.1) | copy-start | bytes 51844
  23.3 7.7 %collective-permute-start.5 = (bf16[3,81,128]{2,1,0:T(8,128)(2,1)S(1)}, bf16[3,81,128]{2,1,0:T(8,128)(2,1)S(1)}, u32[]{:S(2)}, u32[]{:S(2)}) collective-permute-start(bf16[3,81,128]{2,1,0:T(8,128)(2,1)S(1)} %get-tuple-element.63), channel_id=1, source_target_pairs={{0,27},{1,24},{2,25},{3,26},{4,31},{5,28},{6,29},{7,30},{8,3},{9,0... | collective-permute-start | bytes 186632 | tf_op jit(solution)/shard_map/ppermute | solution.py:471
  26.1 5.2 %collective-permute-start.3 = (bf16[6,81,128]{2,1,0:T(8,128)(2,1)S(1)}, bf16[6,81,128]{2,1,0:T(8,128)(2,1)S(1)}, u32[]{:S(2)}, u32[]{:S(2)}) collective-permute-start(bf16[6,81,128]{2,1,0:T(8,128)(2,1)S(1)} %get-tuple-element.61), channel_id=1, source_target_pairs={{0,24},{1,25},{2,26},{3,27},{4,28},{5,29},{6,30},{7,31},{8,0},{9,1... | collective-permute-start | bytes 373256 | tf_op jit(solution)/shard_map/ppermute | solution.py:469
  27.4 5.0 %collective-permute-start.4 = (bf16[6,81,128]{2,1,0:T(8,128)(2,1)S(1)}, bf16[6,81,128]{2,1,0:T(8,128)(2,1)S(1)}, u32[]{:S(2)}, u32[]{:S(2)}) collective-permute-start(bf16[6,81,128]{2,1,0:T(8,128)(2,1)S(1)} %get-tuple-element.62), channel_id=1, source_target_pairs={{0,3},{1,0},{2,1},{3,2},{4,7},{5,4},{6,5},{7,6},{8,11},{9,8},{10,9... | collective-permute-start | bytes 373256 | tf_op jit(solution)/shard_map/ppermute | solution.py:470
  38.7 8.7 %collective-permute-start.8 = (bf16[3,81,128]{2,1,0:T(8,128)(2,1)S(1)}, bf16[3,81,128]{2,1,0:T(8,128)(2,1)S(1)}, u32[]{:S(2)}, u32[]{:S(2)}) collective-permute-start(bf16[3,81,128]{2,1,0:T(8,128)(2,1)S(1)} %get-tuple-element.79), channel_id=1, source_target_pairs={{0,9},{1,10},{2,11},{3,8},{4,13},{5,14},{6,15},{7,12},{8,17},{9,18... | collective-permute-start | bytes 186632 | tf_op jit(solution)/shard_map/ppermute | solution.py:471
  39.3 8.1 %collective-permute-start.6 = (bf16[6,81,128]{2,1,0:T(8,128)(2,1)S(1)}, bf16[6,81,128]{2,1,0:T(8,128)(2,1)S(1)}, u32[]{:S(2)}, u32[]{:S(2)}) collective-permute-start(bf16[6,81,128]{2,1,0:T(8,128)(2,1)S(1)} %get-tuple-element.77), channel_id=1, source_target_pairs={{0,8},{1,9},{2,10},{3,11},{4,12},{5,13},{6,14},{7,15},{8,16},{9,17... | collective-permute-start | bytes 373256 | tf_op jit(solution)/shard_map/ppermute | solution.py:469
  40.6 7.4 %collective-permute-start.7 = (bf16[6,81,128]{2,1,0:T(8,128)(2,1)S(1)}, bf16[6,81,128]{2,1,0:T(8,128)(2,1)S(1)}, u32[]{:S(2)}, u32[]{:S(2)}) collective-permute-start(bf16[6,81,128]{2,1,0:T(8,128)(2,1)S(1)} %get-tuple-element.78), channel_id=1, source_target_pairs={{0,1},{1,2},{2,3},{3,0},{4,5},{5,6},{6,7},{7,4},{8,9},{9,10},{10,1... | collective-permute-start | bytes 373256 | tf_op jit(solution)/shard_map/ppermute | solution.py:470
  54.0 8.2 %collective-permute-start.9 = (bf16[6,81,128]{2,1,0:T(8,128)(2,1)S(1)}, bf16[6,81,128]{2,1,0:T(8,128)(2,1)S(1)}, u32[]{:S(2)}, u32[]{:S(2)}) collective-permute-start(bf16[6,81,128]{2,1,0:T(8,128)(2,1)S(1)} %get-tuple-element.81), channel_id=1, source_target_pairs={{0,24},{1,25},{2,26},{3,27},{4,28},{5,29},{6,30},{7,31},{8,0},{9,1... | collective-permute-start | bytes 373256 | tf_op jit(solution)/shard_map/ppermute | solution.py:469
  56.0 6.2 %collective-permute-start.10 = (bf16[6,81,128]{2,1,0:T(8,128)(2,1)S(1)}, bf16[6,81,128]{2,1,0:T(8,128)(2,1)S(1)}, u32[]{:S(2)}, u32[]{:S(2)}) collective-permute-start(bf16[6,81,128]{2,1,0:T(8,128)(2,1)S(1)} %get-tuple-element.82), channel_id=1, source_target_pairs={{0,3},{1,0},{2,1},{3,2},{4,7},{5,4},{6,5},{7,6},{8,11},{9,8},{10,9... | collective-permute-start | bytes 373256 | tf_op jit(solution)/shard_map/ppermute | solution.py:470
  57.0 5.2 %collective-permute-start.11 = (bf16[3,81,128]{2,1,0:T(8,128)(2,1)S(1)}, bf16[3,81,128]{2,1,0:T(8,128)(2,1)S(1)}, u32[]{:S(2)}, u32[]{:S(2)}) collective-permute-start(bf16[3,81,128]{2,1,0:T(8,128)(2,1)S(1)} %get-tuple-element.83), channel_id=1, source_target_pairs={{0,27},{1,24},{2,25},{3,26},{4,31},{5,28},{6,29},{7,30},{8,3},{9,0... | collective-permute-start | bytes 186632 | tf_op jit(solution)/shard_map/ppermute | solution.py:471
  66.4 4.8 %collective-permute-start.12 = (f32[4,16,128]{2,1,0:T(8,128)S(1)}, f32[4,16,128]{2,1,0:T(8,128)S(1)}, u32[]{:S(2)}, u32[]{:S(2)}) collective-permute-start(f32[4,16,128]{2,1,0:T(8,128)S(1)} %get-tuple-element.87), channel_id=1, source_target_pairs={{0,8},{1,9},{2,10},{3,11},{4,12},{5,13},{6,14},{7,15},{8,16},{9,17... | collective-permute-start | bytes 98312 | tf_op jit(solution)/shard_map/ppermute | solution.py:539
  68.7 5.7 %collective-permute-start.13 = (f32[4,16,128]{2,1,0:T(8,128)S(1)}, f32[4,16,128]{2,1,0:T(8,128)S(1)}, u32[]{:S(2)}, u32[]{:S(2)}) collective-permute-start(f32[4,16,128]{2,1,0:T(8,128)S(1)} %get-tuple-element.89), channel_id=1, source_target_pairs={{0,1},{1,2},{2,3},{3,0},{4,5},{5,6},{6,7},{7,4},{8,9},{9,10},{10,1... | collective-permute-start | bytes 98312 | tf_op jit(solution)/shard_map/ppermute | solution.py:540
